TPU v7x, 512 devices: a whole 4x8x8 slice. The times are simulated.
512 devices in a mesh: grp: 2 (over x_hi), lon: 16 (over y, core), lat: 16 (over z, x_lo).
Axes of the slice: x: 4 (x_hi: 2, x_lo: 2; x = x_hi * 2 + x_lo), y: 8, z: 8, core: 2. Of those that a mesh axis runs over, the one named last changes fastest.
Arguments:
- fields: bfloat16 [6, 2, 192, 192, 512], P('grp', None, 'lat', 'lon'), may hold values from -6 to 6
- surface_mask: int32 [2, 192, 192], P(None, 'lat', 'lon'), may hold values 0 or 1
- w_qkv: bfloat16 [512, 1536], replicated, may hold values from -0.25 to 0.25
- w_out: bfloat16 [512, 512], replicated, may hold values from -0.25 to 0.25
- logit_scale: float32 [8], replicated, may hold values from 2 to 12
- mask_bias: float32 [8], replicated, may hold values from -2 to 2
- w_up: bfloat16 [512, 2048], replicated, may hold values from -0.25 to 0.25
- w_down: bfloat16 [2048, 512], replicated, may hold values from -0.125 to 0.125
Outputs:
- joined: bfloat16 [6, 2, 192, 192, 512], P('grp', None, 'lat', 'lon')
All inputs are finite; a program needn't handle non-finite values. No bound on the sum of `surface_mask` on one device may be relied on, other than what follows from the above.
Results may differ from a plain program's by a relative error of at most 0.006.
Values may be sent and summed in bfloat16 or wider, within the bound.
No kernel may reach another device: no remote copies, remote signals or barrier semaphores. Data moves between devices by JAX's collectives and lax.ppermute only.
A program may use at most 128 MiB of HBM per device.

v0:
```python
import jax
import jax.numpy as jnp
from jax import lax
from jax.sharding import PartitionSpec as P

WLAT = 6
SH_LAT = 3
SH_LON = 6


def passed_along(array, axis, by):
    count = lax.axis_size(axis)
    return lax.ppermute(array, axis, [(i, (i + by) % count) for i in range(count)])


def layer_norm(values):
    centred = values - jnp.mean(values, -1, keepdims=True)
    return centred * lax.rsqrt(jnp.mean(centred * centred, -1, keepdims=True) + 1e-05)


def unit_heads(mixed_part, head_count):
    shaped = mixed_part.reshape(mixed_part.shape[0], head_count, -1)
    scaled = shaped * lax.rsqrt(jnp.mean(shaped * shaped, -1, keepdims=True) + 1e-06)
    return scaled.reshape(mixed_part.shape).astype(jnp.bfloat16)


def project_heads(tokens_in, w_qkv, head_count):
    model_width = tokens_in.shape[-1]
    normed = layer_norm(tokens_in.astype(jnp.float32)).astype(jnp.bfloat16)
    mixed = jnp.dot(normed.reshape(-1, model_width), w_qkv, preferred_element_type=jnp.float32)
    queries = unit_heads(mixed[:, :model_width], head_count).reshape(tokens_in.shape)
    key_part = unit_heads(mixed[:, model_width : 2 * model_width], head_count).reshape(
        tokens_in.shape
    )
    value_part = mixed[:, 2 * model_width :].astype(jnp.bfloat16).reshape(tokens_in.shape)
    return (queries, key_part, value_part)


def window_rows(tensor):
    groups, levels, lat_rows, lon_cells = tensor.shape[:4]
    shaped = tensor.reshape((groups, levels, lat_rows // WLAT, WLAT, lon_cells) + tensor.shape[4:])
    return jnp.moveaxis(shaped, 2, 0).reshape(
        (lat_rows // WLAT, groups * levels * WLAT * lon_cells) + tensor.shape[4:]
    )


def unwindow_rows(tensor, groups, levels, lon_cells):
    windows = tensor.shape[0]
    shaped = tensor.reshape((windows, groups, levels, WLAT, lon_cells) + tensor.shape[2:])
    return jnp.moveaxis(shaped, 0, 2).reshape(
        (groups, levels, windows * WLAT, lon_cells) + tensor.shape[2:]
    )


def region_windows(flag_rows, levels, lon_cells):
    lat_rows = flag_rows.shape[0]
    flag_grid = jnp.broadcast_to(flag_rows[None, :, None], (levels, lat_rows, lon_cells))
    shaped = flag_grid.reshape(levels, lat_rows // WLAT, WLAT, lon_cells)
    return jnp.moveaxis(shaped, 1, 0).reshape(lat_rows // WLAT, -1)


def bias_windows(key_bias):
    head_count, levels, lat_rows, lon_cells = key_bias.shape
    shaped = key_bias.reshape(head_count, levels, lat_rows // WLAT, WLAT, lon_cells)
    return jnp.transpose(shaped, (2, 0, 1, 3, 4)).reshape(lat_rows // WLAT, head_count, -1)


def window_terms(query_win, key_win, value_win, bias_win, query_reg, key_reg, scale):
    head_count = scale.shape[0]
    windows, queries, model_width = query_win.shape
    head_size = model_width // head_count
    key_count = key_win.shape[1]
    query_heads = query_win.reshape(windows, queries, head_count, head_size)
    key_heads = key_win.reshape(windows, key_count, head_count, head_size)
    value_heads = value_win.reshape(windows, key_count, head_count, head_size)
    scores = jnp.einsum(
        "wqhd,wkhd->whqk", query_heads, key_heads, preferred_element_type=jnp.float32
    )
    scores = scores * (scale / head_size)[None, :, None, None] + bias_win[:, :, None, :]
    same_region = query_reg[:, None, :, None] == key_reg[:, None, None, :]
    weights = jnp.where(same_region, jnp.exp(scores), 0.0).astype(jnp.bfloat16)
    totals = jnp.sum(weights.astype(jnp.float32), -1)
    weighted = jnp.einsum(
        "whqk,wkhd->wqhd", weights, value_heads, preferred_element_type=jnp.float32
    )
    return (weighted, totals)


def blocked_terms(query_win, key_win, value_win, bias_win, query_reg, key_reg, scale):
    windows, queries = query_win.shape[:2]
    pairing = 1

    def regroup(tensor):
        return tensor.reshape((windows // pairing, pairing) + tensor.shape[1:])

    def attend_block(block_args):
        return window_terms(
            block_args[0],
            block_args[1],
            block_args[2],
            block_args[3],
            block_args[4],
            block_args[5],
            scale,
        )

    weighted, totals = lax.map(
        attend_block,
        (
            regroup(query_win),
            regroup(key_win),
            regroup(value_win),
            regroup(bias_win),
            regroup(query_reg),
            regroup(key_reg),
        ),
    )
    return (
        weighted.reshape((windows,) + weighted.shape[2:]),
        totals.reshape((windows,) + totals.shape[2:]),
    )


def normalise(weighted, totals, groups, levels, lon_cells):
    ratio = weighted / jnp.transpose(totals, (0, 2, 1))[..., None]
    flat = ratio.astype(jnp.bfloat16).reshape(ratio.shape[0], ratio.shape[1], -1)
    return unwindow_rows(flat, groups, levels, lon_cells)


def project_out(attended, w_out):
    model_width = attended.shape[-1]
    projected = jnp.dot(
        attended.reshape(-1, model_width), w_out, preferred_element_type=jnp.float32
    )
    return projected.astype(jnp.bfloat16).reshape(attended.shape)


def per_device(fields, surface_mask, w_qkv, w_out, logit_scale, mask_bias, w_up, w_down):
    local_groups, levels, lat_rows, lon_cells, model_width = fields.shape
    head_count = logit_scale.shape[0]
    flag_marks = surface_mask.astype(jnp.bfloat16)
    lower_rows, lower_marks = passed_along(
        (fields[:, :, :SH_LAT], flag_marks[:, :SH_LAT]), "lat", -1
    )
    shifted = jnp.concatenate([fields[:, :, SH_LAT:], lower_rows], 2)
    marked = jnp.concatenate([flag_marks[:, SH_LAT:], lower_marks], 1)
    east_rows, east_marks = passed_along(
        (shifted[:, :, :, :SH_LON], marked[:, :, :SH_LON]), "lon", -1
    )
    rolled = jnp.concatenate([shifted[:, :, :, SH_LON:], east_rows], 3)
    rolled_marks = jnp.concatenate([marked[:, :, SH_LON:], east_marks], 2).astype(jnp.float32)
    key_bias = mask_bias[:, None, None, None] * rolled_marks[None]
    total_rows = lat_rows * lax.axis_size("lat")
    first_row = lax.axis_index("lat") * lat_rows
    gathered = lax.all_to_all(rolled, "grp", split_axis=2, concat_axis=0, tiled=True)
    part_rows = lat_rows // lax.axis_size("grp")
    offset = lax.axis_index("grp") * part_rows
    all_groups = gathered.shape[0]
    queries, key_part, value_part = project_heads(gathered, w_qkv, head_count)
    flag_rows = (
        first_row + offset + jnp.arange(part_rows, dtype=jnp.int32) >= total_rows - SH_LAT
    ).astype(jnp.int32)
    region_all = jnp.tile(region_windows(flag_rows, levels, lon_cells), (1, all_groups))
    bias_one = bias_windows(lax.dynamic_slice_in_dim(key_bias, offset, part_rows, 2))
    weighted, totals = blocked_terms(
        window_rows(queries),
        window_rows(key_part),
        window_rows(value_part),
        jnp.tile(bias_one, (1, 1, all_groups)),
        region_all,
        region_all,
        logit_scale,
    )
    attended = normalise(weighted, totals, all_groups, levels, lon_cells)
    projected = lax.all_to_all(
        project_out(attended, w_out), "grp", split_axis=0, concat_axis=2, tiled=True
    )
    west_rim = passed_along(projected[:, :, :, -SH_LON:], "lon", 1)
    unrolled = jnp.concatenate([west_rim, projected[:, :, :, :-SH_LON]], 3)
    north_rim = passed_along(unrolled[:, :, -SH_LAT:], "lat", 1)
    unrolled = jnp.concatenate([north_rim, unrolled[:, :, :-SH_LAT]], 2)
    residual = (fields.astype(jnp.float32) + unrolled.astype(jnp.float32)).astype(jnp.bfloat16)
    mlp_in = layer_norm(residual.astype(jnp.float32)).astype(jnp.bfloat16)
    hidden = jax.nn.gelu(
        jnp.dot(mlp_in.reshape(-1, model_width), w_up, preferred_element_type=jnp.float32),
        approximate=True,
    ).astype(jnp.bfloat16)
    update = jnp.dot(hidden, w_down, preferred_element_type=jnp.float32).reshape(fields.shape)
    return (residual.astype(jnp.float32) + update).astype(jnp.bfloat16)


def solution(mesh):
    return jax.shard_map(
        per_device,
        mesh=mesh,
        in_specs=(
            P("grp", None, "lat", "lon", None),
            P(None, "lat", "lon"),
            P(),
            P(),
            P(),
            P(),
            P(),
            P(),
        ),
        out_specs=P("grp", None, "lat", "lon", None),
        check_vma=False,
    )
```

profile of v0, /device:TPU:25, one launch (start us, length us, event | category | flops | bytes accessed | tf_op | source)
XLA Modules:
  0.0 167.6 jit_solution(8205063492854376368)
XLA Ops:
  0.9 11.6 %collective-permute-start.2 = (bf16[2,3,12]{2,0,1:T(2,128)(2,1)S(1)}, bf16[2,3,12]{2,0,1:T(2,128)(2,1)S(1)}, u32[]{:S(2)}, u32[]{:S(2)}) collective-permute-start(bf16[2,3,12]{2,0,1:T(2,128)(2,1)S(1)} %slice.67), channel_id=1, source_target_pairs={{0,15},{1,0},{2,1},{3,2},{4,3},{5,4},{6,5},{7,6},{8,7},{9,8},{10,9... | collective-permute-start | bytes 440 | tf_op jit(solution)/shard_map/ppermute | solution.py:13
  13.8 2.2 %collective-permute-start = (bf16[3,2,3,12,512]{4,1,3,0,2:T(2,128)(2,1)S(1)}, bf16[3,2,3,12,512]{4,1,3,0,2:T(2,128)(2,1)S(1)}, u32[]{:S(2)}, u32[]{:S(2)}) collective-permute-start(bf16[3,2,3,12,512]{4,1,3,0,2:T(2,128)(2,1)S(1)} %copy.49), channel_id=1, source_target_pairs={{0,15},{1,0},{2,1},{3,2},{4,3},{5,4},{6,5},{7,6},{8,7},{9,8},{10,9... | collective-permute-start | bytes 663560 | tf_op jit(solution)/shard_map/ppermute | solution.py:13
  17.5 4.2 %collective-permute-done = bf16[3,2,3,12,512]{4,1,3,0,2:T(2,128)(2,1)S(1)} collective-permute-done((bf16[3,2,3,12,512]{4,1,3,0,2:T(2,128)(2,1)S(1)}, bf16[3,2,3,12,512]{4,1,3,0,2:T(2,128)(2,1)S(1)}, u32[]{:S(2)}, u32[]{:S(2)}) %collective-permute-start) | collective-permute-done | bytes 221216 | tf_op jit(solution)/shard_map/ppermute | solution.py:13
  23.2 1.8 %collective-permute-start.1 = (bf16[3,2,12,6,512]{4,1,3,0,2:T(2,128)(2,1)}, bf16[3,2,12,6,512]{4,1,3,0,2:T(2,128)(2,1)S(1)}, u32[]{:S(2)}, u32[]{:S(2)}) collective-permute-start(bf16[3,2,12,6,512]{4,1,3,0,2:T(2,128)(2,1)} %get-tuple-element.63), channel_id=1, source_target_pairs={{0,240},{16,0},{32,16},{48,32},{64,48},{80,64},{96,80},{112,96},{1... | collective-permute-start | bytes 1327112 | tf_op jit(solution)/shard_map/ppermute | solution.py:13
  26.8 6.8 %collective-permute-done.1 = bf16[3,2,12,6,512]{4,1,3,0,2:T(2,128)(2,1)S(1)} collective-permute-done((bf16[3,2,12,6,512]{4,1,3,0,2:T(2,128)(2,1)}, bf16[3,2,12,6,512]{4,1,3,0,2:T(2,128)(2,1)S(1)}, u32[]{:S(2)}, u32[]{:S(2)}) %collective-permute-start.1) | collective-permute-done | bytes 442400 | tf_op jit(solution)/shard_map/ppermute | solution.py:13
  33.6 2.1 %pad_maximum_fusion.1 = bf16[3,2,12,12,512]{4,1,3,0,2:T(2,128)(2,1)} fusion(bf16[3,2,12,6,512]{4,1,3,0,2:T(2,128)(2,1)S(1)} %collective-permute-done.1, bf16[3,2,12,6,512]{4,1,3,0,2:T(2,128)(2,1)S(1)} %get-tuple-element.62), kind=kLoop, calls=%fused_computation.39 | loop fusion | flops 442368 | bytes 1769472 | tf_op jit(solution)/shard_map/concatenate | solution.py:150
  35.7 3.7 %all-to-all-start = ((bf16[3,2,12,12,512]{4,1,3,0,2:T(2,128)(2,1)}), bf16[3,2,12,12,512]{4,1,3,0,2:T(2,128)(2,1)S(1)}, u32[]{:S(2)}, u32[]{:S(2)}) async-start(bf16[3,2,12,12,512]{4,1,3,0,2:T(2,128)(2,1)} %pad_maximum_fusion.1), calls=%async_computation | async-start | bytes 1769472 | tf_op jit(solution)/shard_map/all_to_all | solution.py:155
  39.8 11.5 %all-to-all-done = bf16[3,2,12,12,512]{4,1,3,0,2:T(2,128)(2,1)S(1)} async-done(((bf16[3,2,12,12,512]{4,1,3,0,2:T(2,128)(2,1)}), bf16[3,2,12,12,512]{4,1,3,0,2:T(2,128)(2,1)S(1)}, u32[]{:S(2)}, u32[]{:S(2)}) %all-to-all-start) | async-done | bytes 884768 | tf_op jit(solution)/shard_map/all_to_all | solution.py:155
  53.4 1.7 %copy.58 = f32[3,2,2,6,12,512]{5,4,3,1,0,2:T(8,128)} copy(bf16[3,2,2,6,12,512]{5,1,4,0,3,2:T(2,128)(2,1)S(1)} %bitcast.49) | data formatting | bytes 2654208 | tf_op jit(solution)/shard_map/convert_element_type | solution.py:29
  55.3 2.8 %reshape.243 = f32[864,512]{1,0:T(8,128)} reshape(f32[2,3,2,6,12,512]{5,4,3,2,1,0:T(8,128)} %bitcast.47) | data formatting | bytes 3538944 | tf_op jit(solution)/shard_map/convert_element_type | solution.py:29
  58.1 3.5 %fusion.19 = f32[864,1536]{1,0:T(8,128)S(1)} fusion(bf16[512,1536]{1,0:T(8,128)(2,1)} %param.10, f32[864,512]{1,0:T(8,128)} %reshape.243, f32[864]{0:T(1024)S(1)} %rsqrt.36, f32[864]{0:T(1024)S(1)} %div.40), kind=kOutput, calls=%fused_computation.38 | convolution fusion | flops 1360281600 | bytes 8657664 | tf_op jit(solution)/shard_map/dot_general | solution.py:30
  64.2 2.2 %slice_multiply_fusion = (f32[864,512]{1,0:T(8,128)}, f32[864,512]{1,0:T(8,128)}) fusion(f32[864,1536]{1,0:T(8,128)S(1)} %fusion.19), kind=kLoop, calls=%fused_computation.32 | loop fusion | flops 884736 | bytes 7077888 | tf_op jit(solution)/shard_map/mul | solution.py:23
  68.0 2.7 %copy.37 = f32[864,512]{0,1:T(8,128)} copy(f32[864,512]{1,0:T(8,128)} %get-tuple-element.58) | data formatting | bytes 3538944 | tf_op jit(solution)/shard_map/mul | solution.py:23
  73.8 2.8 %copy.38 = f32[864,512]{1,0:T(8,128)} copy(f32[864,512]{0,1:T(8,128)} %bitcast.50) | data formatting | bytes 3538944 | tf_op jit(solution)/shard_map/mul | solution.py:23
  76.6 2.7 %copy.34 = f32[864,512]{0,1:T(8,128)} copy(f32[864,512]{1,0:T(8,128)} %get-tuple-element.59) | data formatting | bytes 3538944 | tf_op jit(solution)/shard_map/mul | solution.py:23
  79.3 1.6 bitcast_reduce_fusion.1
  82.4 2.7 %copy.35 = f32[864,512]{1,0:T(8,128)} copy(f32[864,512]{0,1:T(8,128)} %bitcast.51) | data formatting | bytes 3538944 | tf_op jit(solution)/shard_map/mul | solution.py:23
  85.1 4.9 %multiply_convert_fusion = (bf16[864,512]{1,0:T(8,128)(2,1)}, bf16[864,512]{1,0:T(8,128)(2,1)}) fusion(f32[864,512]{1,0:T(8,128)} %copy.38, f32[864,1536]{1,0:T(8,128)} %copy-done.1, f32[864,512]{1,0:T(8,128)} %copy.35), kind=kLoop, calls=%fused_computation.29 | loop fusion | flops 1769472 | bytes 8847360 | tf_op jit(solution)/shard_map/convert_element_type | solution.py:24
  90.1 2.2 %copy.39 = bf16[864,512]{0,1:T(8,128)(2,1)} copy(bf16[864,512]{1,0:T(8,128)(2,1)} %get-tuple-element.56) | data formatting | bytes 1769472 | tf_op jit(solution)/shard_map/convert_element_type | solution.py:24
  92.3 2.2 %copy.36 = bf16[864,512]{0,1:T(8,128)(2,1)} copy(bf16[864,512]{1,0:T(8,128)(2,1)} %get-tuple-element.57) | data formatting | bytes 1769472 | tf_op jit(solution)/shard_map/convert_element_type | solution.py:24
  94.5 9.4 %convert_reduce_fusion = (f32[8,864]{1,0:T(8,128)S(1)}, bf16[8,864,864]{1,2,0:T(8,128)(2,1)S(1)}) fusion(f32[8,864]{1,0:T(8,128)S(1)} %add.97, f32[8]{0:T(128)S(1)} %broadcast_multiply_fusion.3, bf16[864,8,64]{0,2,1:T(8,128)(2,1)} %bitcast.56, bf16[864,8,64]{0,2,1:T(8,128)(2,1)} %bitcast.55, pred[864,864]{0,1:T(8,128)(4,1)} %broadcast_compare_fusion), kind=kOutput, calls=%fused_computation | convolution fusion | flops 800236800 | bytes 14515232 | tf_op jit(solution)/shard_map/while/body/eval_jaxpr/wqhd,wkhd->whqk/dot_general | solution.py:76
  103.9 2.2 %fusion.29 = f32[8,64,864]{2,1,0:T(8,128)S(1)} fusion(bf16[864,8,64]{0,2,1:T(8,128)(2,1)S(1)} %bitcast.53, bf16[8,864,864]{1,2,0:T(8,128)(2,1)S(1)} %get-tuple-element.67), kind=kOutput, calls=%fused_computation.65 | convolution fusion | flops 764411904 | bytes 14598144 | tf_op jit(solution)/shard_map/while/body/eval_jaxpr/whqk,wkhd->wqhd/dot_general | solution.py:83
  111.2 15.5 %all_to_all.27 = bf16[6,2,6,12,512]{4,1,3,2,0:T(2,128)(2,1)S(1)} all-to-all(bf16[6,2,6,12,512]{4,1,3,2,0:T(2,128)(2,1)S(1)} %copy.42), channel_id=1, replica_groups=mesh['grp'=2,'lon'=16,'lat'=16] {'grp'}, dimensions={0} | all-to-all | bytes 1769472 | tf_op jit(solution)/shard_map/all_to_all | solution.py:175
  127.6 3.1 %collective-permute-start.4 = (bf16[3,2,12,6,512]{4,1,3,2,0:T(2,128)(2,1)S(1)}, bf16[3,2,12,6,512]{4,1,3,2,0:T(2,128)(2,1)S(1)}, u32[]{:S(2)}, u32[]{:S(2)}) collective-permute-start(bf16[3,2,12,6,512]{4,1,3,2,0:T(2,128)(2,1)S(1)} %copy.44), channel_id=1, source_target_pairs={{0,16},{16,32},{32,48},{48,64},{64,80},{80,96},{96,112},{112,128},... | collective-permute-start | bytes 1327112 | tf_op jit(solution)/shard_map/ppermute | solution.py:13
  130.7 5.2 %collective-permute-done.4 = bf16[3,2,12,6,512]{4,1,3,2,0:T(2,128)(2,1)S(1)} collective-permute-done((bf16[3,2,12,6,512]{4,1,3,2,0:T(2,128)(2,1)S(1)}, bf16[3,2,12,6,512]{4,1,3,2,0:T(2,128)(2,1)S(1)}, u32[]{:S(2)}, u32[]{:S(2)}) %collective-permute-start.4) | collective-permute-done | bytes 442400 | tf_op jit(solution)/shard_map/ppermute | solution.py:13
  136.1 1.9 %collective-permute-start.5 = (bf16[3,2,3,12,512]{4,3,2,1,0:T(8,128)(2,1)S(1)}, bf16[3,2,3,12,512]{4,3,2,1,0:T(8,128)(2,1)S(1)}, u32[]{:S(2)}, u32[]{:S(2)}) collective-permute-start(bf16[3,2,3,12,512]{4,3,2,1,0:T(8,128)(2,1)S(1)} %pad_maximum_fusion.2), channel_id=1, source_target_pairs={{0,1},{1,2},{2,3},{3,4},{4,5},{5,6},{6,7},{7,8},{8,9},{9,10},{10,1... | collective-permute-start | bytes 663560 | tf_op jit(solution)/shard_map/ppermute | solution.py:13
  138.1 11.0 %collective-permute-done.5 = bf16[3,2,3,12,512]{4,3,2,1,0:T(8,128)(2,1)S(1)} collective-permute-done((bf16[3,2,3,12,512]{4,3,2,1,0:T(8,128)(2,1)S(1)}, bf16[3,2,3,12,512]{4,3,2,1,0:T(8,128)(2,1)S(1)}, u32[]{:S(2)}, u32[]{:S(2)}) %collective-permute-start.5) | collective-permute-done | bytes 221216 | tf_op jit(solution)/shard_map/ppermute | solution.py:13
  151.7 2.1 %reshape.241 = bf16[864,512]{1,0:T(8,128)(2,1)} reshape(bf16[3,2,12,12,512]{4,3,2,1,0:T(8,128)(2,1)} %fusion.13) | data formatting | bytes 1769472 | tf_op jit(solution)/shard_map/reshape | solution.py:185
  153.8 7.1 %fusion.8 = f32[864,512]{1,0:T(8,128)} fusion(bf16[2048,512]{1,0:T(8,128)(2,1)S(1)} %copy-done, bf16[864,512]{1,0:T(8,128)(2,1)} %reshape.241, bf16[512,2048]{1,0:T(8,128)(2,1)} %param.14), kind=kOutput, calls=%fused_computation.11 | convolution fusion | flops 3639803904 | bytes 6848512 | tf_op jit(solution)/shard_map/dot_general | solution.py:188
  160.9 2.7 %reshape.242 = f32[3,2,12,12,512]{4,3,2,1,0:T(8,128)} reshape(f32[864,512]{1,0:T(8,128)} %fusion.8) | data formatting | bytes 3538944 | tf_op jit(solution)/shard_map/reshape | solution.py:188
  163.6 2.1 %fusion.14 = bf16[3,2,12,12,512]{4,3,2,1,0:T(8,128)(2,1)S(1)} fusion(f32[3,2,12,12,512]{4,3,2,1,0:T(8,128)} %reshape.242, bf16[3,2,12,12,512]{4,3,2,1,0:T(8,128)(2,1)S(1)} %get-tuple-element.55), kind=kLoop, calls=%fused_computation.19 | loop fusion | flops 1327104 | bytes 3538944 | tf_op jit(solution)/shard_map/convert_element_type | solution.py:189
  165.7 1.8 %copy.46 = bf16[3,2,12,12,512]{4,1,3,2,0:T(2,128)(2,1)} copy(bf16[3,2,12,12,512]{4,3,2,1,0:T(8,128)(2,1)S(1)} %fusion.14) | data formatting | bytes 1769472 | tf_op jit(solution)/shard_map/convert_element_type | solution.py:189
  (66 shorter events, 26.7 us)
Async XLA Ops:
  0.0 153.8 %copy-start = (bf16[2048,512]{1,0:T(8,128)(2,1)S(1)}, bf16[2048,512]{1,0:T(8,128)(2,1)}, u32[]{:S(2)}) copy-start(bf16[2048,512]{1,0:T(8,128)(2,1)} %param.15) | copy-start | bytes 6291460
  0.0 17.5 %copy-start.5 = (f32[8]{0:T(128)S(1)}, f32[8]{0:T(128)}, u32[]{:S(2)}) copy-start(f32[8]{0:T(128)} %param.12) | copy-start | bytes 100
  0.9 25.8 %collective-permute-start.2 = (bf16[2,3,12]{2,0,1:T(2,128)(2,1)S(1)}, bf16[2,3,12]{2,0,1:T(2,128)(2,1)S(1)}, u32[]{:S(2)}, u32[]{:S(2)}) collective-permute-start(bf16[2,3,12]{2,0,1:T(2,128)(2,1)S(1)} %slice.67), channel_id=1, source_target_pairs={{0,15},{1,0},{2,1},{3,2},{4,3},{5,4},{6,5},{7,6},{8,7},{9,8},{10,9... | collective-permute-start | bytes 440 | tf_op jit(solution)/shard_map/ppermute | solution.py:13
  13.8 7.9 %collective-permute-start = (bf16[3,2,3,12,512]{4,1,3,0,2:T(2,128)(2,1)S(1)}, bf16[3,2,3,12,512]{4,1,3,0,2:T(2,128)(2,1)S(1)}, u32[]{:S(2)}, u32[]{:S(2)}) collective-permute-start(bf16[3,2,3,12,512]{4,1,3,0,2:T(2,128)(2,1)S(1)} %copy.49), channel_id=1, source_target_pairs={{0,15},{1,0},{2,1},{3,2},{4,3},{5,4},{6,5},{7,6},{8,7},{9,8},{10,9... | collective-permute-start | bytes 663560 | tf_op jit(solution)/shard_map/ppermute | solution.py:13
  23.2 10.4 %collective-permute-start.1 = (bf16[3,2,12,6,512]{4,1,3,0,2:T(2,128)(2,1)}, bf16[3,2,12,6,512]{4,1,3,0,2:T(2,128)(2,1)S(1)}, u32[]{:S(2)}, u32[]{:S(2)}) collective-permute-start(bf16[3,2,12,6,512]{4,1,3,0,2:T(2,128)(2,1)} %get-tuple-element.63), channel_id=1, source_target_pairs={{0,240},{16,0},{32,16},{48,32},{64,48},{80,64},{96,80},{112,96},{1... | collective-permute-start | bytes 1327112 | tf_op jit(solution)/shard_map/ppermute | solution.py:13
  25.3 14.2 %copy-start.3 = (f32[8]{0:T(128)S(1)}, f32[8]{0:T(128)}, u32[]{:S(2)}) copy-start(f32[8]{0:T(128)} %param.13) | copy-start | bytes 100
  26.8 12.6 %collective-permute-start.3 = (bf16[2,12,6]{2,0,1:T(2,128)(2,1)S(1)}, bf16[2,12,6]{2,0,1:T(2,128)(2,1)S(1)}, u32[]{:S(2)}, u32[]{:S(2)}) collective-permute-start(bf16[2,12,6]{2,0,1:T(2,128)(2,1)S(1)} %get-tuple-element.65), channel_id=1, source_target_pairs={{0,240},{16,0},{32,16},{48,32},{64,48},{80,64},{96,80},{112,96},{1... | collective-permute-start | bytes 872 | tf_op jit(solution)/shard_map/ppermute | solution.py:13
  35.7 15.6 %all-to-all-start = ((bf16[3,2,12,12,512]{4,1,3,0,2:T(2,128)(2,1)}), bf16[3,2,12,12,512]{4,1,3,0,2:T(2,128)(2,1)S(1)}, u32[]{:S(2)}, u32[]{:S(2)}) async-start(bf16[3,2,12,12,512]{4,1,3,0,2:T(2,128)(2,1)} %pad_maximum_fusion.1), calls=%async_computation | async-start | bytes 1769472 | tf_op jit(solution)/shard_map/all_to_all | solution.py:155
  61.6 2.6 %copy-start.1 = (f32[864,1536]{1,0:T(8,128)}, f32[864,1536]{1,0:T(8,128)S(1)}, u32[]{:S(2)}) copy-start(f32[864,1536]{1,0:T(8,128)S(1)} %fusion.19) | copy-start | bytes 15925252
  106.1 1.0 copy-start.4
  127.1 22.0 %copy-start.2 = (bf16[3,2,12,12,512]{4,1,3,2,0:T(2,128)(2,1)S(1)}, bf16[3,2,12,12,512]{4,1,3,2,0:T(2,128)(2,1)}, u32[]{:S(2)}) copy-start(bf16[3,2,12,12,512]{4,1,3,2,0:T(2,128)(2,1)} %param.8) | copy-start | bytes 2654212
  127.6 8.4 %collective-permute-start.4 = (bf16[3,2,12,6,512]{4,1,3,2,0:T(2,128)(2,1)S(1)}, bf16[3,2,12,6,512]{4,1,3,2,0:T(2,128)(2,1)S(1)}, u32[]{:S(2)}, u32[]{:S(2)}) collective-permute-start(bf16[3,2,12,6,512]{4,1,3,2,0:T(2,128)(2,1)S(1)} %copy.44), channel_id=1, source_target_pairs={{0,16},{16,32},{32,48},{48,64},{64,80},{80,96},{96,112},{112,128},... | collective-permute-start | bytes 1327112 | tf_op jit(solution)/shard_map/ppermute | solution.py:13
  136.1 12.9 %collective-permute-start.5 = (bf16[3,2,3,12,512]{4,3,2,1,0:T(8,128)(2,1)S(1)}, bf16[3,2,3,12,512]{4,3,2,1,0:T(8,128)(2,1)S(1)}, u32[]{:S(2)}, u32[]{:S(2)}) collective-permute-start(bf16[3,2,3,12,512]{4,3,2,1,0:T(8,128)(2,1)S(1)} %pad_maximum_fusion.2), channel_id=1, source_target_pairs={{0,1},{1,2},{2,3},{3,4},{4,5},{5,6},{6,7},{7,8},{8,9},{9,10},{10,1... | collective-permute-start | bytes 663560 | tf_op jit(solution)/shard_map/ppermute | solution.py:13
where the time goes:
time: 168 us
  local copies, waits for them, and re-layouts  42.9 us (26%)
  waiting for transfers between devices  38.7 us (23%)
  starting transfers between devices  24.4 us (15%)
  matrix products  23.8 us (14%)
  other arithmetic  22 us (13%)
  blocking collectives  15.5 us (9%)
    ppermute x6, waiting for transfers between devices, passed_along(): lax.ppermute(array, axis, [(i, (i + by) % count) for i in range(count)])  27.2 us
    ppermute x6, starting transfers between devices, passed_along(): lax.ppermute(array, axis, [(i, (i + by) % count) for i in range(count)])  20.6 us
    all_to_all x1, blocking collectives, per_device(): lax.all_to_all(project_out(attended, w_out), 'grp', split_axis=0, concat_...  15.5 us
    all_to_all x1, waiting for transfers between devices, per_device(): lax.all_to_all(rolled, 'grp', split_axis=2, concat_axis=0, tiled=True)  11.5 us
    dot_general x1, matrix products, window_terms(): jnp.einsum('wqhd,wkhd->whqk', query_heads, key_heads, preferred_element_t...  9.39 us
    mul x4, local copies, waits for them, and re-layouts, unit_heads(): shaped * lax.rsqrt(jnp.mean(shaped * shaped, -1, keepdims=True) + 1e-06)  8.33 us
    dot_general x1, matrix products, per_device(): jnp.dot(hidden, w_down, preferred_element_type=jnp.float32)  7.14 us
    mul x2, local copies, waits for them, and re-layouts, unit_heads(): shaped * shaped  5.49 us
  transfers between devices with their start and end apart: 7, of which 5 were waited for; matrix products, arithmetic and copies ran while one was open for 5% of the time, Pallas kernels for 0%

commit v1 on v0

v1 whole, which is shorter than its diff:
```python
import functools

import jax
import jax.numpy as jnp
from jax import lax
from jax.experimental import pallas as pl
from jax.experimental.pallas import tpu as pltpu
from jax.sharding import PartitionSpec as P

LANES = 128
SH_LAT = 3
SH_LON = 6
WLAT = 6
LOG2E = 1.4426950408889634
EXCLUDED = -1e30
VMEM = pl.BlockSpec(memory_space=pltpu.VMEM)
SMEM = pl.BlockSpec(memory_space=pltpu.SMEM)


def to_pairs(fields):
    groups, levels, lat_rows, lon_cells, width = fields.shape
    cells = jnp.transpose(fields, (0, 2, 3, 1, 4))
    cells = cells.reshape(groups, lat_rows, lon_cells, levels, width // LANES, LANES)
    cells = jnp.transpose(cells, (0, 1, 2, 4, 3, 5))
    return cells.reshape(groups, lat_rows, lon_cells, levels * (width // LANES), LANES)


def from_pairs(cells, levels):
    groups, lat_rows, lon_cells, rows, lanes = cells.shape
    cells = cells.reshape(groups, lat_rows, lon_cells, rows // levels, levels, lanes)
    cells = jnp.transpose(cells, (0, 1, 2, 4, 3, 5))
    cells = cells.reshape(groups, lat_rows, lon_cells, levels, (rows // levels) * lanes)
    return jnp.transpose(cells, (0, 3, 1, 2, 4))


def shifted(array, axes, by):
    if isinstance(axes, str):
        count = lax.axis_size(axes)
        return lax.ppermute(array, axes, [(i, (i + by) % count) for i in range(count)])
    outer, inner = (lax.axis_size(axis) for axis in axes)
    pairs = [
        (i * inner + j, ((i + by) % outer) * inner + (j + by) % inner)
        for i in range(outer)
        for j in range(inner)
    ]
    return lax.ppermute(array, axes, pairs)


def cells_to_tokens(pieces, cells_scr, tokens_scr, row):
    count = 0
    for piece in pieces:
        size = piece.shape[0]
        cells_scr[count * 8 : (count + size) * 8, :] = piece.reshape(size * 8, LANES).astype(
            jnp.float32
        )
        count += size
    for level in range(2):
        for tile in range(4):
            tokens_scr[tile, row + level * count : row + (level + 1) * count, :] = cells_scr[
                pl.ds(2 * tile + level, count, stride=8), :
            ]


def tokens_to_cells(tokens_scr, row, count, cells_scr):
    for level in range(2):
        for tile in range(4):
            cells_scr[pl.ds(2 * tile + level, count, stride=8), :] = tokens_scr[
                tile, row + level * count : row + (level + 1) * count, :
            ]


def whole_rows(tokens_scr):
    return jnp.concatenate([tokens_scr[tile] for tile in range(4)], axis=1)


def layer_norm(values):
    centred = values - jnp.mean(values, -1, keepdims=True)
    return centred * lax.rsqrt(jnp.mean(centred * centred, -1, keepdims=True) + 1e-05)


def head_squares(values, head_size):
    width = 256
    rows = lax.broadcasted_iota(jnp.int32, (width, width), 0) // head_size
    cols = lax.broadcasted_iota(jnp.int32, (width, width), 1) // head_size
    averaging = jnp.where(rows == cols, 1.0 / head_size, 0.0).astype(jnp.bfloat16)
    squares = (values * values).astype(jnp.bfloat16)
    return jnp.concatenate(
        [
            jnp.dot(
                squares[:, at : at + width], averaging, preferred_element_type=jnp.float32
            )
            for at in range(0, values.shape[1], width)
        ],
        axis=1,
    )


def unit_heads(values, head_size):
    return values * lax.rsqrt(head_squares(values, head_size) + 1e-06)


def load_window_cells(own, east, south, corner, cells_scr, tokens_scr):
    cells_to_tokens([own[0:108]], cells_scr, tokens_scr, 0)
    cells_to_tokens([east[0:108]], cells_scr, tokens_scr, 216)
    cells_to_tokens([own[108:162], east[108:162]], cells_scr, tokens_scr, 432)
    cells_to_tokens([south[0:54], corner[0:54]], cells_scr, tokens_scr, 648)


def attend(query_ref, key_ref, value_ref, rows_ref, bias_ref, head_size, store):
    half = rows_ref.shape[1]
    lane = lax.broadcasted_iota(jnp.int32, (half, LANES), 1)

    def one(step, carry):
        window = step // 4
        pair = step % 4
        base = pl.multiple_of(window * half, 16)
        at = pl.multiple_of(pair * LANES, LANES)
        queries = query_ref[pl.ds(base, half), pl.ds(at, LANES)]
        keys = key_ref[pl.ds(base, half), pl.ds(at, LANES)]
        values = value_ref[pl.ds(base, half), pl.ds(at, LANES)]
        marks = rows_ref[pl.ds(window, 1), :]
        first = rows_ref[pl.ds(2 + window, 1), :]
        second = rows_ref[pl.ds(4 + window, 1), :]
        total = None
        for side in range(2):
            mine = (lane < head_size) if side == 0 else (lane >= head_size)
            scores = lax.dot_general(
                queries,
                jnp.where(mine, keys, jnp.zeros_like(keys)),
                (((1,), (1,)), ((), ())),
                preferred_element_type=jnp.float32,
            )
            bias = marks * bias_ref[2 * pair + side]
            scores = jnp.concatenate(
                [scores[: half // 2] + (bias + first), scores[half // 2 :] + (bias + second)], 0
            )
            weights = jnp.exp2(scores).astype(jnp.bfloat16)
            operand = jnp.concatenate(
                [
                    jnp.where(mine, values, jnp.zeros_like(values)),
                    jnp.where(mine, 1.0, 0.0).astype(jnp.bfloat16),
                ],
                axis=1,
            )
            part = jnp.dot(weights, operand, preferred_element_type=jnp.float32)
            total = part if total is None else total + part
        store(window, pair, base, at, total)
        return carry

    lax.fori_loop(0, 8, one, 0)


def own_kernel(
    head_size,
    own,
    east,
    south,
    corner,
    w_qkv,
    scale,
    rows_ref,
    bias_ref,
    query_out,
    total_out,
    cells_scr,
    tokens_scr,
    key_scr,
    value_scr,
):
    load_window_cells(own, east, south, corner, cells_scr, tokens_scr)
    width = w_qkv.shape[0]
    normed = layer_norm(whole_rows(tokens_scr)).astype(jnp.bfloat16)
    mixed = jnp.dot(normed, w_qkv[:, :width], preferred_element_type=jnp.float32)
    query_out[...] = (unit_heads(mixed, head_size) * scale[...]).astype(jnp.bfloat16)
    mixed = jnp.dot(normed, w_qkv[:, width : 2 * width], preferred_element_type=jnp.float32)
    key_scr[...] = unit_heads(mixed, head_size).astype(jnp.bfloat16)
    value_scr[...] = jnp.dot(
        normed, w_qkv[:, 2 * width :], preferred_element_type=jnp.float32
    ).astype(jnp.bfloat16)

    def store(window, pair, base, at, total):
        total_out[pair, pl.ds(base, total.shape[0]), :] = total

    attend(query_out, key_scr, value_scr, rows_ref, bias_ref, head_size, store)


def partner_kernel(
    head_size,
    own,
    rest,
    query_ref,
    total_in,
    w_kv,
    w_out,
    rows_ref,
    bias_ref,
    own_out,
    east_out,
    south_out,
    corner_out,
    cells_scr,
    tokens_scr,
    key_scr,
    value_scr,
    attended_scr,
):
    load_window_cells(
        own, rest.at[0:162], rest.at[162:216], rest.at[216:270], cells_scr, tokens_scr
    )
    width = w_kv.shape[0]
    normed = layer_norm(whole_rows(tokens_scr)).astype(jnp.bfloat16)
    mixed = jnp.dot(normed, w_kv[:, width : 2 * width], preferred_element_type=jnp.float32)
    key_scr[...] = unit_heads(mixed, head_size).astype(jnp.bfloat16)
    value_scr[...] = jnp.dot(
        normed, w_kv[:, 2 * width :], preferred_element_type=jnp.float32
    ).astype(jnp.bfloat16)

    def store(window, pair, base, at, total):
        span = pl.ds(base, total.shape[0])
        total = total + total_in[pair, span, :]
        attended_scr[span, pl.ds(at, LANES)] = (total[:, :LANES] / total[:, LANES:]).astype(
            jnp.bfloat16
        )

    attend(query_ref, key_scr, value_scr, rows_ref, bias_ref, head_size, store)
    projected = jnp.dot(attended_scr[...], w_out[...], preferred_element_type=jnp.float32)
    for tile in range(4):
        tokens_scr[tile] = projected[:, tile * LANES : (tile + 1) * LANES]

    def put(row, count, outs):
        tokens_to_cells(tokens_scr, row, count, cells_scr)
        at = 0
        for out, first, size in outs:
            out[first : first + size] = (
                cells_scr[at * 8 : (at + size) * 8, :].astype(jnp.bfloat16).reshape(size, 8, LANES)
            )
            at += size

    put(0, 108, [(own_out, 0, 108)])
    put(216, 108, [(east_out, 0, 108)])
    put(432, 108, [(own_out, 108, 54), (east_out, 108, 54)])
    put(648, 108, [(south_out, 0, 54), (corner_out, 0, 54)])


def joining_kernel(
    fields, own, west, north, corner, w_up, w_down, out, cells_scr, tokens_scr, normed_scr, chunk
):
    groups = fields.shape[0]

    def add(g, lats, lons, piece, first, shape):
        size = shape[0] * shape[1]
        term = piece[first + g * size : first + (g + 1) * size].astype(jnp.float32)
        term = term.reshape(shape + (8, LANES))
        summed = fields[g, lats[0] : lats[1], lons[0] : lons[1]].astype(jnp.float32) + term
        cells_scr[g, lats[0] : lats[1], lons[0] : lons[1]] = summed.astype(jnp.bfloat16).astype(
            jnp.float32
        )

    for g in range(groups):
        for lons, big, small in (((6, 12), own, north), ((0, 6), west, corner)):
            add(g, (3, 9), lons, big, 0, (6, 6))
            add(g, (9, 12), lons, big, 108, (3, 6))
            add(g, (0, 3), lons, small, 0, (3, 6))
    cells = groups * 144
    flat = cells_scr.reshape(cells * 8, LANES)
    for level in range(2):
        for tile in range(4):
            tokens_scr[level * cells : (level + 1) * cells, tile * LANES : (tile + 1) * LANES] = (
                flat[pl.ds(2 * tile + level, cells, stride=8), :]
            )
    normed_scr[...] = layer_norm(tokens_scr[...]).astype(jnp.bfloat16)

    def one(step, carry):
        span = pl.ds(pl.multiple_of(step * chunk, 16), chunk)
        hidden = jnp.dot(normed_scr[span, :], w_up[...], preferred_element_type=jnp.float32)
        hidden = jax.nn.gelu(hidden, approximate=True).astype(jnp.bfloat16)
        tokens_scr[span, :] = tokens_scr[span, :] + jnp.dot(
            hidden, w_down[...], preferred_element_type=jnp.float32
        )
        return carry

    lax.fori_loop(0, 2 * cells // chunk, one, 0)
    for level in range(2):
        for tile in range(4):
            flat[pl.ds(2 * tile + level, cells, stride=8), :] = tokens_scr[
                level * cells : (level + 1) * cells, tile * LANES : (tile + 1) * LANES
            ]
    out[...] = cells_scr[...].astype(jnp.bfloat16)


def mark_rows(own, east, south, corner, groups, last_band):
    def part(marks, lats, lons):
        block = marks[:, lats[0] : lats[1], lons[0] : lons[1]].reshape(2, 1, -1)
        return jnp.broadcast_to(block, (2, groups, block.shape[2])).reshape(2, -1)

    upper = jnp.concatenate(
        [part(own, (3, 9), (6, 12)).reshape(-1), part(east, (3, 9), (0, 6)).reshape(-1)]
    )
    lower = jnp.concatenate(
        [
            jnp.concatenate([part(own, (9, 12), (6, 12)), part(east, (9, 12), (0, 6))], 1).reshape(-1),
            jnp.concatenate([part(south, (0, 3), (6, 12)), part(corner, (0, 3), (0, 6))], 1).reshape(-1),
        ]
    )
    keys = upper.shape[0]
    later = jnp.arange(keys) >= keys // 2
    none = jnp.zeros((keys,), jnp.float32)
    out_first = jnp.where(last_band & later, EXCLUDED, 0.0)
    out_second = jnp.where(last_band & ~later, EXCLUDED, 0.0)
    return jnp.stack([upper, lower, none, out_first, none, out_second, none, none])


def per_device(fields, surface_mask, w_qkv, w_out, logit_scale, mask_bias, w_up, w_down):
    groups, levels, lat_rows, lon_cells, width = fields.shape
    heads = logit_scale.shape[0]
    head_size = width // heads
    tokens = groups * levels * lat_rows * lon_cells
    cells = to_pairs(fields)
    tile = (8, LANES)
    flags = surface_mask.reshape(-1).astype(jnp.bfloat16)
    flags = jnp.pad(flags, (0, 8 * LANES - flags.shape[0])).reshape((1,) + tile)

    def piece(lats, lons):
        return cells[:, lats[0] : lats[1], lons[0] : lons[1]].reshape((-1,) + tile)

    own = jnp.concatenate([piece((3, 9), (6, 12)), piece((9, 12), (6, 12))])
    east = jnp.concatenate([piece((3, 9), (0, 6)), piece((9, 12), (0, 6)), flags])
    south = jnp.concatenate([piece((0, 3), (6, 12)), flags])
    corner = jnp.concatenate([piece((0, 3), (0, 6)), flags])
    east = shifted(east, "lon", -1)
    south = shifted(south, "lat", -1)
    corner = shifted(corner, ("lon", "lat"), -1)
    own_across = shifted(own, "grp", 1)
    rest_across = shifted(jnp.concatenate([east[:162], south[:54], corner[:54]]), "grp", 1)

    def marks_of(received):
        flat = received.reshape(-1)[: levels * lat_rows * lon_cells].astype(jnp.float32)
        return flat.reshape(levels, lat_rows, lon_cells)

    last_band = lax.axis_index("lat") == lax.axis_size("lat") - 1
    rows = mark_rows(
        surface_mask.astype(jnp.float32),
        marks_of(east[162]),
        marks_of(south[54]),
        marks_of(corner[54]),
        groups,
        last_band,
    )
    scale = jnp.repeat(logit_scale * (LOG2E / head_size), head_size)[None]
    bias = mask_bias * LOG2E
    half_cells = groups * lat_rows * lon_cells // 4
    scratch = [
        pltpu.VMEM((half_cells * 8, LANES), jnp.float32),
        pltpu.VMEM((4, tokens, LANES), jnp.float32),
        pltpu.VMEM((tokens, width), jnp.bfloat16),
        pltpu.VMEM((tokens, width), jnp.bfloat16),
    ]
    queries, totals = pl.pallas_call(
        functools.partial(own_kernel, head_size),
        name="own",
        out_shape=(
            jax.ShapeDtypeStruct((tokens, width), jnp.bfloat16),
            jax.ShapeDtypeStruct((4, tokens, 2 * LANES), jnp.float32),
        ),
        in_specs=[VMEM] * 7 + [SMEM],
        out_specs=(VMEM, VMEM),
        scratch_shapes=scratch,
        cost_estimate=pl.CostEstimate(
            flops=6 * 10**9, bytes_accessed=8 * 10**6, transcendentals=3 * 10**6
        ),
    )(own, east, south, corner, w_qkv, scale, rows, bias)
    shapes = [jax.ShapeDtypeStruct((n,) + tile, jnp.bfloat16) for n in (162, 162, 54, 54)]
    own, east, south, corner = pl.pallas_call(
        functools.partial(partner_kernel, head_size),
        name="partner",
        out_shape=shapes,
        in_specs=[VMEM] * 7 + [SMEM],
        out_specs=[VMEM] * 4,
        scratch_shapes=scratch + [pltpu.VMEM((tokens, width), jnp.bfloat16)],
        cost_estimate=pl.CostEstimate(
            flops=6 * 10**9, bytes_accessed=8 * 10**6, transcendentals=3 * 10**6
        ),
    )(own_across, rest_across, queries, totals, w_qkv, w_out, rows, bias)
    east = shifted(east, "lon", 1)
    south = shifted(south, "lat", 1)
    corner = shifted(corner, ("lon", "lat"), 1)
    joined = pl.pallas_call(
        functools.partial(joining_kernel, chunk=288),
        name="joining",
        out_shape=jax.ShapeDtypeStruct(cells.shape, jnp.bfloat16),
        in_specs=[VMEM] * 7,
        out_specs=VMEM,
        scratch_shapes=[
            pltpu.VMEM(cells.shape, jnp.float32),
            pltpu.VMEM((tokens, width), jnp.float32),
            pltpu.VMEM((tokens, width), jnp.bfloat16),
        ],
        cost_estimate=pl.CostEstimate(
            flops=4 * 10**9, bytes_accessed=8 * 10**6, transcendentals=2 * 10**6
        ),
    )(cells, own, east, south, corner, w_up, w_down)
    return from_pairs(joined, levels)


def solution(mesh):
    return jax.shard_map(
        per_device,
        mesh=mesh,
        in_specs=(
            P("grp", None, "lat", "lon", None),
            P(None, "lat", "lon"),
            P(),
            P(),
            P(),
            P(),
            P(),
            P(),
        ),
        out_specs=P("grp", None, "lat", "lon", None),
        check_vma=False,
    )
```

time: 168 us -> 86.7 us (0.52)
  the two profiles are of different devices: /device:TPU:25 before, /device:TPU:4 now
where the time goes in v1:
time: 86.7 us; the launch traced here: 86.3 us
  Pallas kernels  38.5 us (44%)
  starting transfers between devices  29.9 us (34%)
  waiting for transfers between devices  8.58 us (10%)
  local copies, waits for them, and re-layouts  7.12 us (8%)
  other arithmetic  1.91 us (2%)
    ppermute x6, starting transfers between devices, shifted(): lax.ppermute(array, axes, [(i, (i + by) % count) for i in range(count)])  23.2 us
    pallas_call x1, Pallas kernels, per_device(): pl.pallas_call(functools.partial(partner_kernel, head_size), name='partne...  14.6 us
    pallas_call x1, Pallas kernels, per_device(): pl.pallas_call(functools.partial(own_kernel, head_size), name='own', out_...  13.8 us
    pallas_call x1, Pallas kernels, per_device(): pl.pallas_call(functools.partial(joining_kernel, chunk=288), name='joinin...  10 us
    ppermute x2, starting transfers between devices, shifted(): return lax.ppermute(array, axes, pairs)  6.72 us
    ppermute x2, waiting for transfers between devices, shifted(): return lax.ppermute(array, axes, pairs)  4.65 us
    ppermute x6, waiting for transfers between devices, shifted(): lax.ppermute(array, axes, [(i, (i + by) % count) for i in range(count)])  3.93 us
    slice x2, local copies, waits for them, and re-layouts, piece(): return cells[:, lats[0]:lats[1], lons[0]:lons[1]].reshape((-1,) + tile)  2.2 us
  transfers between devices with their start and end apart: 8, of which 2 were waited for; matrix products, arithmetic and copies ran while one was open for 6% of the time, Pallas kernels for 16%

profile of v1, /device:TPU:4, one launch (start us, length us, event | category | flops | bytes accessed | tf_op | source)
XLA Modules:
  0.0 86.3 jit_solution(6330981165943338026)
XLA Ops:
  0.0 1.1 %fusion.1 = (bf16[3,3,6,8,128]{4,3,2,1,0:T(8,128)(2,1)S(1)}, bf16[3,3,6,8,128]{4,3,2,1,0:T(8,128)(2,1)S(1)}, bf16[3,3,6,8,128]{4,3,2,1,0:T(8,128)(2,1)S(1)}, bf16[3,3,6,8,128]{4,3,2,1,0:T(8,128)(2,1)S(1)}) fusion(bf16[3,12,12,8,128]{4,3,2,1,0:T(8,128)(2,1)} %bitcast.30), kind=kLoop, calls=%fused_computation.21 | loop fusion | bytes 884736 | tf_op jit(solution)/shard_map/slice | solution.py:324
  1.1 0.8 fusion.2
  1.9 0.1 convert_element_type.29
  2.1 11.6 %collective-permute-start.2 = (bf16[55,8,128]{2,1,0:T(8,128)(2,1)S(1)}, bf16[55,8,128]{2,1,0:T(8,128)(2,1)S(1)}, u32[]{:S(2)}, u32[]{:S(2)}) collective-permute-start(bf16[55,8,128]{2,1,0:T(8,128)(2,1)S(1)} %get-tuple-element.25), channel_id=1, source_target_pairs={{0,15},{1,0},{2,1},{3,2},{4,3},{5,4},{6,5},{7,6},{8,7},{9,8},{10,9... | collective-permute-start | bytes 337928 | tf_op jit(solution)/shard_map/ppermute | solution.py:39
  13.7 4.8 %collective-permute-start.3 = (bf16[55,8,128]{2,1,0:T(8,128)(2,1)S(1)}, bf16[55,8,128]{2,1,0:T(8,128)(2,1)S(1)}, u32[]{:S(2)}, u32[]{:S(2)}) collective-permute-start(bf16[55,8,128]{2,1,0:T(8,128)(2,1)S(1)} %get-tuple-element.26), channel_id=1, source_target_pairs={{0,255},{1,240},{2,241},{3,242},{4,243},{5,244},{6,245},{7,246},{8... | collective-permute-start | bytes 337928 | tf_op jit(solution)/shard_map/ppermute | solution.py:46
  18.5 1.1 %fusion = (bf16[3,6,6,8,128]{4,3,2,1,0:T(8,128)(2,1)S(1)}, bf16[3,6,6,8,128]{4,3,2,1,0:T(8,128)(2,1)S(1)}) fusion(bf16[3,12,12,8,128]{4,3,2,1,0:T(8,128)(2,1)} %bitcast.31), kind=kLoop, calls=%fused_computation.20 | loop fusion | bytes 884736 | tf_op jit(solution)/shard_map/slice | solution.py:324
  19.6 1.1 %collective-permute-start.1 = (bf16[163,8,128]{2,1,0:T(8,128)(2,1)S(1)}, bf16[163,8,128]{2,1,0:T(8,128)(2,1)S(1)}, u32[]{:S(2)}, u32[]{:S(2)}) collective-permute-start(bf16[163,8,128]{2,1,0:T(8,128)(2,1)S(1)} %pad_maximum_fusion.1), channel_id=1, source_target_pairs={{0,240},{16,0},{32,16},{48,32},{64,48},{80,64},{96,80},{112,96},{1... | collective-permute-start | bytes 1001480 | tf_op jit(solution)/shard_map/ppermute | solution.py:39
  20.8 2.4 %collective-permute-start = (bf16[162,8,128]{2,1,0:T(8,128)(2,1)S(1)}, bf16[162,8,128]{2,1,0:T(8,128)(2,1)S(1)}, u32[]{:S(2)}, u32[]{:S(2)}) collective-permute-start(bf16[162,8,128]{2,1,0:T(8,128)(2,1)S(1)} %pad_maximum_fusion.2.own), channel_id=1, source_target_pairs={{0,256},{256,0},{1,257},{257,1},{2,258},{258,2},{3,259},{259,3},{4... | collective-permute-start | bytes 995336 | tf_op jit(solution)/shard_map/ppermute | solution.py:39
  23.3 0.1 broadcast_in_dim.64
  23.4 0.1 reshape.109
  23.5 0.6 broadcast_multiply_fusion.bias_ref
  24.3 0.7 broadcast_in_dim_reshape.3.scale
  25.1 0.1 convert_element_type.33
  25.2 0.1 reshape.118
  25.3 0.1 reshape.112
  25.4 0.1 convert_element_type.34
  25.6 0.1 reshape.113
  25.8 0.1 reshape.114
  26.0 0.1 reshape.117
  26.7 4.9 %collective-permute-start.4 = (bf16[270,8,128]{2,1,0:T(8,128)(2,1)S(1)}, bf16[270,8,128]{2,1,0:T(8,128)(2,1)S(1)}, u32[]{:S(2)}, u32[]{:S(2)}) collective-permute-start(bf16[270,8,128]{2,1,0:T(8,128)(2,1)S(1)} %pad_maximum_fusion), channel_id=1, source_target_pairs={{0,256},{256,0},{1,257},{257,1},{2,258},{258,2},{3,259},{259,3},{4... | collective-permute-start | bytes 1658888 | tf_op jit(solution)/shard_map/ppermute | solution.py:39
  31.8 0.6 stack.17.rows_ref
  32.5 13.8 %own.1 = (bf16[864,512]{1,0:T(8,128)(2,1)}, f32[4,864,256]{2,1,0:T(8,128)}) custom-call(bf16[162,8,128]{2,1,0:T(8,128)(2,1)} %copy-done.1, bf16[163,8,128]{2,1,0:T(8,128)(2,1)} %copy-done, bf16[55,8,128]{2,1,0:T(8,128)(2,1)} %copy-done.2, bf16[55,8,128]{2,1,0:T(8,128)(2,1)} %copy-done.3, bf16[512,1536]{1,0:T(8,128)(2,1)} %w_kv.1, ...), custom_call_target="tpu_custom_call" | custom-call | flops 6000000000 | bytes 8000000 | tf_op jit(solution)/shard_map/own/pallas_call | solution.py:358
  46.3 0.7 copy-done.5
  47.0 0.2 copy-done.4
  47.2 14.6 %partner.1 = (bf16[162,8,128]{2,1,0:T(8,128)(2,1)}, bf16[162,8,128]{2,1,0:T(8,128)(2,1)}, bf16[54,8,128]{2,1,0:T(8,128)(2,1)}, bf16[54,8,128]{2,1,0:T(8,128)(2,1)}) custom-call(bf16[162,8,128]{2,1,0:T(8,128)(2,1)} %copy-done.5, bf16[270,8,128]{2,1,0:T(8,128)(2,1)} %copy-done.4, bf16[864,512]{1,0:T(8,128)(2,1)} %get-tuple-element.11.query_ref, ...), custom_call_target="tpu_custom_call" | custom-call | flops 6000000000 | bytes 8000000 | tf_op jit(solution)/shard_map/partner/pallas_call | solution.py:373
  61.9 3.1 %collective-permute-start.6 = (bf16[54,8,128]{2,1,0:T(8,128)(2,1)}, bf16[54,8,128]{2,1,0:T(8,128)(2,1)S(1)}, u32[]{:S(2)}, u32[]{:S(2)}) collective-permute-start(bf16[54,8,128]{2,1,0:T(8,128)(2,1)} %get-tuple-element.15), channel_id=1, source_target_pairs={{0,1},{1,2},{2,3},{3,4},{4,5},{5,6},{6,7},{7,8},{8,9},{9,10},{10,1... | collective-permute-start | bytes 331784 | tf_op jit(solution)/shard_map/ppermute | solution.py:39
  65.0 1.9 %collective-permute-start.7 = (bf16[54,8,128]{2,1,0:T(8,128)(2,1)}, bf16[54,8,128]{2,1,0:T(8,128)(2,1)S(1)}, u32[]{:S(2)}, u32[]{:S(2)}) collective-permute-start(bf16[54,8,128]{2,1,0:T(8,128)(2,1)} %get-tuple-element.16), channel_id=1, source_target_pairs={{0,17},{1,18},{2,19},{3,20},{4,21},{5,22},{6,23},{7,24},{8,25},{9,... | collective-permute-start | bytes 331784 | tf_op jit(solution)/shard_map/ppermute | solution.py:46
  66.9 3.9 %collective-permute-done.6.north = bf16[54,8,128]{2,1,0:T(8,128)(2,1)S(1)} collective-permute-done((bf16[54,8,128]{2,1,0:T(8,128)(2,1)}, bf16[54,8,128]{2,1,0:T(8,128)(2,1)S(1)}, u32[]{:S(2)}, u32[]{:S(2)}) %collective-permute-start.6) | collective-permute-done | bytes 110624 | tf_op jit(solution)/shard_map/ppermute | solution.py:39
  70.8 4.7 %collective-permute-done.7.corner = bf16[54,8,128]{2,1,0:T(8,128)(2,1)S(1)} collective-permute-done((bf16[54,8,128]{2,1,0:T(8,128)(2,1)}, bf16[54,8,128]{2,1,0:T(8,128)(2,1)S(1)}, u32[]{:S(2)}, u32[]{:S(2)}) %collective-permute-start.7) | collective-permute-done | bytes 110624 | tf_op jit(solution)/shard_map/ppermute | solution.py:46
  75.5 0.6 copy-done.8
  76.1 0.1 copy-done.6
  76.3 10.0 %joining.1 = bf16[3,12,12,8,128]{4,3,2,1,0:T(8,128)(2,1)} custom-call(bf16[3,12,12,8,128]{4,3,2,1,0:T(8,128)(2,1)} %bitcast.32, bf16[162,8,128]{2,1,0:T(8,128)(2,1)} %get-tuple-element.13.own, bf16[162,8,128]{2,1,0:T(8,128)(2,1)} %copy-done.6, bf16[54,8,128]{2,1,0:T(8,128)(2,1)} %copy-done.7, bf16[54,8,128]{2,1,0:T(8,128)(2,1)} %copy-done.8, ...), custom_call_target="tpu_custom_call" | custom-call | flops 4000000000 | bytes 8000000 | tf_op jit(solution)/shard_map/joining/pallas_call | solution.py:387
  (71 shorter events, 1.6 us)
Async XLA Ops:
  0.0 23.5 %copy-start.9 = (f32[8]{0:T(128)S(1)}, f32[8]{0:T(128)}, u32[]{:S(2)}) copy-start(f32[8]{0:T(128)} %param.13) | copy-start | bytes 100
  0.0 24.1 %copy-start.10 = (f32[8]{0:T(128)S(1)}, f32[8]{0:T(128)}, u32[]{:S(2)}) copy-start(f32[8]{0:T(128)} %param.12) | copy-start | bytes 100
  2.1 23.0 %collective-permute-start.2 = (bf16[55,8,128]{2,1,0:T(8,128)(2,1)S(1)}, bf16[55,8,128]{2,1,0:T(8,128)(2,1)S(1)}, u32[]{:S(2)}, u32[]{:S(2)}) collective-permute-start(bf16[55,8,128]{2,1,0:T(8,128)(2,1)S(1)} %get-tuple-element.25), channel_id=1, source_target_pairs={{0,15},{1,0},{2,1},{3,2},{4,3},{5,4},{6,5},{7,6},{8,7},{9,8},{10,9... | collective-permute-start | bytes 337928 | tf_op jit(solution)/shard_map/ppermute | solution.py:39
  13.7 11.8 %collective-permute-start.3 = (bf16[55,8,128]{2,1,0:T(8,128)(2,1)S(1)}, bf16[55,8,128]{2,1,0:T(8,128)(2,1)S(1)}, u32[]{:S(2)}, u32[]{:S(2)}) collective-permute-start(bf16[55,8,128]{2,1,0:T(8,128)(2,1)S(1)} %get-tuple-element.26), channel_id=1, source_target_pairs={{0,255},{1,240},{2,241},{3,242},{4,243},{5,244},{6,245},{7,246},{8... | collective-permute-start | bytes 337928 | tf_op jit(solution)/shard_map/ppermute | solution.py:46
  19.6 6.3 %collective-permute-start.1 = (bf16[163,8,128]{2,1,0:T(8,128)(2,1)S(1)}, bf16[163,8,128]{2,1,0:T(8,128)(2,1)S(1)}, u32[]{:S(2)}, u32[]{:S(2)}) collective-permute-start(bf16[163,8,128]{2,1,0:T(8,128)(2,1)S(1)} %pad_maximum_fusion.1), channel_id=1, source_target_pairs={{0,240},{16,0},{32,16},{48,32},{64,48},{80,64},{96,80},{112,96},{1... | collective-permute-start | bytes 1001480 | tf_op jit(solution)/shard_map/ppermute | solution.py:39
  20.8 11.7 %copy-start.1 = (bf16[162,8,128]{2,1,0:T(8,128)(2,1)}, bf16[162,8,128]{2,1,0:T(8,128)(2,1)S(1)}, u32[]{:S(2)}) copy-start(bf16[162,8,128]{2,1,0:T(8,128)(2,1)S(1)} %pad_maximum_fusion.2.own) | copy-start | bytes 995332
  20.8 25.5 %collective-permute-start = (bf16[162,8,128]{2,1,0:T(8,128)(2,1)S(1)}, bf16[162,8,128]{2,1,0:T(8,128)(2,1)S(1)}, u32[]{:S(2)}, u32[]{:S(2)}) collective-permute-start(bf16[162,8,128]{2,1,0:T(8,128)(2,1)S(1)} %pad_maximum_fusion.2.own), channel_id=1, source_target_pairs={{0,256},{256,0},{1,257},{257,1},{2,258},{258,2},{3,259},{259,3},{4... | collective-permute-start | bytes 995336 | tf_op jit(solution)/shard_map/ppermute | solution.py:39
  25.0 7.4 %copy-start.2 = (bf16[55,8,128]{2,1,0:T(8,128)(2,1)}, bf16[55,8,128]{2,1,0:T(8,128)(2,1)S(1)}, u32[]{:S(2)}) copy-start(bf16[55,8,128]{2,1,0:T(8,128)(2,1)S(1)} %collective-permute-done.2.south) | copy-start | bytes 337924
  25.4 7.0 %copy-start.3 = (bf16[55,8,128]{2,1,0:T(8,128)(2,1)}, bf16[55,8,128]{2,1,0:T(8,128)(2,1)S(1)}, u32[]{:S(2)}) copy-start(bf16[55,8,128]{2,1,0:T(8,128)(2,1)S(1)} %collective-permute-done.3.corner) | copy-start | bytes 337924
  25.9 6.5 %copy-start = (bf16[163,8,128]{2,1,0:T(8,128)(2,1)}, bf16[163,8,128]{2,1,0:T(8,128)(2,1)S(1)}, u32[]{:S(2)}) copy-start(bf16[163,8,128]{2,1,0:T(8,128)(2,1)S(1)} %collective-permute-done.1.east) | copy-start | bytes 1001476
  26.7 19.6 %collective-permute-start.4 = (bf16[270,8,128]{2,1,0:T(8,128)(2,1)S(1)}, bf16[270,8,128]{2,1,0:T(8,128)(2,1)S(1)}, u32[]{:S(2)}, u32[]{:S(2)}) collective-permute-start(bf16[270,8,128]{2,1,0:T(8,128)(2,1)S(1)} %pad_maximum_fusion), channel_id=1, source_target_pairs={{0,256},{256,0},{1,257},{257,1},{2,258},{258,2},{3,259},{259,3},{4... | collective-permute-start | bytes 1658888 | tf_op jit(solution)/shard_map/ppermute | solution.py:39
  46.3 0.7 copy-start.5
  46.3 0.9 %copy-start.4 = (bf16[270,8,128]{2,1,0:T(8,128)(2,1)}, bf16[270,8,128]{2,1,0:T(8,128)(2,1)S(1)}, u32[]{:S(2)}) copy-start(bf16[270,8,128]{2,1,0:T(8,128)(2,1)S(1)} %collective-permute-done.4.rest) | copy-start | bytes 1658884
  61.9 13.6 %collective-permute-start.5 = (bf16[162,8,128]{2,1,0:T(8,128)(2,1)}, bf16[162,8,128]{2,1,0:T(8,128)(2,1)S(1)}, u32[]{:S(2)}, u32[]{:S(2)}) collective-permute-start(bf16[162,8,128]{2,1,0:T(8,128)(2,1)} %get-tuple-element.14), channel_id=1, source_target_pairs={{0,16},{16,32},{32,48},{48,64},{64,80},{80,96},{96,112},{112,128},... | collective-permute-start | bytes 995336 | tf_op jit(solution)/shard_map/ppermute | solution.py:39
  61.9 8.9 %collective-permute-start.6 = (bf16[54,8,128]{2,1,0:T(8,128)(2,1)}, bf16[54,8,128]{2,1,0:T(8,128)(2,1)S(1)}, u32[]{:S(2)}, u32[]{:S(2)}) collective-permute-start(bf16[54,8,128]{2,1,0:T(8,128)(2,1)} %get-tuple-element.15), channel_id=1, source_target_pairs={{0,1},{1,2},{2,3},{3,4},{4,5},{5,6},{6,7},{7,8},{8,9},{9,10},{10,1... | collective-permute-start | bytes 331784 | tf_op jit(solution)/shard_map/ppermute | solution.py:39
  65.0 10.5 %collective-permute-start.7 = (bf16[54,8,128]{2,1,0:T(8,128)(2,1)}, bf16[54,8,128]{2,1,0:T(8,128)(2,1)S(1)}, u32[]{:S(2)}, u32[]{:S(2)}) collective-permute-start(bf16[54,8,128]{2,1,0:T(8,128)(2,1)} %get-tuple-element.16), channel_id=1, source_target_pairs={{0,17},{1,18},{2,19},{3,20},{4,21},{5,22},{6,23},{7,24},{8,25},{9,... | collective-permute-start | bytes 331784 | tf_op jit(solution)/shard_map/ppermute | solution.py:46
  70.8 4.7 %copy-start.7 = (bf16[54,8,128]{2,1,0:T(8,128)(2,1)}, bf16[54,8,128]{2,1,0:T(8,128)(2,1)S(1)}, u32[]{:S(2)}) copy-start(bf16[54,8,128]{2,1,0:T(8,128)(2,1)S(1)} %collective-permute-done.6.north) | copy-start | bytes 331780
  75.5 0.6 copy-start.8
  75.5 0.8 copy-start.6

commit v2 on v1

v2 whole, which is shorter than its diff:
```python
import functools

import jax
import jax.numpy as jnp
import numpy as np
from jax import lax
from jax.experimental import pallas as pl
from jax.experimental.pallas import tpu as pltpu
from jax.sharding import PartitionSpec as P

LANES = 128
SH_LAT = 3
SH_LON = 6
WLAT = 6
LOG2E = 1.4426950408889634
EXCLUDED = -1e30
VMEM = pl.BlockSpec(memory_space=pltpu.VMEM)
SMEM = pl.BlockSpec(memory_space=pltpu.SMEM)
ROOM = pltpu.CompilerParams(vmem_limit_bytes=24 << 20)


def to_pairs(fields):
    groups, levels, lat_rows, lon_cells, width = fields.shape
    cells = jnp.transpose(fields, (0, 2, 3, 1, 4))
    cells = cells.reshape(groups, lat_rows, lon_cells, levels, width // LANES, LANES)
    cells = jnp.transpose(cells, (0, 1, 2, 4, 3, 5))
    return cells.reshape(groups, lat_rows, lon_cells, levels * (width // LANES), LANES)


def from_pairs(cells, levels):
    groups, lat_rows, lon_cells, rows, lanes = cells.shape
    cells = cells.reshape(groups, lat_rows, lon_cells, rows // levels, levels, lanes)
    cells = jnp.transpose(cells, (0, 1, 2, 4, 3, 5))
    cells = cells.reshape(groups, lat_rows, lon_cells, levels, (rows // levels) * lanes)
    return jnp.transpose(cells, (0, 3, 1, 2, 4))


def shifted(array, axes, by):
    if isinstance(axes, str):
        count = lax.axis_size(axes)
        return lax.ppermute(array, axes, [(i, (i + by) % count) for i in range(count)])
    outer, inner = (lax.axis_size(axis) for axis in axes)
    pairs = [
        (i * inner + j, ((i + by) % outer) * inner + (j + by) % inner)
        for i in range(outer)
        for j in range(inner)
    ]
    return lax.ppermute(array, axes, pairs)


def cells_to_tokens(pieces, cells_scr, tokens_scr, row):
    count = 0
    for piece in pieces:
        size = piece.shape[0]
        cells_scr[count * 8 : (count + size) * 8, :] = piece.reshape(size * 8, LANES).astype(
            jnp.float32
        )
        count += size
    for level in range(2):
        for tile in range(4):
            tokens_scr[tile, row + level * count : row + (level + 1) * count, :] = cells_scr[
                pl.ds(2 * tile + level, count, stride=8), :
            ]


def tokens_to_cells(tokens_scr, row, count, cells_scr):
    for level in range(2):
        for tile in range(4):
            cells_scr[pl.ds(2 * tile + level, count, stride=8), :] = tokens_scr[
                tile, row + level * count : row + (level + 1) * count, :
            ]


def whole_rows(tokens_scr):
    return jnp.concatenate([tokens_scr[tile] for tile in range(4)], axis=1)


def layer_norm(values):
    centred = values - jnp.mean(values, -1, keepdims=True)
    return centred * lax.rsqrt(jnp.mean(centred * centred, -1, keepdims=True) + 1e-05)


def head_squares(values, head_size):
    width = 256
    rows = lax.broadcasted_iota(jnp.int32, (width, width), 0) // head_size
    cols = lax.broadcasted_iota(jnp.int32, (width, width), 1) // head_size
    averaging = jnp.where(rows == cols, 1.0 / head_size, 0.0).astype(jnp.bfloat16)
    squares = (values * values).astype(jnp.bfloat16)
    return jnp.concatenate(
        [
            jnp.dot(
                squares[:, at : at + width], averaging, preferred_element_type=jnp.float32
            )
            for at in range(0, values.shape[1], width)
        ],
        axis=1,
    )


def unit_heads(values, head_size):
    return values * lax.rsqrt(head_squares(values, head_size) + 1e-06)


def window_columns(part):
    rows, lanes = [], []
    for source_parts in part:
        for level in range(2):
            for source, lats, lons in source_parts:
                for _ in range(3):
                    for lat in range(*lats):
                        for lon in range(*lons):
                            rows.append(24 * source + 2 * lat + level)
                            lanes.append(lon)
    keys = np.arange(len(rows))
    pick_row = np.zeros((96, len(rows)), np.float32)
    pick_row[np.array(rows), keys] = 1
    pick_lane = np.zeros((16, len(rows)), np.float32)
    pick_lane[np.array(lanes), keys] = 1
    return pick_row, pick_lane


def pack_kernel(cells, mask, own, west, north, flags, sems):
    copies = []
    for g in range(3):
        for dst, first, lats, lons in (
            (west, 0, (3, 9), (0, 6)),
            (west, 108, (9, 12), (0, 6)),
            (west, 162, (0, 3), (0, 6)),
            (own, 0, (3, 9), (6, 12)),
            (own, 108, (9, 12), (6, 12)),
            (north, 0, (0, 3), (6, 12)),
        ):
            rows = lats[1] - lats[0]
            copies.append(
                pltpu.make_async_copy(
                    cells.at[g, lats[0] : lats[1], lons[0] : lons[1]],
                    dst.at[pl.ds(first + g * rows * 6, rows * 6)].reshape(rows, 6, 8, LANES),
                    sems,
                )
            )
    for copy in copies:
        copy.start()
    flags[...] = jnp.zeros(flags.shape, jnp.float32)
    for lat in range(12):
        flags[2 * lat : 2 * lat + 2, 0:12] = mask[lat].astype(jnp.float32)
    tile = flags[...].astype(jnp.bfloat16).reshape(3, 8, LANES)
    west[216:219] = tile
    north[54:57] = tile
    for copy in copies:
        copy.wait()


def attend(query_ref, key_ref, value_ref, bias_ref, head_size, store):
    half = query_ref.shape[0]
    lane = lax.broadcasted_iota(jnp.int32, (half, LANES), 1)

    def one(pair, carry):
        at = pl.multiple_of(pair * LANES, LANES)
        queries = query_ref[:, pl.ds(at, LANES)]
        keys = key_ref[:, pl.ds(at, LANES)]
        values = value_ref[:, pl.ds(at, LANES)]
        total = None
        for side in range(2):
            mine = (lane < head_size) if side == 0 else (lane >= head_size)
            scores = lax.dot_general(
                queries,
                jnp.where(mine, keys, jnp.zeros_like(keys)),
                (((1,), (1,)), ((), ())),
                preferred_element_type=jnp.float32,
            )
            first = bias_ref[pl.ds(2 * pair + side, 1), :]
            second = bias_ref[pl.ds(8 + 2 * pair + side, 1), :]
            scores = jnp.concatenate(
                [scores[: half // 2] + first, scores[half // 2 :] + second], 0
            )
            weights = jnp.exp2(scores).astype(jnp.bfloat16)
            operand = jnp.concatenate(
                [
                    jnp.where(mine, values, jnp.zeros_like(values)),
                    jnp.where(mine, 1.0, 0.0).astype(jnp.bfloat16),
                ],
                axis=1,
            )
            part = jnp.dot(weights, operand, preferred_element_type=jnp.float32)
            total = part if total is None else total + part
        store(pair, at, total)
        return carry

    [one(p, 0) for p in range(4)]


def gather(window, own, east, south, cells_scr, tokens_scr):
    if window == 0:
        cells_to_tokens([own[0:108]], cells_scr, tokens_scr, 0)
        cells_to_tokens([east[0:108]], cells_scr, tokens_scr, 216)
    else:
        cells_to_tokens([own[108:162], east[108:162]], cells_scr, tokens_scr, 0)
        cells_to_tokens([south[0:108]], cells_scr, tokens_scr, 216)


def own_kernel(
    head_size,
    window,
    own,
    east,
    south,
    north,
    w_qkv,
    params,
    pick_row,
    pick_lane,
    query_out,
    total_out,
    bias_out,
    cells_scr,
    tokens_scr,
    key_scr,
    value_scr,
):
    gather(window, own, east, south, cells_scr, tokens_scr)
    width = w_qkv.shape[0]
    marks = [north[54:57], east[216:219]]
    if window == 1:
        marks += [south[108:111], south[111:114]]
    marks = jnp.concatenate([m.reshape(24, LANES).astype(jnp.float32) for m in marks], 0)
    spread = lax.dot_general(
        marks,
        pick_row[0 : marks.shape[0], :],
        (((0,), (0,)), ((), ())),
        preferred_element_type=jnp.float32,
    )
    marks = jnp.sum(spread[0:16] * pick_lane[...], 0, keepdims=True)
    bias = params[4:12, 0:1] * marks
    bias_out[0:8, :] = bias
    bias_out[8:16, :] = bias
    if window == 1:
        keys = marks.shape[1]
        later = lax.broadcasted_iota(jnp.int32, (8, keys), 1) >= keys // 2
        excluded = params[12:13, 0:1]
        bias_out[0:8, :] = bias + jnp.where(later, excluded, 0.0)
        bias_out[8:16, :] = bias + jnp.where(later, 0.0, excluded)
    scale = jnp.concatenate([params[i : i + 1, :] for i in range(4)], 1)
    normed = layer_norm(whole_rows(tokens_scr)).astype(jnp.bfloat16)
    mixed = jnp.dot(normed, w_qkv[:, :width], preferred_element_type=jnp.float32)
    query_out[...] = (unit_heads(mixed, head_size) * scale).astype(jnp.bfloat16)
    mixed = jnp.dot(normed, w_qkv[:, width : 2 * width], preferred_element_type=jnp.float32)
    key_scr[...] = unit_heads(mixed, head_size).astype(jnp.bfloat16)
    value_scr[...] = jnp.dot(
        normed, w_qkv[:, 2 * width :], preferred_element_type=jnp.float32
    ).astype(jnp.bfloat16)

    def store(pair, at, total):
        total_out[pair] = total

    attend(query_out, key_scr, value_scr, bias_out, head_size, store)


def partner_kernel(
    head_size,
    window,
    own,
    east,
    south,
    query_ref,
    total_in,
    bias_ref,
    w_qkv,
    w_out,
    *rest,
):
    outs, (cells_scr, tokens_scr, key_scr, value_scr, attended_scr) = rest[:-5], rest[-5:]
    gather(window, own, east, south, cells_scr, tokens_scr)
    width = w_qkv.shape[0]
    normed = layer_norm(whole_rows(tokens_scr)).astype(jnp.bfloat16)
    mixed = jnp.dot(normed, w_qkv[:, width : 2 * width], preferred_element_type=jnp.float32)
    key_scr[...] = unit_heads(mixed, head_size).astype(jnp.bfloat16)
    value_scr[...] = jnp.dot(
        normed, w_qkv[:, 2 * width :], preferred_element_type=jnp.float32
    ).astype(jnp.bfloat16)

    def store(pair, at, total):
        total = total + total_in[pair]
        attended_scr[:, pl.ds(at, LANES)] = (total[:, :LANES] / total[:, LANES:]).astype(
            jnp.bfloat16
        )

    attend(query_ref, key_scr, value_scr, bias_ref, head_size, store)
    projected = jnp.dot(attended_scr[...], w_out[...], preferred_element_type=jnp.float32)
    for tile in range(4):
        tokens_scr[tile] = projected[:, tile * LANES : (tile + 1) * LANES]

    def put(row, count, outs):
        tokens_to_cells(tokens_scr, row, count, cells_scr)
        at = 0
        for out, size in outs:
            out[...] = (
                cells_scr[at * 8 : (at + size) * 8, :].astype(jnp.bfloat16).reshape(size, 8, LANES)
            )
            at += size

    if window == 0:
        put(0, 108, [(outs[0], 108)])
        put(216, 108, [(outs[1], 108)])
    else:
        put(0, 108, [(outs[0], 54), (outs[1], 54)])
        put(216, 108, [(outs[2], 54), (outs[3], 54)])


def joining_kernel(bands, chunk, fields, w_up, w_down, *rest):
    pieces, (out, cells_scr, tokens_scr, normed_scr) = rest[: 2 * len(bands)], rest[-4:]
    groups = fields.shape[0]
    at = 0
    for band, (first, rows) in enumerate(bands):
        for g in range(groups):
            for side, lons in enumerate(((6, 12), (0, 6))):
                size = rows * 6
                term = pieces[2 * band + side][g * size : (g + 1) * size].astype(jnp.float32)
                term = term.reshape(rows, 6, 8, LANES)
                summed = fields[g, first : first + rows, lons[0] : lons[1]].astype(jnp.float32)
                summed = (summed + term).astype(jnp.bfloat16).astype(jnp.float32)
                cells_scr[g, at : at + rows, lons[0] : lons[1]] = summed
        at += rows
    cells = groups * at * 12
    flat = cells_scr.reshape(cells * 8, LANES)
    for level in range(2):
        for tile in range(4):
            tokens_scr[level * cells : (level + 1) * cells, tile * LANES : (tile + 1) * LANES] = (
                flat[pl.ds(2 * tile + level, cells, stride=8), :]
            )
    normed_scr[...] = layer_norm(tokens_scr[...]).astype(jnp.bfloat16)

    def one(step, carry):
        span = pl.ds(pl.multiple_of(step * chunk, 16), chunk)
        hidden = jnp.dot(normed_scr[span, :], w_up[...], preferred_element_type=jnp.float32)
        hidden = jax.nn.gelu(hidden, approximate=True).astype(jnp.bfloat16)
        tokens_scr[span, :] = tokens_scr[span, :] + jnp.dot(
            hidden, w_down[...], preferred_element_type=jnp.float32
        )
        return carry

    lax.fori_loop(0, 2 * cells // chunk, one, 0)
    for level in range(2):
        for tile in range(4):
            flat[pl.ds(2 * tile + level, cells, stride=8), :] = tokens_scr[
                level * cells : (level + 1) * cells, tile * LANES : (tile + 1) * LANES
            ]
    if len(bands) == 1:
        out[...] = cells_scr[...].astype(jnp.bfloat16)
        return
    done = rest[2 * len(bands)]
    at = 0
    for first, rows in bands:
        out[:, first : first + rows] = cells_scr[:, at : at + rows].astype(jnp.bfloat16)
        at += rows
    out[:, 3:9] = done[...]


def per_device(fields, surface_mask, w_qkv, w_out, logit_scale, mask_bias, w_up, w_down):
    groups, levels, lat_rows, lon_cells, width = fields.shape
    heads = logit_scale.shape[0]
    head_size = width // heads
    half = groups * levels * lat_rows * lon_cells // 2
    cells = to_pairs(fields)
    tile = (8, LANES)

    def pieces(*counts):
        return tuple(jax.ShapeDtypeStruct((n,) + tile, jnp.bfloat16) for n in counts)

    def call(kernel, name, outs, scratch, flops, arrays):
        return pl.pallas_call(
            kernel,
            name=name,
            compiler_params=ROOM,
            out_shape=outs,
            in_specs=[VMEM] * len(arrays),
            out_specs=jax.tree.map(lambda _: VMEM, outs),
            scratch_shapes=scratch,
            cost_estimate=pl.CostEstimate(
                flops=flops, bytes_accessed=4 * 10**6, transcendentals=10**6
            ),
        )(*arrays)

    own, west, north = pl.pallas_call(
        pack_kernel,
        name="pack",
        compiler_params=ROOM,
        out_shape=pieces(162, 219, 57),
        in_specs=[pl.BlockSpec(memory_space=pltpu.HBM), VMEM],
        out_specs=(VMEM, VMEM, VMEM),
        scratch_shapes=[pltpu.VMEM((24, LANES), jnp.float32), pltpu.SemaphoreType.DMA],
    )(cells, jnp.transpose(surface_mask, (1, 0, 2)))
    east = shifted(west, "lon", -1)
    own_across = shifted(own, "grp", 1)
    south = shifted(
        jnp.concatenate([north[:54], east[162:216], north[54:], east[216:]]), "lat", -1
    )
    east_across = shifted(east[:162], "grp", 1)
    south_across = shifted(south[:108], "grp", 1)

    last_band = lax.axis_index("lat") == lax.axis_size("lat") - 1
    params = jnp.concatenate(
        [
            jnp.repeat(logit_scale * (LOG2E / head_size), head_size).reshape(-1, LANES),
            jnp.broadcast_to((mask_bias * LOG2E)[:, None], (heads, LANES)),
            jnp.full((1, LANES), jnp.where(last_band, EXCLUDED, 0.0)),
        ]
    )
    layout = (
        (((0, (3, 9), (6, 12)),), ((1, (3, 9), (0, 6)),)),
        (((0, (9, 12), (6, 12)), (1, (9, 12), (0, 6))), ((2, (0, 3), (6, 12)), (3, (0, 3), (0, 6)))),
    )
    scratch = [
        pltpu.VMEM((half * 2, LANES), jnp.float32),
        pltpu.VMEM((4, half, LANES), jnp.float32),
        pltpu.VMEM((half, width), jnp.bfloat16),
        pltpu.VMEM((half, width), jnp.bfloat16),
    ]
    firsts = []
    for window in range(2):
        pick_row, pick_lane = window_columns(layout[window])
        firsts.append(
            call(
                functools.partial(own_kernel, head_size, window),
                "own",
                (
                    jax.ShapeDtypeStruct((half, width), jnp.bfloat16),
                    jax.ShapeDtypeStruct((4, half, 2 * LANES), jnp.float32),
                    jax.ShapeDtypeStruct((16, half), jnp.float32),
                ),
                scratch,
                3 * 10**9,
                (own, east, south if window else own, north, w_qkv, params, pick_row, pick_lane),
            )
        )
    scratch = scratch + [pltpu.VMEM((half, width), jnp.bfloat16)]
    upper_own, upper_east = call(
        functools.partial(partner_kernel, head_size, 0),
        "partner",
        pieces(108, 108),
        scratch,
        3 * 10**9,
        (own_across, east_across, own_across) + tuple(firsts[0]) + (w_qkv, w_out),
    )
    upper_west = shifted(upper_east, "lon", 1)
    lower_own, lower_east, lower_south, lower_corner = call(
        functools.partial(partner_kernel, head_size, 1),
        "partner",
        pieces(54, 54, 54, 54),
        scratch,
        3 * 10**9,
        (own_across, east_across, south_across) + tuple(firsts[1]) + (w_qkv, w_out),
    )
    lower_south = shifted(lower_south, "lat", 1)
    lower_corner = shifted(lower_corner, ("lon", "lat"), 1)
    lower_west = shifted(lower_east, "lon", 1)
    scratch = [
        pltpu.VMEM((groups, lat_rows // 2, lon_cells) + tile, jnp.float32),
        pltpu.VMEM((half, width), jnp.float32),
        pltpu.VMEM((half, width), jnp.bfloat16),
    ]
    upper = call(
        functools.partial(joining_kernel, ((3, 6),), 144),
        "joining",
        jax.ShapeDtypeStruct((groups, lat_rows // 2) + cells.shape[2:], jnp.bfloat16),
        scratch,
        2 * 10**9,
        (cells, w_up, w_down, upper_own, upper_west),
    )
    joined = call(
        functools.partial(joining_kernel, ((9, 3), (0, 3)), 144),
        "joining",
        jax.ShapeDtypeStruct(cells.shape, jnp.bfloat16),
        scratch,
        2 * 10**9,
        (cells, w_up, w_down, lower_own, lower_west, lower_south, lower_corner, upper),
    )
    return from_pairs(joined, levels)


def solution(mesh):
    return jax.shard_map(
        per_device,
        mesh=mesh,
        in_specs=(
            P("grp", None, "lat", "lon", None),
            P(None, "lat", "lon"),
            P(),
            P(),
            P(),
            P(),
            P(),
            P(),
        ),
        out_specs=P("grp", None, "lat", "lon", None),
        check_vma=False,
    )
```

time: 86.7 us -> 68.1 us (0.79)
  the two profiles are of different devices: /device:TPU:4 before, /device:TPU:25 now
where the time goes in v2:
time: 68.1 us; the launch traced here: 67.7 us
  starting transfers between devices  29.3 us (43%)
  Pallas kernels  23.3 us (34%)
  waiting for transfers between devices  9.41 us (14%)
  local copies, waits for them, and re-layouts  3.01 us (4%)
  other arithmetic  2.33 us (3%)
    ppermute x8, starting transfers between devices, shifted(): lax.ppermute(array, axes, [(i, (i + by) % count) for i in range(count)])  27.2 us
    pallas_call x6, Pallas kernels, call(): pl.pallas_call(kernel, name=name, compiler_params=ROOM, out_shape=outs, i...  23 us
    ppermute x8, waiting for transfers between devices, shifted(): lax.ppermute(array, axes, [(i, (i + by) % count) for i in range(count)])  7.25 us
    ppermute x1, waiting for transfers between devices, shifted(): return lax.ppermute(array, axes, pairs)  2.16 us
    ppermute x1, starting transfers between devices, shifted(): return lax.ppermute(array, axes, pairs)  2.14 us
    unnamed x22, local copies, waits for them, and re-layouts  1.92 us
  transfers between devices with their start and end apart: 9, of which 3 were waited for; matrix products, arithmetic and copies ran while one was open for 5% of the time, Pallas kernels for 27%

profile of v2, /device:TPU:25, one launch (start us, length us, event | category | flops | bytes accessed | tf_op | source)
XLA Modules:
  0.0 67.7 jit_solution(2207907735261183250)
XLA Ops:
  0.0 1.2 %copy-done = bf16[3,2,12,12,512]{4,1,3,2,0:T(2,128)(2,1)S(1)} copy-done((bf16[3,2,12,12,512]{4,1,3,2,0:T(2,128)(2,1)S(1)}, bf16[3,2,12,12,512]{4,1,3,2,0:T(2,128)(2,1)}, u32[]{:S(2)}) %copy-start) | copy-done | bytes 884760
  1.2 0.7 %copy-done.2 = s32[2,12,12]{2,0,1:T(2,128)S(1)} copy-done((s32[2,12,12]{2,0,1:T(2,128)S(1)}, s32[2,12,12]{2,0,1:T(2,128)}, u32[]{:S(2)}) %copy-start.2) | copy-done | bytes 1176
  1.9 0.3 pack.1
  2.2 4.8 %collective-permute-start = (bf16[162,8,128]{2,1,0:T(8,128)(2,1)S(1)}, bf16[162,8,128]{2,1,0:T(8,128)(2,1)S(1)}, u32[]{:S(2)}, u32[]{:S(2)}) collective-permute-start(bf16[162,8,128]{2,1,0:T(8,128)(2,1)S(1)} %get-tuple-element.20.own.south), channel_id=1, source_target_pairs={{0,256},{256,0},{1,257},{257,1},{2,258},{258,2},{3,259},{259,3},{4... | collective-permute-start | bytes 995336 | tf_op jit(solution)/shard_map/ppermute | solution.py:41
  7.0 1.0 %collective-permute-start.1 = (bf16[219,8,128]{2,1,0:T(8,128)(2,1)S(1)}, bf16[219,8,128]{2,1,0:T(8,128)(2,1)S(1)}, u32[]{:S(2)}, u32[]{:S(2)}) collective-permute-start(bf16[219,8,128]{2,1,0:T(8,128)(2,1)S(1)} %get-tuple-element.21), channel_id=1, source_target_pairs={{0,240},{16,0},{32,16},{48,32},{64,48},{80,64},{96,80},{112,96},{1... | collective-permute-start | bytes 1345544 | tf_op jit(solution)/shard_map/ppermute | solution.py:41
  8.0 0.7 slice.19
  8.6 0.7 broadcast_multiply_fusion
  9.3 0.1 pad.2.clone
  9.3 0.1 pad.1.clone
  9.4 0.7 broadcast_multiply_fusion.1
  10.1 0.1 broadcast_in_dim.16
  10.2 0.1 broadcast_in_dim.17
  10.2 0.1 broadcast_in_dim.18
  10.3 0.1 maximum_maximum_fusion.params
  10.4 6.0 %collective-permute-done.1.east = bf16[219,8,128]{2,1,0:T(8,128)(2,1)S(1)} collective-permute-done((bf16[219,8,128]{2,1,0:T(8,128)(2,1)S(1)}, bf16[219,8,128]{2,1,0:T(8,128)(2,1)S(1)}, u32[]{:S(2)}, u32[]{:S(2)}) %collective-permute-start.1) | collective-permute-done | bytes 448544 | tf_op jit(solution)/shard_map/ppermute | solution.py:41
  16.4 0.9 %pad_maximum_fusion = bf16[114,8,128]{2,1,0:T(8,128)(2,1)S(1)} fusion(bf16[3,8,128]{2,1,0:T(8,128)(2,1)S(1)} %slice.26, bf16[3,8,128]{2,1,0:T(8,128)(2,1)S(1)} %slice.21, bf16[54,8,128]{2,1,0:T(8,128)(2,1)S(1)} %slice.25, bf16[54,8,128]{2,1,0:T(8,128)(2,1)} %slice.19), kind=kLoop, calls=%fused_computation | loop fusion | flops 350208 | bytes 466944 | tf_op jit(solution)/shard_map/concatenate | solution.py:395
  17.4 10.7 %collective-permute-start.3 = (bf16[114,8,128]{2,1,0:T(8,128)(2,1)S(1)}, bf16[114,8,128]{2,1,0:T(8,128)(2,1)S(1)}, u32[]{:S(2)}, u32[]{:S(2)}) collective-permute-start(bf16[114,8,128]{2,1,0:T(8,128)(2,1)S(1)} %pad_maximum_fusion), channel_id=1, source_target_pairs={{0,15},{1,0},{2,1},{3,2},{4,3},{5,4},{6,5},{7,6},{8,7},{9,8},{10,9... | collective-permute-start | bytes 700424 | tf_op jit(solution)/shard_map/ppermute | solution.py:41
  28.1 0.0 copy-start.7
  28.2 4.0 %collective-permute-start.2 = (bf16[162,8,128]{2,1,0:T(8,128)(2,1)S(1)}, bf16[162,8,128]{2,1,0:T(8,128)(2,1)S(1)}, u32[]{:S(2)}, u32[]{:S(2)}) collective-permute-start(bf16[162,8,128]{2,1,0:T(8,128)(2,1)S(1)} %slice.24), channel_id=1, source_target_pairs={{0,256},{256,0},{1,257},{257,1},{2,258},{258,2},{3,259},{259,3},{4... | collective-permute-start | bytes 995336 | tf_op jit(solution)/shard_map/ppermute | solution.py:41
  32.2 3.7 %own.3 = (bf16[432,512]{1,0:T(8,128)(2,1)S(1)}, f32[4,432,256]{2,1,0:T(8,128)S(1)}, f32[16,432]{1,0:T(8,128)S(1)}) custom-call(bf16[162,8,128]{2,1,0:T(8,128)(2,1)S(1)} %get-tuple-element.20.own.south, bf16[219,8,128]{2,1,0:T(8,128)(2,1)S(1)} %collective-permute-done.1.east, bf16[162,8,128]{2,1,0:T(8,128)(2,1)S(1)} %get-tuple-element.20.own.south, ...), custom_call_target="tpu_custom_call" | custom-call | flops 3000000000 | bytes 4000000 | tf_op jit(solution)/shard_map/own/pallas_call | solution.py:370
  36.0 3.2 %collective-permute-start.4 = (bf16[108,8,128]{2,1,0:T(8,128)(2,1)S(1)}, bf16[108,8,128]{2,1,0:T(8,128)(2,1)S(1)}, u32[]{:S(2)}, u32[]{:S(2)}) collective-permute-start(bf16[108,8,128]{2,1,0:T(8,128)(2,1)S(1)} %slice.27), channel_id=1, source_target_pairs={{0,256},{256,0},{1,257},{257,1},{2,258},{258,2},{3,259},{259,3},{4... | collective-permute-start | bytes 663560 | tf_op jit(solution)/shard_map/ppermute | solution.py:41
  39.2 3.7 %own.2 = (bf16[432,512]{1,0:T(8,128)(2,1)S(1)}, f32[4,432,256]{2,1,0:T(8,128)S(1)}, f32[16,432]{1,0:T(8,128)S(1)}) custom-call(bf16[162,8,128]{2,1,0:T(8,128)(2,1)S(1)} %get-tuple-element.20.own.south, bf16[219,8,128]{2,1,0:T(8,128)(2,1)S(1)} %collective-permute-done.1.east, bf16[114,8,128]{2,1,0:T(8,128)(2,1)S(1)} %collective-permute-done.3.south, ...), custom_call_target="tpu_custom_call" | custom-call | flops 3000000000 | bytes 4000000 | tf_op jit(solution)/shard_map/own/pallas_call | solution.py:370
  43.0 3.7 %partner.3 = (bf16[108,8,128]{2,1,0:T(8,128)(2,1)S(1)}, bf16[108,8,128]{2,1,0:T(8,128)(2,1)S(1)}) custom-call(bf16[162,8,128]{2,1,0:T(8,128)(2,1)S(1)} %collective-permute-done.own.south, bf16[162,8,128]{2,1,0:T(8,128)(2,1)S(1)} %collective-permute-done.2.east, bf16[162,8,128]{2,1,0:T(8,128)(2,1)S(1)} %collective-permute-done.own.south, ...), custom_call_target="tpu_custom_call" | custom-call | flops 3000000000 | bytes 4000000 | tf_op jit(solution)/shard_map/partner/pallas_call | solution.py:370
  46.7 0.6 collective-permute-start.8
  47.3 3.7 %partner.2 = (bf16[54,8,128]{2,1,0:T(8,128)(2,1)S(1)}, bf16[54,8,128]{2,1,0:T(8,128)(2,1)S(1)}, bf16[54,8,128]{2,1,0:T(8,128)(2,1)S(1)}, bf16[54,8,128]{2,1,0:T(8,128)(2,1)S(1)}) custom-call(bf16[162,8,128]{2,1,0:T(8,128)(2,1)S(1)} %collective-permute-done.own.south, bf16[162,8,128]{2,1,0:T(8,128)(2,1)S(1)} %collective-permute-done.2.east, ...), custom_call_target="tpu_custom_call" | custom-call | flops 3000000000 | bytes 4000000 | tf_op jit(solution)/shard_map/partner/pallas_call | solution.py:370
  51.1 0.9 %collective-permute-start.5 = (bf16[54,8,128]{2,1,0:T(8,128)(2,1)S(1)}, bf16[54,8,128]{2,1,0:T(8,128)(2,1)S(1)}, u32[]{:S(2)}, u32[]{:S(2)}) collective-permute-start(bf16[54,8,128]{2,1,0:T(8,128)(2,1)S(1)} %get-tuple-element.27), channel_id=1, source_target_pairs={{0,16},{16,32},{32,48},{48,64},{64,80},{80,96},{96,112},{112,128},... | collective-permute-start | bytes 331784 | tf_op jit(solution)/shard_map/ppermute | solution.py:41
  52.0 1.9 %collective-permute-start.6 = (bf16[54,8,128]{2,1,0:T(8,128)(2,1)S(1)}, bf16[54,8,128]{2,1,0:T(8,128)(2,1)S(1)}, u32[]{:S(2)}, u32[]{:S(2)}) collective-permute-start(bf16[54,8,128]{2,1,0:T(8,128)(2,1)S(1)} %get-tuple-element.28), channel_id=1, source_target_pairs={{0,1},{1,2},{2,3},{3,4},{4,5},{5,6},{6,7},{7,8},{8,9},{9,10},{10,1... | collective-permute-start | bytes 331784 | tf_op jit(solution)/shard_map/ppermute | solution.py:41
  53.9 2.1 %collective-permute-start.7 = (bf16[54,8,128]{2,1,0:T(8,128)(2,1)S(1)}, bf16[54,8,128]{2,1,0:T(8,128)(2,1)S(1)}, u32[]{:S(2)}, u32[]{:S(2)}) collective-permute-start(bf16[54,8,128]{2,1,0:T(8,128)(2,1)S(1)} %get-tuple-element.29), channel_id=1, source_target_pairs={{0,17},{1,18},{2,19},{3,20},{4,21},{5,22},{6,23},{7,24},{8,25},{9,... | collective-permute-start | bytes 331784 | tf_op jit(solution)/shard_map/ppermute | solution.py:48
  56.1 3.6 %joining.2.rest_4_ = bf16[3,6,12,8,128]{4,3,2,1,0:T(8,128)(2,1)S(1)} custom-call(bf16[3,12,12,8,128]{4,3,2,1,0:T(8,128)(2,1)S(1)} %bitcast.17, bf16[512,2048]{1,0:T(8,128)(2,1)S(1)} %copy-done.3, bf16[2048,512]{1,0:T(8,128)(2,1)S(1)} %copy-done.4, bf16[108,8,128]{2,1,0:T(8,128)(2,1)S(1)} %get-tuple-element.33.rest_0_, ...), custom_call_target="tpu_custom_call" | custom-call | flops 2000000000 | bytes 4000000 | tf_op jit(solution)/shard_map/joining/pallas_call | solution.py:370
  59.7 1.2 %collective-permute-done.6.rest_2_ = bf16[54,8,128]{2,1,0:T(8,128)(2,1)S(1)} collective-permute-done((bf16[54,8,128]{2,1,0:T(8,128)(2,1)S(1)}, bf16[54,8,128]{2,1,0:T(8,128)(2,1)S(1)}, u32[]{:S(2)}, u32[]{:S(2)}) %collective-permute-start.6) | collective-permute-done | bytes 110624 | tf_op jit(solution)/shard_map/ppermute | solution.py:41
  60.9 2.2 %collective-permute-done.7.rest_3_ = bf16[54,8,128]{2,1,0:T(8,128)(2,1)S(1)} collective-permute-done((bf16[54,8,128]{2,1,0:T(8,128)(2,1)S(1)}, bf16[54,8,128]{2,1,0:T(8,128)(2,1)S(1)}, u32[]{:S(2)}, u32[]{:S(2)}) %collective-permute-start.7) | collective-permute-done | bytes 110624 | tf_op jit(solution)/shard_map/ppermute | solution.py:48
  63.1 4.6 %joining.3 = bf16[3,12,12,8,128]{4,3,2,1,0:T(8,128)(2,1)} custom-call(bf16[3,12,12,8,128]{4,3,2,1,0:T(8,128)(2,1)S(1)} %bitcast.18, bf16[512,2048]{1,0:T(8,128)(2,1)S(1)} %copy-done.3, bf16[2048,512]{1,0:T(8,128)(2,1)S(1)} %copy-done.4, bf16[54,8,128]{2,1,0:T(8,128)(2,1)S(1)} %get-tuple-element.26.rest_0_, ...), custom_call_target="tpu_custom_call" | custom-call | flops 2000000000 | bytes 4000000 | tf_op jit(solution)/shard_map/joining/pallas_call | solution.py:370
  (30 shorter events, 0.1 us)
Async XLA Ops:
  0.0 1.2 %copy-start = (bf16[3,2,12,12,512]{4,1,3,2,0:T(2,128)(2,1)S(1)}, bf16[3,2,12,12,512]{4,1,3,2,0:T(2,128)(2,1)}, u32[]{:S(2)}) copy-start(bf16[3,2,12,12,512]{4,1,3,2,0:T(2,128)(2,1)} %param.12) | copy-start | bytes 2654212
  1.2 0.7 %copy-start.2 = (s32[2,12,12]{2,0,1:T(2,128)S(1)}, s32[2,12,12]{2,0,1:T(2,128)}, u32[]{:S(2)}) copy-start(s32[2,12,12]{2,0,1:T(2,128)} %param.13) | copy-start | bytes 3460
  1.9 30.3 %copy-start.5 = (bf16[512,1536]{1,0:T(8,128)(2,1)S(1)}, bf16[512,1536]{1,0:T(8,128)(2,1)}, u32[]{:S(2)}) copy-start(bf16[512,1536]{1,0:T(8,128)(2,1)} %w_qkv.7) | copy-start | bytes 4718596
  1.9 30.3 %copy-start.8 = (f32[96,432]{1,0:T(8,128)S(1)}, f32[96,432]{1,0:T(8,128)}, u32[]{:S(2)}) copy-start(f32[96,432]{1,0:T(8,128)} %constant.22.clone.pick_row) | copy-start | bytes 497668
  1.9 30.3 %copy-start.10 = (f32[16,432]{1,0:T(8,128)S(1)}, f32[16,432]{1,0:T(8,128)}, u32[]{:S(2)}) copy-start(f32[16,432]{1,0:T(8,128)} %constant.23.clone.pick_lane) | copy-start | bytes 82948
  2.2 40.8 %collective-permute-start = (bf16[162,8,128]{2,1,0:T(8,128)(2,1)S(1)}, bf16[162,8,128]{2,1,0:T(8,128)(2,1)S(1)}, u32[]{:S(2)}, u32[]{:S(2)}) collective-permute-start(bf16[162,8,128]{2,1,0:T(8,128)(2,1)S(1)} %get-tuple-element.20.own.south), channel_id=1, source_target_pairs={{0,256},{256,0},{1,257},{257,1},{2,258},{258,2},{3,259},{259,3},{4... | collective-permute-start | bytes 995336 | tf_op jit(solution)/shard_map/ppermute | solution.py:41
  7.0 9.4 %collective-permute-start.1 = (bf16[219,8,128]{2,1,0:T(8,128)(2,1)S(1)}, bf16[219,8,128]{2,1,0:T(8,128)(2,1)S(1)}, u32[]{:S(2)}, u32[]{:S(2)}) collective-permute-start(bf16[219,8,128]{2,1,0:T(8,128)(2,1)S(1)} %get-tuple-element.21), channel_id=1, source_target_pairs={{0,240},{16,0},{32,16},{48,32},{64,48},{80,64},{96,80},{112,96},{1... | collective-permute-start | bytes 1345544 | tf_op jit(solution)/shard_map/ppermute | solution.py:41
  17.4 18.6 %collective-permute-start.3 = (bf16[114,8,128]{2,1,0:T(8,128)(2,1)S(1)}, bf16[114,8,128]{2,1,0:T(8,128)(2,1)S(1)}, u32[]{:S(2)}, u32[]{:S(2)}) collective-permute-start(bf16[114,8,128]{2,1,0:T(8,128)(2,1)S(1)} %pad_maximum_fusion), channel_id=1, source_target_pairs={{0,15},{1,0},{2,1},{3,2},{4,3},{5,4},{6,5},{7,6},{8,7},{9,8},{10,9... | collective-permute-start | bytes 700424 | tf_op jit(solution)/shard_map/ppermute | solution.py:41
  28.1 11.1 %copy-start.7 = (f32[96,432]{1,0:T(8,128)S(1)}, f32[96,432]{1,0:T(8,128)}, u32[]{:S(2)}) copy-start(f32[96,432]{1,0:T(8,128)} %constant.24.clone.pick_row) | copy-start | bytes 497668
  28.2 11.1 %copy-start.9 = (f32[16,432]{1,0:T(8,128)S(1)}, f32[16,432]{1,0:T(8,128)}, u32[]{:S(2)}) copy-start(f32[16,432]{1,0:T(8,128)} %constant.25.clone.pick_lane) | copy-start | bytes 82948
  28.2 14.8 %collective-permute-start.2 = (bf16[162,8,128]{2,1,0:T(8,128)(2,1)S(1)}, bf16[162,8,128]{2,1,0:T(8,128)(2,1)S(1)}, u32[]{:S(2)}, u32[]{:S(2)}) collective-permute-start(bf16[162,8,128]{2,1,0:T(8,128)(2,1)S(1)} %slice.24), channel_id=1, source_target_pairs={{0,256},{256,0},{1,257},{257,1},{2,258},{258,2},{3,259},{259,3},{4... | collective-permute-start | bytes 995336 | tf_op jit(solution)/shard_map/ppermute | solution.py:41
  36.0 7.0 %copy-start.6 = (bf16[512,512]{1,0:T(8,128)(2,1)S(1)}, bf16[512,512]{1,0:T(8,128)(2,1)}, u32[]{:S(2)}) copy-start(bf16[512,512]{1,0:T(8,128)(2,1)} %w_out.3) | copy-start | bytes 1572868
  36.0 11.3 %collective-permute-start.4 = (bf16[108,8,128]{2,1,0:T(8,128)(2,1)S(1)}, bf16[108,8,128]{2,1,0:T(8,128)(2,1)S(1)}, u32[]{:S(2)}, u32[]{:S(2)}) collective-permute-start(bf16[108,8,128]{2,1,0:T(8,128)(2,1)S(1)} %slice.27), channel_id=1, source_target_pairs={{0,256},{256,0},{1,257},{257,1},{2,258},{258,2},{3,259},{259,3},{4... | collective-permute-start | bytes 663560 | tf_op jit(solution)/shard_map/ppermute | solution.py:41
  46.7 9.4 %collective-permute-start.8 = (bf16[108,8,128]{2,1,0:T(8,128)(2,1)S(1)}, bf16[108,8,128]{2,1,0:T(8,128)(2,1)S(1)}, u32[]{:S(2)}, u32[]{:S(2)}) collective-permute-start(bf16[108,8,128]{2,1,0:T(8,128)(2,1)S(1)} %get-tuple-element.34), channel_id=1, source_target_pairs={{0,16},{16,32},{32,48},{48,64},{64,80},{80,96},{96,112},{112,128},... | collective-permute-start | bytes 663560 | tf_op jit(solution)/shard_map/ppermute | solution.py:41
  47.3 8.7 %copy-start.1 = (bf16[3,2,12,12,512]{4,1,3,2,0:T(2,128)(2,1)S(1)}, bf16[3,2,12,12,512]{4,1,3,2,0:T(2,128)(2,1)}, u32[]{:S(2)}) copy-start(bf16[3,2,12,12,512]{4,1,3,2,0:T(2,128)(2,1)} %param.12) | copy-start | bytes 2654212
  47.3 8.7 %copy-start.3 = (bf16[512,2048]{1,0:T(8,128)(2,1)S(1)}, bf16[512,2048]{1,0:T(8,128)(2,1)}, u32[]{:S(2)}) copy-start(bf16[512,2048]{1,0:T(8,128)(2,1)} %w_up.3) | copy-start | bytes 6291460
  47.3 8.7 %copy-start.4 = (bf16[2048,512]{1,0:T(8,128)(2,1)S(1)}, bf16[2048,512]{1,0:T(8,128)(2,1)}, u32[]{:S(2)}) copy-start(bf16[2048,512]{1,0:T(8,128)(2,1)} %w_down.3) | copy-start | bytes 6291460
  51.1 8.6 %collective-permute-start.5 = (bf16[54,8,128]{2,1,0:T(8,128)(2,1)S(1)}, bf16[54,8,128]{2,1,0:T(8,128)(2,1)S(1)}, u32[]{:S(2)}, u32[]{:S(2)}) collective-permute-start(bf16[54,8,128]{2,1,0:T(8,128)(2,1)S(1)} %get-tuple-element.27), channel_id=1, source_target_pairs={{0,16},{16,32},{32,48},{48,64},{64,80},{80,96},{96,112},{112,128},... | collective-permute-start | bytes 331784 | tf_op jit(solution)/shard_map/ppermute | solution.py:41
  52.0 9.0 %collective-permute-start.6 = (bf16[54,8,128]{2,1,0:T(8,128)(2,1)S(1)}, bf16[54,8,128]{2,1,0:T(8,128)(2,1)S(1)}, u32[]{:S(2)}, u32[]{:S(2)}) collective-permute-start(bf16[54,8,128]{2,1,0:T(8,128)(2,1)S(1)} %get-tuple-element.28), channel_id=1, source_target_pairs={{0,1},{1,2},{2,3},{3,4},{4,5},{5,6},{6,7},{7,8},{8,9},{9,10},{10,1... | collective-permute-start | bytes 331784 | tf_op jit(solution)/shard_map/ppermute | solution.py:41
  53.9 9.2 %collective-permute-start.7 = (bf16[54,8,128]{2,1,0:T(8,128)(2,1)S(1)}, bf16[54,8,128]{2,1,0:T(8,128)(2,1)S(1)}, u32[]{:S(2)}, u32[]{:S(2)}) collective-permute-start(bf16[54,8,128]{2,1,0:T(8,128)(2,1)S(1)} %get-tuple-element.29), channel_id=1, source_target_pairs={{0,17},{1,18},{2,19},{3,20},{4,21},{5,22},{6,23},{7,24},{8,25},{9,... | collective-permute-start | bytes 331784 | tf_op jit(solution)/shard_map/ppermute | solution.py:48

commit v3 on v2

--- a/solution.py
+++ b/solution.py
@@ -8,10 +8,8 @@
 from jax.experimental.pallas import tpu as pltpu
 from jax.sharding import PartitionSpec as P
 
+
 LANES = 128
-SH_LAT = 3
-SH_LON = 6
-WLAT = 6
 LOG2E = 1.4426950408889634
 EXCLUDED = -1e30
 VMEM = pl.BlockSpec(memory_space=pltpu.VMEM)
@@ -35,15 +33,18 @@
     return jnp.transpose(cells, (0, 3, 1, 2, 4))
 
 
-def shifted(array, axes, by):
-    if isinstance(axes, str):
-        count = lax.axis_size(axes)
-        return lax.ppermute(array, axes, [(i, (i + by) % count) for i in range(count)])
-    outer, inner = (lax.axis_size(axis) for axis in axes)
+def shifted(array, lon=0, lat=0, across=False):
+    axes = ("grp", "lon", "lat")
+    sizes = [lax.axis_size(axis) for axis in axes]
+
+    def place(g, i, j):
+        return (g * sizes[1] + i % sizes[1]) * sizes[2] + j % sizes[2]
+
     pairs = [
-        (i * inner + j, ((i + by) % outer) * inner + (j + by) % inner)
-        for i in range(outer)
-        for j in range(inner)
+        (place(g, i, j), place(1 - g if across else g, i + lon, j + lat))
+        for g in range(sizes[0])
+        for i in range(sizes[1])
+        for j in range(sizes[2])
     ]
     return lax.ppermute(array, axes, pairs)
 
@@ -150,6 +151,17 @@
         copy.wait()
 
 
+def again_kernel(east, out):
+    out[...] = east[0:162]
+
+
+def southward_kernel(east, north, after, out):
+    out[0:54] = north[0:54]
+    out[54:108] = east[162:216]
+    out[108:111] = north[54:57]
+    out[111:114] = east[216:219]
+
+
 def attend(query_ref, key_ref, value_ref, bias_ref, head_size, store):
     half = query_ref.shape[0]
     lane = lax.broadcasted_iota(jnp.int32, (half, LANES), 1)
@@ -204,9 +216,11 @@
     own,
     east,
     south,
+    after,
     north,
     w_qkv,
-    params,
+    logit_scale,
+    mask_bias,
     pick_row,
     pick_lane,
     query_out,
@@ -230,16 +244,24 @@
         preferred_element_type=jnp.float32,
     )
     marks = jnp.sum(spread[0:16] * pick_lane[...], 0, keepdims=True)
-    bias = params[4:12, 0:1] * marks
+    heads = mask_bias.shape[1]
+    rows = lax.broadcasted_iota(jnp.int32, (heads, heads), 0)
+    cols = lax.broadcasted_iota(jnp.int32, (heads, heads), 1)
+    column = jnp.sum(jnp.where(rows == cols, mask_bias[...], 0.0), 1, keepdims=True)
+    bias = (column * LOG2E) * marks
     bias_out[0:8, :] = bias
     bias_out[8:16, :] = bias
     if window == 1:
         keys = marks.shape[1]
         later = lax.broadcasted_iota(jnp.int32, (8, keys), 1) >= keys // 2
-        excluded = params[12:13, 0:1]
+        last = lax.axis_index("lat") == lax.axis_size("lat") - 1
+        excluded = jnp.where(last, EXCLUDED, 0.0)
         bias_out[0:8, :] = bias + jnp.where(later, excluded, 0.0)
         bias_out[8:16, :] = bias + jnp.where(later, 0.0, excluded)
-    scale = jnp.concatenate([params[i : i + 1, :] for i in range(4)], 1)
+    head = lax.broadcasted_iota(jnp.int32, (1, width), 1) // head_size
+    scale = jnp.zeros((1, width), jnp.float32)
+    for i in range(heads):
+        scale = jnp.where(head == i, logit_scale[0:1, i : i + 1] * (LOG2E / head_size), scale)
     normed = layer_norm(whole_rows(tokens_scr)).astype(jnp.bfloat16)
     mixed = jnp.dot(normed, w_qkv[:, :width], preferred_element_type=jnp.float32)
     query_out[...] = (unit_heads(mixed, head_size) * scale).astype(jnp.bfloat16)
@@ -306,12 +328,13 @@
         put(216, 108, [(outs[2], 54), (outs[3], 54)])
 
 
-def joining_kernel(bands, chunk, fields, w_up, w_down, *rest):
-    pieces, (out, cells_scr, tokens_scr, normed_scr) = rest[: 2 * len(bands)], rest[-4:]
-    groups = fields.shape[0]
-    at = 0
-    for band, (first, rows) in enumerate(bands):
-        for g in range(groups):
+def joining_kernel(bands, fields, w_up, w_down, *rest):
+    pieces, (out, cells_scr, tokens_scr) = rest[: 2 * len(bands)], rest[-3:]
+    if len(bands) == 2:
+        out[:, 3:9] = rest[2 * len(bands)][...]
+    for g in range(fields.shape[0]):
+        at = 0
+        for band, (first, rows) in enumerate(bands):
             for side, lons in enumerate(((6, 12), (0, 6))):
                 size = rows * 6
                 term = pieces[2 * band + side][g * size : (g + 1) * size].astype(jnp.float32)
@@ -319,40 +342,31 @@
                 summed = fields[g, first : first + rows, lons[0] : lons[1]].astype(jnp.float32)
                 summed = (summed + term).astype(jnp.bfloat16).astype(jnp.float32)
                 cells_scr[g, at : at + rows, lons[0] : lons[1]] = summed
-        at += rows
-    cells = groups * at * 12
-    flat = cells_scr.reshape(cells * 8, LANES)
-    for level in range(2):
-        for tile in range(4):
-            tokens_scr[level * cells : (level + 1) * cells, tile * LANES : (tile + 1) * LANES] = (
-                flat[pl.ds(2 * tile + level, cells, stride=8), :]
-            )
-    normed_scr[...] = layer_norm(tokens_scr[...]).astype(jnp.bfloat16)
-
-    def one(step, carry):
-        span = pl.ds(pl.multiple_of(step * chunk, 16), chunk)
-        hidden = jnp.dot(normed_scr[span, :], w_up[...], preferred_element_type=jnp.float32)
+            at += rows
+        cells = at * 12
+        flat = cells_scr.at[g].reshape(cells * 8, LANES)
+        for level in range(2):
+            for tile in range(4):
+                tokens_scr[
+                    g, level * cells : (level + 1) * cells, tile * LANES : (tile + 1) * LANES
+                ] = flat[pl.ds(2 * tile + level, cells, stride=8), :]
+        residual = tokens_scr[g]
+        normed = layer_norm(residual).astype(jnp.bfloat16)
+        hidden = jnp.dot(normed, w_up[...], preferred_element_type=jnp.float32)
         hidden = jax.nn.gelu(hidden, approximate=True).astype(jnp.bfloat16)
-        tokens_scr[span, :] = tokens_scr[span, :] + jnp.dot(
-            hidden, w_down[...], preferred_element_type=jnp.float32
-        )
-        return carry
-
-    lax.fori_loop(0, 2 * cells // chunk, one, 0)
-    for level in range(2):
-        for tile in range(4):
-            flat[pl.ds(2 * tile + level, cells, stride=8), :] = tokens_scr[
-                level * cells : (level + 1) * cells, tile * LANES : (tile + 1) * LANES
-            ]
-    if len(bands) == 1:
-        out[...] = cells_scr[...].astype(jnp.bfloat16)
-        return
-    done = rest[2 * len(bands)]
-    at = 0
-    for first, rows in bands:
-        out[:, first : first + rows] = cells_scr[:, at : at + rows].astype(jnp.bfloat16)
-        at += rows
-    out[:, 3:9] = done[...]
+        joined = residual + jnp.dot(hidden, w_down[...], preferred_element_type=jnp.float32)
+        for level in range(2):
+            for tile in range(4):
+                flat[pl.ds(2 * tile + level, cells, stride=8), :] = joined[
+                    level * cells : (level + 1) * cells, tile * LANES : (tile + 1) * LANES
+                ]
+        if len(bands) == 1:
+            out[g] = cells_scr[g].astype(jnp.bfloat16)
+        else:
+            at = 0
+            for first, rows in bands:
+                out[g, first : first + rows] = cells_scr[g, at : at + rows].astype(jnp.bfloat16)
+                at += rows
 
 
 def per_device(fields, surface_mask, w_qkv, w_out, logit_scale, mask_bias, w_up, w_down):
@@ -366,10 +380,9 @@
     def pieces(*counts):
         return tuple(jax.ShapeDtypeStruct((n,) + tile, jnp.bfloat16) for n in counts)
 
-    def call(kernel, name, outs, scratch, flops, arrays):
+    def call(kernel, outs, scratch, flops, arrays):
         return pl.pallas_call(
             kernel,
-            name=name,
             compiler_params=ROOM,
             out_shape=outs,
             in_specs=[VMEM] * len(arrays),
@@ -389,22 +402,11 @@
         out_specs=(VMEM, VMEM, VMEM),
         scratch_shapes=[pltpu.VMEM((24, LANES), jnp.float32), pltpu.SemaphoreType.DMA],
     )(cells, jnp.transpose(surface_mask, (1, 0, 2)))
-    east = shifted(west, "lon", -1)
-    own_across = shifted(own, "grp", 1)
-    south = shifted(
-        jnp.concatenate([north[:54], east[162:216], north[54:], east[216:]]), "lat", -1
-    )
-    east_across = shifted(east[:162], "grp", 1)
-    south_across = shifted(south[:108], "grp", 1)
-
-    last_band = lax.axis_index("lat") == lax.axis_size("lat") - 1
-    params = jnp.concatenate(
-        [
-            jnp.repeat(logit_scale * (LOG2E / head_size), head_size).reshape(-1, LANES),
-            jnp.broadcast_to((mask_bias * LOG2E)[:, None], (heads, LANES)),
-            jnp.full((1, LANES), jnp.where(last_band, EXCLUDED, 0.0)),
-        ]
-    )
+    east = shifted(west, lon=-1)
+    own_across = shifted(own, across=True)
+    east_again = call(again_kernel, pieces(162)[0], [], 10**6, (east,))
+    east_across = shifted(east_again, across=True)
+
     layout = (
         (((0, (3, 9), (6, 12)),), ((1, (3, 9), (0, 6)),)),
         (((0, (9, 12), (6, 12)), (1, (9, 12), (0, 6))), ((2, (0, 3), (6, 12)), (3, (0, 3), (0, 6)))),
@@ -415,64 +417,63 @@
         pltpu.VMEM((half, width), jnp.bfloat16),
         pltpu.VMEM((half, width), jnp.bfloat16),
     ]
-    firsts = []
-    for window in range(2):
+    late = scratch + [pltpu.VMEM((half, width), jnp.bfloat16)]
+
+    def own_part(window, arrays):
         pick_row, pick_lane = window_columns(layout[window])
-        firsts.append(
-            call(
-                functools.partial(own_kernel, head_size, window),
-                "own",
-                (
-                    jax.ShapeDtypeStruct((half, width), jnp.bfloat16),
-                    jax.ShapeDtypeStruct((4, half, 2 * LANES), jnp.float32),
-                    jax.ShapeDtypeStruct((16, half), jnp.float32),
-                ),
-                scratch,
-                3 * 10**9,
-                (own, east, south if window else own, north, w_qkv, params, pick_row, pick_lane),
-            )
+        return call(
+            functools.partial(own_kernel, head_size, window),
+            (
+                jax.ShapeDtypeStruct((half, width), jnp.bfloat16),
+                jax.ShapeDtypeStruct((4, half, 2 * LANES), jnp.float32),
+                jax.ShapeDtypeStruct((16, half), jnp.float32),
+            ),
+            scratch,
+            3 * 10**9,
+            arrays + (w_qkv, logit_scale[None], mask_bias[None], pick_row, pick_lane),
         )
-    scratch = scratch + [pltpu.VMEM((half, width), jnp.bfloat16)]
-    upper_own, upper_east = call(
-        functools.partial(partner_kernel, head_size, 0),
-        "partner",
-        pieces(108, 108),
-        scratch,
-        3 * 10**9,
-        (own_across, east_across, own_across) + tuple(firsts[0]) + (w_qkv, w_out),
-    )
-    upper_west = shifted(upper_east, "lon", 1)
-    lower_own, lower_east, lower_south, lower_corner = call(
-        functools.partial(partner_kernel, head_size, 1),
-        "partner",
-        pieces(54, 54, 54, 54),
-        scratch,
-        3 * 10**9,
-        (own_across, east_across, south_across) + tuple(firsts[1]) + (w_qkv, w_out),
-    )
-    lower_south = shifted(lower_south, "lat", 1)
-    lower_corner = shifted(lower_corner, ("lon", "lat"), 1)
-    lower_west = shifted(lower_east, "lon", 1)
+
+    def partner_part(window, counts, arrays, first):
+        return call(
+            functools.partial(partner_kernel, head_size, window),
+            pieces(*counts),
+            late,
+            3 * 10**9,
+            arrays + tuple(first) + (w_qkv, w_out),
+        )
+
+    first = own_part(0, (own, east, north, north, north))
+    south = call(southward_kernel, pieces(114)[0], [], 10**6, (east, north, first[2]))
+    south_across = shifted(south, lat=-1, across=True)
+    south = shifted(south, lat=-1)
+    upper_own, upper_east = partner_part(
+        0, (108, 108), (own_across, east_across, own_across), first
+    )
+    upper_west = shifted(upper_east, lon=1)
+    first = own_part(1, (own, east, south, upper_own, north))
+    lower_own, lower_east, lower_south, lower_corner = partner_part(
+        1, (54, 54, 54, 54), (own_across, east_across, south_across), first
+    )
+    lower_north = shifted(lower_south, lat=1)
+    lower_northwest = shifted(lower_corner, lon=1, lat=1)
+    lower_west = shifted(lower_east, lon=1)
     scratch = [
         pltpu.VMEM((groups, lat_rows // 2, lon_cells) + tile, jnp.float32),
-        pltpu.VMEM((half, width), jnp.float32),
-        pltpu.VMEM((half, width), jnp.bfloat16),
+        pltpu.VMEM((groups, half // groups, width), jnp.float32),
     ]
     upper = call(
-        functools.partial(joining_kernel, ((3, 6),), 144),
-        "joining",
+        functools.partial(joining_kernel, ((3, 6),)),
         jax.ShapeDtypeStruct((groups, lat_rows // 2) + cells.shape[2:], jnp.bfloat16),
         scratch,
         2 * 10**9,
         (cells, w_up, w_down, upper_own, upper_west),
     )
     joined = call(
-        functools.partial(joining_kernel, ((9, 3), (0, 3)), 144),
-        "joining",
+        functools.partial(joining_kernel, ((9, 3), (0, 3))),
         jax.ShapeDtypeStruct(cells.shape, jnp.bfloat16),
         scratch,
         2 * 10**9,
-        (cells, w_up, w_down, lower_own, lower_west, lower_south, lower_corner, upper),
+        (cells, w_up, w_down, lower_own, lower_west, lower_north, lower_northwest, upper),
     )
     return from_pairs(joined, levels)
 

time: 68.1 us -> 64.9 us (0.953)
  the two profiles are of different devices: /device:TPU:25 before, /device:TPU:41 now
where the time goes in v3:
time: 64.9 us; the launch traced here: 64.5 us
  starting transfers between devices  28.3 us (44%)
  Pallas kernels  21.7 us (33%)
  waiting for transfers between devices  12.3 us (19%)
  local copies, waits for them, and re-layouts  1.96 us (3%)
    ppermute x9, starting transfers between devices, shifted(): return lax.ppermute(array, axes, pairs)  28.3 us
    pallas_call x8, Pallas kernels, call(): pl.pallas_call(kernel, compiler_params=ROOM, out_shape=outs, in_specs=[VM...  21.4 us
    ppermute x9, waiting for transfers between devices, shifted(): return lax.ppermute(array, axes, pairs)  12.3 us
    unnamed x26, local copies, waits for them, and re-layouts  1.96 us
  transfers between devices with their start and end apart: 9, of which 4 were waited for; matrix products, arithmetic and copies ran while one was open for 0% of the time, Pallas kernels for 27%

profile of v3, /device:TPU:41, one launch (start us, length us, event | category | flops | bytes accessed | tf_op | source)
XLA Modules:
  0.0 64.5 jit_solution(5884870736296674567)
XLA Ops:
  0.0 1.2 %copy-done = bf16[3,2,12,12,512]{4,1,3,2,0:T(2,128)(2,1)S(1)} copy-done((bf16[3,2,12,12,512]{4,1,3,2,0:T(2,128)(2,1)S(1)}, bf16[3,2,12,12,512]{4,1,3,2,0:T(2,128)(2,1)}, u32[]{:S(2)}) %copy-start) | copy-done | bytes 884760
  1.2 0.7 %copy-done.2 = s32[2,12,12]{2,0,1:T(2,128)S(1)} copy-done((s32[2,12,12]{2,0,1:T(2,128)S(1)}, s32[2,12,12]{2,0,1:T(2,128)}, u32[]{:S(2)}) %copy-start.2) | copy-done | bytes 1176
  1.9 0.3 pack.1
  2.2 0.7 %collective-permute-start.1 = (bf16[219,8,128]{2,1,0:T(8,128)(2,1)S(1)}, bf16[219,8,128]{2,1,0:T(8,128)(2,1)S(1)}, u32[]{:S(2)}, u32[]{:S(2)}) collective-permute-start(bf16[219,8,128]{2,1,0:T(8,128)(2,1)S(1)} %get-tuple-element.21), channel_id=1, source_target_pairs={{0,240},{1,241},{2,242},{3,243},{4,244},{5,245},{6,246},{7,247},{8... | collective-permute-start | bytes 1345544 | tf_op jit(solution)/shard_map/ppermute | solution.py:49
  2.9 4.6 %collective-permute-start = (bf16[162,8,128]{2,1,0:T(8,128)(2,1)S(1)}, bf16[162,8,128]{2,1,0:T(8,128)(2,1)S(1)}, u32[]{:S(2)}, u32[]{:S(2)}) collective-permute-start(bf16[162,8,128]{2,1,0:T(8,128)(2,1)S(1)} %get-tuple-element.20.own), channel_id=1, source_target_pairs={{0,256},{1,257},{2,258},{3,259},{4,260},{5,261},{6,262},{7,263},{8... | collective-permute-start | bytes 995336 | tf_op jit(solution)/shard_map/ppermute | solution.py:49
  7.6 2.8 %collective-permute-done.1.east = bf16[219,8,128]{2,1,0:T(8,128)(2,1)S(1)} collective-permute-done((bf16[219,8,128]{2,1,0:T(8,128)(2,1)S(1)}, bf16[219,8,128]{2,1,0:T(8,128)(2,1)S(1)}, u32[]{:S(2)}, u32[]{:S(2)}) %collective-permute-start.1) | collective-permute-done | bytes 448544 | tf_op jit(solution)/shard_map/ppermute | solution.py:49
  10.4 4.6 %collective-permute-start.2 = (bf16[162,8,128]{2,1,0:T(8,128)(2,1)S(1)}, bf16[162,8,128]{2,1,0:T(8,128)(2,1)S(1)}, u32[]{:S(2)}, u32[]{:S(2)}) collective-permute-start(bf16[162,8,128]{2,1,0:T(8,128)(2,1)S(1)} %shard_map.118), channel_id=1, source_target_pairs={{0,256},{1,257},{2,258},{3,259},{4,260},{5,261},{6,262},{7,263},{8... | collective-permute-start | bytes 995336 | tf_op jit(solution)/shard_map/ppermute | solution.py:49
  15.1 3.7 %shard_map.119 = (bf16[432,512]{1,0:T(8,128)(2,1)S(1)}, f32[4,432,256]{2,1,0:T(8,128)S(1)}, f32[16,432]{1,0:T(8,128)S(1)}) custom-call(bf16[162,8,128]{2,1,0:T(8,128)(2,1)S(1)} %get-tuple-element.20.own, bf16[219,8,128]{2,1,0:T(8,128)(2,1)S(1)} %collective-permute-done.1.east, bf16[57,8,128]{2,1,0:T(8,128)(2,1)S(1)} %get-tuple-element.22.south.after.north, ...), custom_call_target="tpu_custom_call" | custom-call | flops 3000000000 | bytes 4000000 | tf_op jit(solution)/shard_map/pallas_call | solution.py:384
  18.8 0.0 copy-start.6
  18.8 11.4 %collective-permute-start.3 = (bf16[114,8,128]{2,1,0:T(8,128)(2,1)S(1)}, bf16[114,8,128]{2,1,0:T(8,128)(2,1)S(1)}, u32[]{:S(2)}, u32[]{:S(2)}) collective-permute-start(bf16[114,8,128]{2,1,0:T(8,128)(2,1)S(1)} %shard_map.120), channel_id=1, source_target_pairs={{0,271},{1,256},{2,257},{3,258},{4,259},{5,260},{6,261},{7,262},{8... | collective-permute-start | bytes 700424 | tf_op jit(solution)/shard_map/ppermute | solution.py:49
  30.2 2.1 %collective-permute-start.4 = (bf16[114,8,128]{2,1,0:T(8,128)(2,1)S(1)}, bf16[114,8,128]{2,1,0:T(8,128)(2,1)S(1)}, u32[]{:S(2)}, u32[]{:S(2)}) collective-permute-start(bf16[114,8,128]{2,1,0:T(8,128)(2,1)S(1)} %shard_map.120), channel_id=1, source_target_pairs={{0,15},{1,0},{2,1},{3,2},{4,3},{5,4},{6,5},{7,6},{8,7},{9,8},{10,9... | collective-permute-start | bytes 700424 | tf_op jit(solution)/shard_map/ppermute | solution.py:49
  32.3 0.0 collective-permute-done.own.south
  32.4 0.0 collective-permute-done.2.east
  32.4 0.0 copy-start.9
  32.4 0.0 copy-start.11
  32.4 3.7 %shard_map.121 = (bf16[108,8,128]{2,1,0:T(8,128)(2,1)S(1)}, bf16[108,8,128]{2,1,0:T(8,128)(2,1)S(1)}) custom-call(bf16[162,8,128]{2,1,0:T(8,128)(2,1)S(1)} %collective-permute-done.own.south, bf16[162,8,128]{2,1,0:T(8,128)(2,1)S(1)} %collective-permute-done.2.east, bf16[162,8,128]{2,1,0:T(8,128)(2,1)S(1)} %collective-permute-done.own.south, ...), custom_call_target="tpu_custom_call" | custom-call | flops 3000000000 | bytes 4000000 | tf_op jit(solution)/shard_map/pallas_call | solution.py:384
  36.1 0.1 collective-permute-start.8
  36.2 4.5 %collective-permute-done.4.south = bf16[114,8,128]{2,1,0:T(8,128)(2,1)S(1)} collective-permute-done((bf16[114,8,128]{2,1,0:T(8,128)(2,1)S(1)}, bf16[114,8,128]{2,1,0:T(8,128)(2,1)S(1)}, u32[]{:S(2)}, u32[]{:S(2)}) %collective-permute-start.4) | collective-permute-done | bytes 233504 | tf_op jit(solution)/shard_map/ppermute | solution.py:49
  40.7 3.7 %shard_map.122 = (bf16[432,512]{1,0:T(8,128)(2,1)S(1)}, f32[4,432,256]{2,1,0:T(8,128)S(1)}, f32[16,432]{1,0:T(8,128)S(1)}) custom-call(bf16[162,8,128]{2,1,0:T(8,128)(2,1)S(1)} %get-tuple-element.20.own, bf16[219,8,128]{2,1,0:T(8,128)(2,1)S(1)} %collective-permute-done.1.east, bf16[114,8,128]{2,1,0:T(8,128)(2,1)S(1)} %collective-permute-done.4.south, ...), custom_call_target="tpu_custom_call" | custom-call | flops 3000000000 | bytes 4000000 | tf_op jit(solution)/shard_map/pallas_call | solution.py:384
  44.4 0.0 collective-permute-done.3.south
  44.4 0.0 copy-start.1
  44.5 0.0 copy-start.3
  44.5 0.0 copy-start.4
  44.5 3.7 %shard_map.123 = (bf16[54,8,128]{2,1,0:T(8,128)(2,1)S(1)}, bf16[54,8,128]{2,1,0:T(8,128)(2,1)S(1)}, bf16[54,8,128]{2,1,0:T(8,128)(2,1)S(1)}, bf16[54,8,128]{2,1,0:T(8,128)(2,1)S(1)}) custom-call(bf16[162,8,128]{2,1,0:T(8,128)(2,1)S(1)} %collective-permute-done.own.south, bf16[162,8,128]{2,1,0:T(8,128)(2,1)S(1)} %collective-permute-done.2.east, ...), custom_call_target="tpu_custom_call" | custom-call | flops 3000000000 | bytes 4000000 | tf_op jit(solution)/shard_map/pallas_call | solution.py:384
  48.2 0.7 %collective-permute-start.5 = (bf16[54,8,128]{2,1,0:T(8,128)(2,1)S(1)}, bf16[54,8,128]{2,1,0:T(8,128)(2,1)S(1)}, u32[]{:S(2)}, u32[]{:S(2)}) collective-permute-start(bf16[54,8,128]{2,1,0:T(8,128)(2,1)S(1)} %get-tuple-element.31), channel_id=1, source_target_pairs={{0,16},{1,17},{2,18},{3,19},{4,20},{5,21},{6,22},{7,23},{8,24},{9,... | collective-permute-start | bytes 331784 | tf_op jit(solution)/shard_map/ppermute | solution.py:49
  48.9 1.9 %collective-permute-start.6 = (bf16[54,8,128]{2,1,0:T(8,128)(2,1)S(1)}, bf16[54,8,128]{2,1,0:T(8,128)(2,1)S(1)}, u32[]{:S(2)}, u32[]{:S(2)}) collective-permute-start(bf16[54,8,128]{2,1,0:T(8,128)(2,1)S(1)} %get-tuple-element.32), channel_id=1, source_target_pairs={{0,1},{1,2},{2,3},{3,4},{4,5},{5,6},{6,7},{7,8},{8,9},{9,10},{10,1... | collective-permute-start | bytes 331784 | tf_op jit(solution)/shard_map/ppermute | solution.py:49
  50.8 2.1 %collective-permute-start.7 = (bf16[54,8,128]{2,1,0:T(8,128)(2,1)S(1)}, bf16[54,8,128]{2,1,0:T(8,128)(2,1)S(1)}, u32[]{:S(2)}, u32[]{:S(2)}) collective-permute-start(bf16[54,8,128]{2,1,0:T(8,128)(2,1)S(1)} %get-tuple-element.33), channel_id=1, source_target_pairs={{0,17},{1,18},{2,19},{3,20},{4,21},{5,22},{6,23},{7,24},{8,25},{9,... | collective-permute-start | bytes 331784 | tf_op jit(solution)/shard_map/ppermute | solution.py:49
  53.0 2.8 %shard_map.124.rest_4_ = bf16[3,6,12,8,128]{4,3,2,1,0:T(8,128)(2,1)S(1)} custom-call(bf16[3,12,12,8,128]{4,3,2,1,0:T(8,128)(2,1)S(1)} %bitcast.18, bf16[512,2048]{1,0:T(8,128)(2,1)S(1)} %copy-done.3, bf16[2048,512]{1,0:T(8,128)(2,1)S(1)} %copy-done.4, bf16[108,8,128]{2,1,0:T(8,128)(2,1)S(1)} %get-tuple-element.26.after.rest_0_, ...), custom_call_target="tpu_custom_call" | custom-call | flops 2000000000 | bytes 4000000 | tf_op jit(solution)/shard_map/pallas_call | solution.py:384
  55.7 0.0 collective-permute-done.5.rest_1_
  55.8 2.9 %collective-permute-done.6.rest_2_ = bf16[54,8,128]{2,1,0:T(8,128)(2,1)S(1)} collective-permute-done((bf16[54,8,128]{2,1,0:T(8,128)(2,1)S(1)}, bf16[54,8,128]{2,1,0:T(8,128)(2,1)S(1)}, u32[]{:S(2)}, u32[]{:S(2)}) %collective-permute-start.6) | collective-permute-done | bytes 110624 | tf_op jit(solution)/shard_map/ppermute | solution.py:49
  58.6 2.1 %collective-permute-done.7.rest_3_ = bf16[54,8,128]{2,1,0:T(8,128)(2,1)S(1)} collective-permute-done((bf16[54,8,128]{2,1,0:T(8,128)(2,1)S(1)}, bf16[54,8,128]{2,1,0:T(8,128)(2,1)S(1)}, u32[]{:S(2)}, u32[]{:S(2)}) %collective-permute-start.7) | collective-permute-done | bytes 110624 | tf_op jit(solution)/shard_map/ppermute | solution.py:49
  60.7 3.8 %shard_map.125 = bf16[3,12,12,8,128]{4,3,2,1,0:T(8,128)(2,1)} custom-call(bf16[3,12,12,8,128]{4,3,2,1,0:T(8,128)(2,1)S(1)} %bitcast.19, bf16[512,2048]{1,0:T(8,128)(2,1)S(1)} %copy-done.3, bf16[2048,512]{1,0:T(8,128)(2,1)S(1)} %copy-done.4, bf16[54,8,128]{2,1,0:T(8,128)(2,1)S(1)} %get-tuple-element.30.rest_0_, ...), custom_call_target="tpu_custom_call" | custom-call | flops 2000000000 | bytes 4000000 | tf_op jit(solution)/shard_map/pallas_call | solution.py:384
  (21 shorter events, 0.1 us)
Async XLA Ops:
  0.0 15.0 %copy-start.7 = (f32[8]{0:T(128)S(1)}, f32[8]{0:T(128)}, u32[]{:S(2)}) copy-start(f32[8]{0:T(128)} %param.16) | copy-start | bytes 100
  0.0 15.0 %copy-start.8 = (f32[8]{0:T(128)S(1)}, f32[8]{0:T(128)}, u32[]{:S(2)}) copy-start(f32[8]{0:T(128)} %param.17) | copy-start | bytes 100
  0.0 1.2 %copy-start = (bf16[3,2,12,12,512]{4,1,3,2,0:T(2,128)(2,1)S(1)}, bf16[3,2,12,12,512]{4,1,3,2,0:T(2,128)(2,1)}, u32[]{:S(2)}) copy-start(bf16[3,2,12,12,512]{4,1,3,2,0:T(2,128)(2,1)} %param.12) | copy-start | bytes 2654212
  1.2 0.7 %copy-start.2 = (s32[2,12,12]{2,0,1:T(2,128)S(1)}, s32[2,12,12]{2,0,1:T(2,128)}, u32[]{:S(2)}) copy-start(s32[2,12,12]{2,0,1:T(2,128)} %param.13) | copy-start | bytes 3460
  1.9 13.1 %copy-start.5 = (bf16[512,1536]{1,0:T(8,128)(2,1)S(1)}, bf16[512,1536]{1,0:T(8,128)(2,1)}, u32[]{:S(2)}) copy-start(bf16[512,1536]{1,0:T(8,128)(2,1)} %w_qkv.7) | copy-start | bytes 4718596
  1.9 13.1 %copy-start.10 = (f32[96,432]{1,0:T(8,128)S(1)}, f32[96,432]{1,0:T(8,128)}, u32[]{:S(2)}) copy-start(f32[96,432]{1,0:T(8,128)} %constant.8.clone.pick_row) | copy-start | bytes 497668
  1.9 13.1 %copy-start.12 = (f32[16,432]{1,0:T(8,128)S(1)}, f32[16,432]{1,0:T(8,128)}, u32[]{:S(2)}) copy-start(f32[16,432]{1,0:T(8,128)} %constant.9.clone.pick_lane) | copy-start | bytes 82948
  2.2 8.1 %collective-permute-start.1 = (bf16[219,8,128]{2,1,0:T(8,128)(2,1)S(1)}, bf16[219,8,128]{2,1,0:T(8,128)(2,1)S(1)}, u32[]{:S(2)}, u32[]{:S(2)}) collective-permute-start(bf16[219,8,128]{2,1,0:T(8,128)(2,1)S(1)} %get-tuple-element.21), channel_id=1, source_target_pairs={{0,240},{1,241},{2,242},{3,243},{4,244},{5,245},{6,246},{7,247},{8... | collective-permute-start | bytes 1345544 | tf_op jit(solution)/shard_map/ppermute | solution.py:49
  2.9 29.4 %collective-permute-start = (bf16[162,8,128]{2,1,0:T(8,128)(2,1)S(1)}, bf16[162,8,128]{2,1,0:T(8,128)(2,1)S(1)}, u32[]{:S(2)}, u32[]{:S(2)}) collective-permute-start(bf16[162,8,128]{2,1,0:T(8,128)(2,1)S(1)} %get-tuple-element.20.own), channel_id=1, source_target_pairs={{0,256},{1,257},{2,258},{3,259},{4,260},{5,261},{6,262},{7,263},{8... | collective-permute-start | bytes 995336 | tf_op jit(solution)/shard_map/ppermute | solution.py:49
  10.4 22.0 %collective-permute-start.2 = (bf16[162,8,128]{2,1,0:T(8,128)(2,1)S(1)}, bf16[162,8,128]{2,1,0:T(8,128)(2,1)S(1)}, u32[]{:S(2)}, u32[]{:S(2)}) collective-permute-start(bf16[162,8,128]{2,1,0:T(8,128)(2,1)S(1)} %shard_map.118), channel_id=1, source_target_pairs={{0,256},{1,257},{2,258},{3,259},{4,260},{5,261},{6,262},{7,263},{8... | collective-permute-start | bytes 995336 | tf_op jit(solution)/shard_map/ppermute | solution.py:49
  18.8 13.6 %copy-start.6 = (bf16[512,512]{1,0:T(8,128)(2,1)S(1)}, bf16[512,512]{1,0:T(8,128)(2,1)}, u32[]{:S(2)}) copy-start(bf16[512,512]{1,0:T(8,128)(2,1)} %w_out.3) | copy-start | bytes 1572868
  18.8 25.6 %collective-permute-start.3 = (bf16[114,8,128]{2,1,0:T(8,128)(2,1)S(1)}, bf16[114,8,128]{2,1,0:T(8,128)(2,1)S(1)}, u32[]{:S(2)}, u32[]{:S(2)}) collective-permute-start(bf16[114,8,128]{2,1,0:T(8,128)(2,1)S(1)} %shard_map.120), channel_id=1, source_target_pairs={{0,271},{1,256},{2,257},{3,258},{4,259},{5,260},{6,261},{7,262},{8... | collective-permute-start | bytes 700424 | tf_op jit(solution)/shard_map/ppermute | solution.py:49
  30.2 10.5 %collective-permute-start.4 = (bf16[114,8,128]{2,1,0:T(8,128)(2,1)S(1)}, bf16[114,8,128]{2,1,0:T(8,128)(2,1)S(1)}, u32[]{:S(2)}, u32[]{:S(2)}) collective-permute-start(bf16[114,8,128]{2,1,0:T(8,128)(2,1)S(1)} %shard_map.120), channel_id=1, source_target_pairs={{0,15},{1,0},{2,1},{3,2},{4,3},{5,4},{6,5},{7,6},{8,7},{9,8},{10,9... | collective-permute-start | bytes 700424 | tf_op jit(solution)/shard_map/ppermute | solution.py:49
  32.4 8.3 %copy-start.9 = (f32[96,432]{1,0:T(8,128)S(1)}, f32[96,432]{1,0:T(8,128)}, u32[]{:S(2)}) copy-start(f32[96,432]{1,0:T(8,128)} %constant.10.clone.pick_row) | copy-start | bytes 497668
  32.4 8.3 %copy-start.11 = (f32[16,432]{1,0:T(8,128)S(1)}, f32[16,432]{1,0:T(8,128)}, u32[]{:S(2)}) copy-start(f32[16,432]{1,0:T(8,128)} %constant.11.clone.pick_lane) | copy-start | bytes 82948
  36.1 16.8 %collective-permute-start.8 = (bf16[108,8,128]{2,1,0:T(8,128)(2,1)S(1)}, bf16[108,8,128]{2,1,0:T(8,128)(2,1)S(1)}, u32[]{:S(2)}, u32[]{:S(2)}) collective-permute-start(bf16[108,8,128]{2,1,0:T(8,128)(2,1)S(1)} %get-tuple-element.34), channel_id=1, source_target_pairs={{0,16},{1,17},{2,18},{3,19},{4,20},{5,21},{6,22},{7,23},{8,24},{9,... | collective-permute-start | bytes 663560 | tf_op jit(solution)/shard_map/ppermute | solution.py:49
  44.4 8.5 %copy-start.1 = (bf16[3,2,12,12,512]{4,1,3,2,0:T(2,128)(2,1)S(1)}, bf16[3,2,12,12,512]{4,1,3,2,0:T(2,128)(2,1)}, u32[]{:S(2)}) copy-start(bf16[3,2,12,12,512]{4,1,3,2,0:T(2,128)(2,1)} %param.12) | copy-start | bytes 2654212
  44.5 8.5 %copy-start.3 = (bf16[512,2048]{1,0:T(8,128)(2,1)S(1)}, bf16[512,2048]{1,0:T(8,128)(2,1)}, u32[]{:S(2)}) copy-start(bf16[512,2048]{1,0:T(8,128)(2,1)} %w_up.3) | copy-start | bytes 6291460
  44.5 8.5 %copy-start.4 = (bf16[2048,512]{1,0:T(8,128)(2,1)S(1)}, bf16[2048,512]{1,0:T(8,128)(2,1)}, u32[]{:S(2)}) copy-start(bf16[2048,512]{1,0:T(8,128)(2,1)} %w_down.3) | copy-start | bytes 6291460
  48.2 7.6 %collective-permute-start.5 = (bf16[54,8,128]{2,1,0:T(8,128)(2,1)S(1)}, bf16[54,8,128]{2,1,0:T(8,128)(2,1)S(1)}, u32[]{:S(2)}, u32[]{:S(2)}) collective-permute-start(bf16[54,8,128]{2,1,0:T(8,128)(2,1)S(1)} %get-tuple-element.31), channel_id=1, source_target_pairs={{0,16},{1,17},{2,18},{3,19},{4,20},{5,21},{6,22},{7,23},{8,24},{9,... | collective-permute-start | bytes 331784 | tf_op jit(solution)/shard_map/ppermute | solution.py:49
  48.9 9.8 %collective-permute-start.6 = (bf16[54,8,128]{2,1,0:T(8,128)(2,1)S(1)}, bf16[54,8,128]{2,1,0:T(8,128)(2,1)S(1)}, u32[]{:S(2)}, u32[]{:S(2)}) collective-permute-start(bf16[54,8,128]{2,1,0:T(8,128)(2,1)S(1)} %get-tuple-element.32), channel_id=1, source_target_pairs={{0,1},{1,2},{2,3},{3,4},{4,5},{5,6},{6,7},{7,8},{8,9},{9,10},{10,1... | collective-permute-start | bytes 331784 | tf_op jit(solution)/shard_map/ppermute | solution.py:49
  50.8 10.0 %collective-permute-start.7 = (bf16[54,8,128]{2,1,0:T(8,128)(2,1)S(1)}, bf16[54,8,128]{2,1,0:T(8,128)(2,1)S(1)}, u32[]{:S(2)}, u32[]{:S(2)}) collective-permute-start(bf16[54,8,128]{2,1,0:T(8,128)(2,1)S(1)} %get-tuple-element.33), channel_id=1, source_target_pairs={{0,17},{1,18},{2,19},{3,20},{4,21},{5,22},{6,23},{7,24},{8,25},{9,... | collective-permute-start | bytes 331784 | tf_op jit(solution)/shard_map/ppermute | solution.py:49

commit v4 on v3

--- a/solution.py
+++ b/solution.py
@@ -10,6 +10,7 @@
 
 
 LANES = 128
+SH_LAT = 3
 LOG2E = 1.4426950408889634
 EXCLUDED = -1e30
 VMEM = pl.BlockSpec(memory_space=pltpu.VMEM)
@@ -120,8 +121,10 @@
     return pick_row, pick_lane
 
 
-def pack_kernel(cells, mask, own, west, north, flags, sems):
+def pack_kernel(cells, mask_hbm, own, west, north, flags, mask, sems):
     copies = []
+    mask_copy = pltpu.make_async_copy(mask_hbm, mask, sems.at[1])
+    mask_copy.start()
     for g in range(3):
         for dst, first, lats, lons in (
             (west, 0, (3, 9), (0, 6)),
@@ -136,12 +139,13 @@
                 pltpu.make_async_copy(
                     cells.at[g, lats[0] : lats[1], lons[0] : lons[1]],
                     dst.at[pl.ds(first + g * rows * 6, rows * 6)].reshape(rows, 6, 8, LANES),
-                    sems,
+                    sems.at[0],
                 )
             )
     for copy in copies:
         copy.start()
     flags[...] = jnp.zeros(flags.shape, jnp.float32)
+    mask_copy.wait()
     for lat in range(12):
         flags[2 * lat : 2 * lat + 2, 0:12] = mask[lat].astype(jnp.float32)
     tile = flags[...].astype(jnp.bfloat16).reshape(3, 8, LANES)
@@ -210,6 +214,27 @@
         cells_to_tokens([south[0:108]], cells_scr, tokens_scr, 216)
 
 
+def project(normed, w_qkv, logit_scale, head_size):
+    width = w_qkv.shape[0]
+    head = lax.broadcasted_iota(jnp.int32, (1, width), 1) // head_size
+    scale = jnp.zeros((1, width), jnp.float32)
+    for i in range(width // head_size):
+        scale = jnp.where(head == i, logit_scale[0:1, i : i + 1] * (LOG2E / head_size), scale)
+    mixed = jnp.dot(normed, w_qkv[:, :width], preferred_element_type=jnp.float32)
+    queries = unit_heads(mixed, head_size) * scale
+    mixed = jnp.dot(normed, w_qkv[:, width : 2 * width], preferred_element_type=jnp.float32)
+    keys = unit_heads(mixed, head_size)
+    values = jnp.dot(normed, w_qkv[:, 2 * width :], preferred_element_type=jnp.float32)
+    return queries, keys, values
+
+
+def early_kernel(head_size, own, w_qkv, logit_scale, out, cells_scr, tokens_scr):
+    cells_to_tokens([own[0:108]], cells_scr, tokens_scr, 0)
+    normed = layer_norm(whole_rows(tokens_scr)).astype(jnp.bfloat16)
+    for i, part in enumerate(project(normed, w_qkv, logit_scale, head_size)):
+        out[i] = part
+
+
 def own_kernel(
     head_size,
     window,
@@ -231,8 +256,10 @@
     key_scr,
     value_scr,
 ):
-    gather(window, own, east, south, cells_scr, tokens_scr)
-    width = w_qkv.shape[0]
+    if window == 0:
+        cells_to_tokens([east[0:108]], cells_scr, tokens_scr, 216)
+    else:
+        gather(window, own, east, south, cells_scr, tokens_scr)
     marks = [north[54:57], east[216:219]]
     if window == 1:
         marks += [south[108:111], south[111:114]]
@@ -258,18 +285,17 @@
         excluded = jnp.where(last, EXCLUDED, 0.0)
         bias_out[0:8, :] = bias + jnp.where(later, excluded, 0.0)
         bias_out[8:16, :] = bias + jnp.where(later, 0.0, excluded)
-    head = lax.broadcasted_iota(jnp.int32, (1, width), 1) // head_size
-    scale = jnp.zeros((1, width), jnp.float32)
-    for i in range(heads):
-        scale = jnp.where(head == i, logit_scale[0:1, i : i + 1] * (LOG2E / head_size), scale)
-    normed = layer_norm(whole_rows(tokens_scr)).astype(jnp.bfloat16)
-    mixed = jnp.dot(normed, w_qkv[:, :width], preferred_element_type=jnp.float32)
-    query_out[...] = (unit_heads(mixed, head_size) * scale).astype(jnp.bfloat16)
-    mixed = jnp.dot(normed, w_qkv[:, width : 2 * width], preferred_element_type=jnp.float32)
-    key_scr[...] = unit_heads(mixed, head_size).astype(jnp.bfloat16)
-    value_scr[...] = jnp.dot(
-        normed, w_qkv[:, 2 * width :], preferred_element_type=jnp.float32
-    ).astype(jnp.bfloat16)
+    tokens = whole_rows(tokens_scr)
+    if window == 0:
+        half = tokens.shape[0] // 2
+        normed = layer_norm(tokens[half:]).astype(jnp.bfloat16)
+        parts = project(normed, w_qkv, logit_scale, head_size)
+        parts = [jnp.concatenate([south[i], part], 0) for i, part in enumerate(parts)]
+    else:
+        normed = layer_norm(tokens).astype(jnp.bfloat16)
+        parts = project(normed, w_qkv, logit_scale, head_size)
+    for ref, part in zip((query_out, key_scr, value_scr), parts):
+        ref[...] = part.astype(jnp.bfloat16)
 
     def store(pair, at, total):
         total_out[pair] = total
@@ -291,6 +317,8 @@
     *rest,
 ):
     outs, (cells_scr, tokens_scr, key_scr, value_scr, attended_scr) = rest[:-5], rest[-5:]
+    if window == 1:
+        upper_east, outs = outs[0], outs[1:]
     gather(window, own, east, south, cells_scr, tokens_scr)
     width = w_qkv.shape[0]
     normed = layer_norm(whole_rows(tokens_scr)).astype(jnp.bfloat16)
@@ -324,49 +352,60 @@
         put(0, 108, [(outs[0], 108)])
         put(216, 108, [(outs[1], 108)])
     else:
-        put(0, 108, [(outs[0], 54), (outs[1], 54)])
+        put(0, 108, [(outs[0], 54), (outs[1].at[0:54], 54)])
         put(216, 108, [(outs[2], 54), (outs[3], 54)])
-
-
-def joining_kernel(bands, fields, w_up, w_down, *rest):
-    pieces, (out, cells_scr, tokens_scr) = rest[: 2 * len(bands)], rest[-3:]
+        outs[1][54:162] = upper_east[...]
+
+
+def joining_kernel(bands, batches, fields, w_up, w_down, *rest):
+    pieces, rest = rest[: 2 * len(bands)], rest[2 * len(bands) :]
+    copies = []
     if len(bands) == 2:
-        out[:, 3:9] = rest[2 * len(bands)][...]
-    for g in range(fields.shape[0]):
-        at = 0
-        for band, (first, rows) in enumerate(bands):
-            for side, lons in enumerate(((6, 12), (0, 6))):
-                size = rows * 6
-                term = pieces[2 * band + side][g * size : (g + 1) * size].astype(jnp.float32)
-                term = term.reshape(rows, 6, 8, LANES)
-                summed = fields[g, first : first + rows, lons[0] : lons[1]].astype(jnp.float32)
-                summed = (summed + term).astype(jnp.bfloat16).astype(jnp.float32)
-                cells_scr[g, at : at + rows, lons[0] : lons[1]] = summed
-            at += rows
-        cells = at * 12
-        flat = cells_scr.at[g].reshape(cells * 8, LANES)
+        out, cells_scr, tokens_scr = rest
+    else:
+        done, out, cells_scr, tokens_scr, rounded, sems = rest
+        copies.append(pltpu.make_async_copy(done, out.at[:, 3:12], sems.at[0]))
+        copies[0].start()
+    for batch, (start, stop) in enumerate(batches):
+        for g in range(start, stop):
+            at = 0
+            for band, (first, rows, skips) in enumerate(bands):
+                for side, lons in enumerate(((6, 12), (0, 6))):
+                    size = rows * 6
+                    begin = skips[side] + g * size
+                    term = pieces[2 * band + side][begin : begin + size].astype(jnp.float32)
+                    term = term.reshape(rows, 6, 8, LANES)
+                    summed = fields[g, first : first + rows, lons[0] : lons[1]]
+                    summed = (summed.astype(jnp.float32) + term).astype(jnp.bfloat16)
+                    cells_scr[g, at : at + rows, lons[0] : lons[1]] = summed.astype(jnp.float32)
+                at += rows
+        cells = (stop - start) * at * 12
+        flat = cells_scr.at[start:stop].reshape(cells * 8, LANES)
         for level in range(2):
             for tile in range(4):
                 tokens_scr[
-                    g, level * cells : (level + 1) * cells, tile * LANES : (tile + 1) * LANES
+                    batch, level * cells : (level + 1) * cells, tile * LANES : (tile + 1) * LANES
                 ] = flat[pl.ds(2 * tile + level, cells, stride=8), :]
-        residual = tokens_scr[g]
+        residual = tokens_scr[batch]
         normed = layer_norm(residual).astype(jnp.bfloat16)
         hidden = jnp.dot(normed, w_up[...], preferred_element_type=jnp.float32)
         hidden = jax.nn.gelu(hidden, approximate=True).astype(jnp.bfloat16)
-        joined = residual + jnp.dot(hidden, w_down[...], preferred_element_type=jnp.float32)
+        tokens_scr[batch] = residual + jnp.dot(
+            hidden, w_down[...], preferred_element_type=jnp.float32
+        )
         for level in range(2):
             for tile in range(4):
-                flat[pl.ds(2 * tile + level, cells, stride=8), :] = joined[
-                    level * cells : (level + 1) * cells, tile * LANES : (tile + 1) * LANES
+                flat[pl.ds(2 * tile + level, cells, stride=8), :] = tokens_scr[
+                    batch, level * cells : (level + 1) * cells, tile * LANES : (tile + 1) * LANES
                 ]
-        if len(bands) == 1:
-            out[g] = cells_scr[g].astype(jnp.bfloat16)
-        else:
-            at = 0
-            for first, rows in bands:
-                out[g, first : first + rows] = cells_scr[g, at : at + rows].astype(jnp.bfloat16)
-                at += rows
+        if len(bands) == 2:
+            out[start:stop] = cells_scr[start:stop].astype(jnp.bfloat16)
+    if len(bands) == 1:
+        rounded[...] = cells_scr[...].astype(jnp.bfloat16)
+        copies.append(pltpu.make_async_copy(rounded, out.at[:, 0:3], sems.at[1]))
+        copies[1].start()
+    for copy in copies:
+        copy.wait()
 
 
 def per_device(fields, surface_mask, w_qkv, w_out, logit_scale, mask_bias, w_up, w_down):
@@ -380,13 +419,13 @@
     def pieces(*counts):
         return tuple(jax.ShapeDtypeStruct((n,) + tile, jnp.bfloat16) for n in counts)
 
-    def call(kernel, outs, scratch, flops, arrays):
+    def call(kernel, outs, scratch, flops, arrays, space=VMEM):
         return pl.pallas_call(
             kernel,
             compiler_params=ROOM,
             out_shape=outs,
             in_specs=[VMEM] * len(arrays),
-            out_specs=jax.tree.map(lambda _: VMEM, outs),
+            out_specs=jax.tree.map(lambda _: space, outs),
             scratch_shapes=scratch,
             cost_estimate=pl.CostEstimate(
                 flops=flops, bytes_accessed=4 * 10**6, transcendentals=10**6
@@ -398,10 +437,17 @@
         name="pack",
         compiler_params=ROOM,
         out_shape=pieces(162, 219, 57),
-        in_specs=[pl.BlockSpec(memory_space=pltpu.HBM), VMEM],
+        in_specs=[pl.BlockSpec(memory_space=pltpu.HBM)] * 2,
         out_specs=(VMEM, VMEM, VMEM),
-        scratch_shapes=[pltpu.VMEM((24, LANES), jnp.float32), pltpu.SemaphoreType.DMA],
-    )(cells, jnp.transpose(surface_mask, (1, 0, 2)))
+        scratch_shapes=[
+            pltpu.VMEM((24, LANES), jnp.float32),
+            pltpu.VMEM((lat_rows, levels, lon_cells), jnp.int32),
+            pltpu.SemaphoreType.DMA((2,)),
+        ],
+    )(
+        pltpu.with_memory_space_constraint(cells, pltpu.HBM),
+        pltpu.with_memory_space_constraint(jnp.transpose(surface_mask, (1, 0, 2)), pltpu.HBM),
+    )
     east = shifted(west, lon=-1)
     own_across = shifted(own, across=True)
     east_again = call(again_kernel, pieces(162)[0], [], 10**6, (east,))
@@ -433,47 +479,67 @@
             arrays + (w_qkv, logit_scale[None], mask_bias[None], pick_row, pick_lane),
         )
 
-    def partner_part(window, counts, arrays, first):
+    def partner_part(window, counts, arrays, first, more):
         return call(
             functools.partial(partner_kernel, head_size, window),
             pieces(*counts),
             late,
             3 * 10**9,
-            arrays + tuple(first) + (w_qkv, w_out),
+            arrays + tuple(first) + (w_qkv, w_out) + more,
         )
 
-    first = own_part(0, (own, east, north, north, north))
+    early = call(
+        functools.partial(early_kernel, head_size),
+        jax.ShapeDtypeStruct((3, half // 2, width), jnp.float32),
+        [
+            pltpu.VMEM((half * 2, LANES), jnp.float32),
+            pltpu.VMEM((4, half // 2, LANES), jnp.float32),
+        ],
+        3 * 10**8,
+        (own, w_qkv, logit_scale[None]),
+    )
+    first = own_part(0, (own, east, early, north, north))
     south = call(southward_kernel, pieces(114)[0], [], 10**6, (east, north, first[2]))
     south_across = shifted(south, lat=-1, across=True)
     south = shifted(south, lat=-1)
     upper_own, upper_east = partner_part(
-        0, (108, 108), (own_across, east_across, own_across), first
-    )
-    upper_west = shifted(upper_east, lon=1)
+        0, (108, 108), (own_across, east_across, own_across), first, ()
+    )
     first = own_part(1, (own, east, south, upper_own, north))
-    lower_own, lower_east, lower_south, lower_corner = partner_part(
-        1, (54, 54, 54, 54), (own_across, east_across, south_across), first
-    )
+    lower_own, all_east, lower_south, lower_corner = partner_part(
+        1, (54, 162, 54, 54), (own_across, east_across, south_across), first, (upper_east,)
+    )
+    west = shifted(all_east, lon=1)
+    lower_northwest = shifted(lower_corner, lon=1, lat=1)
     lower_north = shifted(lower_south, lat=1)
-    lower_northwest = shifted(lower_corner, lon=1, lat=1)
-    lower_west = shifted(lower_east, lon=1)
-    scratch = [
-        pltpu.VMEM((groups, lat_rows // 2, lon_cells) + tile, jnp.float32),
-        pltpu.VMEM((groups, half // groups, width), jnp.float32),
-    ]
+    rest = (groups, lat_rows - SH_LAT, lon_cells) + tile
+    edge = (groups, SH_LAT, lon_cells) + tile
     upper = call(
-        functools.partial(joining_kernel, ((3, 6),)),
-        jax.ShapeDtypeStruct((groups, lat_rows // 2) + cells.shape[2:], jnp.bfloat16),
-        scratch,
-        2 * 10**9,
-        (cells, w_up, w_down, upper_own, upper_west),
+        functools.partial(
+            joining_kernel,
+            ((3, 6, (0, 54)), (9, 3, (0, 0))),
+            [(g, g + 1) for g in range(groups)],
+        ),
+        jax.ShapeDtypeStruct(rest, jnp.bfloat16),
+        [
+            pltpu.VMEM(rest, jnp.float32),
+            pltpu.VMEM((groups, half // 2, width), jnp.float32),
+        ],
+        3 * 10**9,
+        (cells, w_up, w_down, upper_own, west, lower_own, west),
     )
     joined = call(
-        functools.partial(joining_kernel, ((9, 3), (0, 3))),
+        functools.partial(joining_kernel, ((0, 3, (0, 0)),), [(0, groups)]),
         jax.ShapeDtypeStruct(cells.shape, jnp.bfloat16),
-        scratch,
-        2 * 10**9,
-        (cells, w_up, w_down, lower_own, lower_west, lower_north, lower_northwest, upper),
+        [
+            pltpu.VMEM(edge, jnp.float32),
+            pltpu.VMEM((1, half // 2, width), jnp.float32),
+            pltpu.VMEM(edge, jnp.bfloat16),
+            pltpu.SemaphoreType.DMA((2,)),
+        ],
+        10**9,
+        (cells, w_up, w_down, lower_north, lower_northwest, upper),
+        pl.BlockSpec(memory_space=pltpu.HBM),
     )
     return from_pairs(joined, levels)
 

time: 64.9 us -> 60.9 us (0.938)
  the two profiles are of different devices: /device:TPU:41 before, /device:TPU:4 now
where the time goes in v4:
time: 60.9 us; the launch traced here: 60.6 us
  starting transfers between devices  31.8 us (52%)
  Pallas kernels  23.2 us (38%)
  waiting for transfers between devices  5.03 us (8%)
    ppermute x8, starting transfers between devices, shifted(): return lax.ppermute(array, axes, pairs)  31.8 us
    pallas_call x9, Pallas kernels, call(): pl.pallas_call(kernel, compiler_params=ROOM, out_shape=outs, in_specs=[VM...  21.9 us
    ppermute x8, waiting for transfers between devices, shifted(): return lax.ppermute(array, axes, pairs)  5.03 us
    pallas_call x1, Pallas kernels, per_device(): pl.pallas_call(pack_kernel, name='pack', compiler_params=ROOM, out_shape=...  1.35 us
  transfers between devices with their start and end apart: 8, of which 3 were waited for; matrix products, arithmetic and copies ran while one was open for 0% of the time, Pallas kernels for 26%

profile of v4, /device:TPU:4, one launch (start us, length us, event | category | flops | bytes accessed | tf_op | source)
XLA Modules:
  0.0 60.6 jit_solution(18108727855154699912)
XLA Ops:
  0.0 1.3 %pack.1 = (bf16[162,8,128]{2,1,0:T(8,128)(2,1)S(1)}, bf16[219,8,128]{2,1,0:T(8,128)(2,1)S(1)}, bf16[57,8,128]{2,1,0:T(8,128)(2,1)S(1)}) custom-call(bf16[3,12,12,8,128]{4,3,2,1,0:T(8,128)(2,1)} %bitcast.17, s32[12,2,12]{2,1,0:T(2,128)} %bitcast.25), custom_call_target="tpu_custom_call" | custom-call | tf_op jit(solution)/shard_map/pack/pallas_call | solution.py:435
  1.4 2.9 %collective-permute-start.1 = (bf16[219,8,128]{2,1,0:T(8,128)(2,1)S(1)}, bf16[219,8,128]{2,1,0:T(8,128)(2,1)S(1)}, u32[]{:S(2)}, u32[]{:S(2)}) collective-permute-start(bf16[219,8,128]{2,1,0:T(8,128)(2,1)S(1)} %get-tuple-element.21), channel_id=1, source_target_pairs={{0,240},{1,241},{2,242},{3,243},{4,244},{5,245},{6,246},{7,247},{8... | collective-permute-start | bytes 1345544 | tf_op jit(solution)/shard_map/ppermute | solution.py:50
  4.3 4.9 %collective-permute-start = (bf16[162,8,128]{2,1,0:T(8,128)(2,1)S(1)}, bf16[162,8,128]{2,1,0:T(8,128)(2,1)S(1)}, u32[]{:S(2)}, u32[]{:S(2)}) collective-permute-start(bf16[162,8,128]{2,1,0:T(8,128)(2,1)S(1)} %get-tuple-element.20.own), channel_id=1, source_target_pairs={{0,256},{1,257},{2,258},{3,259},{4,260},{5,261},{6,262},{7,263},{8... | collective-permute-start | bytes 995336 | tf_op jit(solution)/shard_map/ppermute | solution.py:50
  9.2 1.0 %collective-permute-done.1.east = bf16[219,8,128]{2,1,0:T(8,128)(2,1)S(1)} collective-permute-done((bf16[219,8,128]{2,1,0:T(8,128)(2,1)S(1)}, bf16[219,8,128]{2,1,0:T(8,128)(2,1)S(1)}, u32[]{:S(2)}, u32[]{:S(2)}) %collective-permute-start.1) | collective-permute-done | bytes 448544 | tf_op jit(solution)/shard_map/ppermute | solution.py:50
  10.2 0.0 copy-start.6
  10.2 0.0 copy-start.8
  10.2 0.0 copy-start.10
  10.2 5.0 %collective-permute-start.2 = (bf16[162,8,128]{2,1,0:T(8,128)(2,1)S(1)}, bf16[162,8,128]{2,1,0:T(8,128)(2,1)S(1)}, u32[]{:S(2)}, u32[]{:S(2)}) collective-permute-start(bf16[162,8,128]{2,1,0:T(8,128)(2,1)S(1)} %shard_map.118), channel_id=1, source_target_pairs={{0,256},{1,257},{2,258},{3,259},{4,260},{5,261},{6,262},{7,263},{8... | collective-permute-start | bytes 995336 | tf_op jit(solution)/shard_map/ppermute | solution.py:50
  15.3 1.0 %shard_map.119.south = f32[3,216,512]{2,1,0:T(8,128)S(1)} custom-call(bf16[162,8,128]{2,1,0:T(8,128)(2,1)S(1)} %get-tuple-element.20.own, bf16[512,1536]{1,0:T(8,128)(2,1)S(1)} %copy-done.3, f32[1,8]{1,0:T(1,128)S(1)} %bitcast.20), custom_call_target="tpu_custom_call" | custom-call | flops 300000000 | bytes 4000000 | tf_op jit(solution)/shard_map/pallas_call | solution.py:423
  16.3 3.3 %shard_map.120 = (bf16[432,512]{1,0:T(8,128)(2,1)S(1)}, f32[4,432,256]{2,1,0:T(8,128)S(1)}, f32[16,432]{1,0:T(8,128)S(1)}) custom-call(bf16[162,8,128]{2,1,0:T(8,128)(2,1)S(1)} %get-tuple-element.20.own, bf16[219,8,128]{2,1,0:T(8,128)(2,1)S(1)} %collective-permute-done.1.east, f32[3,216,512]{2,1,0:T(8,128)S(1)} %shard_map.119.south, ...), custom_call_target="tpu_custom_call" | custom-call | flops 3000000000 | bytes 4000000 | tf_op jit(solution)/shard_map/pallas_call | solution.py:423
  19.6 0.0 copy-start.5
  19.6 10.2 %collective-permute-start.4 = (bf16[114,8,128]{2,1,0:T(8,128)(2,1)S(1)}, bf16[114,8,128]{2,1,0:T(8,128)(2,1)S(1)}, u32[]{:S(2)}, u32[]{:S(2)}) collective-permute-start(bf16[114,8,128]{2,1,0:T(8,128)(2,1)S(1)} %shard_map.121), channel_id=1, source_target_pairs={{0,15},{1,0},{2,1},{3,2},{4,3},{5,4},{6,5},{7,6},{8,7},{9,8},{10,9... | collective-permute-start | bytes 700424 | tf_op jit(solution)/shard_map/ppermute | solution.py:50
  29.8 3.6 %collective-permute-start.3 = (bf16[114,8,128]{2,1,0:T(8,128)(2,1)S(1)}, bf16[114,8,128]{2,1,0:T(8,128)(2,1)S(1)}, u32[]{:S(2)}, u32[]{:S(2)}) collective-permute-start(bf16[114,8,128]{2,1,0:T(8,128)(2,1)S(1)} %shard_map.121), channel_id=1, source_target_pairs={{0,271},{1,256},{2,257},{3,258},{4,259},{5,260},{6,261},{7,262},{8... | collective-permute-start | bytes 700424 | tf_op jit(solution)/shard_map/ppermute | solution.py:50
  33.4 0.0 collective-permute-done.own.south
  33.4 0.0 collective-permute-done.2.east
  33.4 0.0 copy-start.7
  33.4 0.0 copy-start.9
  33.5 3.7 %shard_map.122 = (bf16[108,8,128]{2,1,0:T(8,128)(2,1)S(1)}, bf16[108,8,128]{2,1,0:T(8,128)(2,1)S(1)}) custom-call(bf16[162,8,128]{2,1,0:T(8,128)(2,1)S(1)} %collective-permute-done.own.south, bf16[162,8,128]{2,1,0:T(8,128)(2,1)S(1)} %collective-permute-done.2.east, bf16[162,8,128]{2,1,0:T(8,128)(2,1)S(1)} %collective-permute-done.own.south, ...), custom_call_target="tpu_custom_call" | custom-call | flops 3000000000 | bytes 4000000 | tf_op jit(solution)/shard_map/pallas_call | solution.py:423
  37.1 0.0 collective-permute-done.4.south
  37.2 3.7 %shard_map.123 = (bf16[432,512]{1,0:T(8,128)(2,1)S(1)}, f32[4,432,256]{2,1,0:T(8,128)S(1)}, f32[16,432]{1,0:T(8,128)S(1)}) custom-call(bf16[162,8,128]{2,1,0:T(8,128)(2,1)S(1)} %get-tuple-element.20.own, bf16[219,8,128]{2,1,0:T(8,128)(2,1)S(1)} %collective-permute-done.1.east, bf16[114,8,128]{2,1,0:T(8,128)(2,1)S(1)} %collective-permute-done.4.south, ...), custom_call_target="tpu_custom_call" | custom-call | flops 3000000000 | bytes 4000000 | tf_op jit(solution)/shard_map/pallas_call | solution.py:423
  40.9 0.0 copy-start
  40.9 0.0 copy-start.1
  40.9 0.0 copy-start.2
  40.9 3.7 %shard_map.124 = (bf16[54,8,128]{2,1,0:T(8,128)(2,1)S(1)}, bf16[162,8,128]{2,1,0:T(8,128)(2,1)S(1)}, bf16[54,8,128]{2,1,0:T(8,128)(2,1)S(1)}, bf16[54,8,128]{2,1,0:T(8,128)(2,1)S(1)}) custom-call(bf16[162,8,128]{2,1,0:T(8,128)(2,1)S(1)} %collective-permute-done.own.south, bf16[162,8,128]{2,1,0:T(8,128)(2,1)S(1)} %collective-permute-done.2.east, ...), custom_call_target="tpu_custom_call" | custom-call | flops 3000000000 | bytes 4000000 | tf_op jit(solution)/shard_map/pallas_call | solution.py:423
  44.7 0.0 collective-permute-start.7
  44.7 3.1 %collective-permute-start.5 = (bf16[54,8,128]{2,1,0:T(8,128)(2,1)S(1)}, bf16[54,8,128]{2,1,0:T(8,128)(2,1)S(1)}, u32[]{:S(2)}, u32[]{:S(2)}) collective-permute-start(bf16[54,8,128]{2,1,0:T(8,128)(2,1)S(1)} %get-tuple-element.31), channel_id=1, source_target_pairs={{0,1},{1,2},{2,3},{3,4},{4,5},{5,6},{6,7},{7,8},{8,9},{9,10},{10,1... | collective-permute-start | bytes 331784 | tf_op jit(solution)/shard_map/ppermute | solution.py:50
  47.8 2.1 %collective-permute-start.6 = (bf16[54,8,128]{2,1,0:T(8,128)(2,1)S(1)}, bf16[54,8,128]{2,1,0:T(8,128)(2,1)S(1)}, u32[]{:S(2)}, u32[]{:S(2)}) collective-permute-start(bf16[54,8,128]{2,1,0:T(8,128)(2,1)S(1)} %get-tuple-element.32), channel_id=1, source_target_pairs={{0,17},{1,18},{2,19},{3,20},{4,21},{5,22},{6,23},{7,24},{8,25},{9,... | collective-permute-start | bytes 331784 | tf_op jit(solution)/shard_map/ppermute | solution.py:50
  49.9 2.5 %collective-permute-done.7.rest_1_.rest_3_ = bf16[162,8,128]{2,1,0:T(8,128)(2,1)S(1)} collective-permute-done((bf16[162,8,128]{2,1,0:T(8,128)(2,1)S(1)}, bf16[162,8,128]{2,1,0:T(8,128)(2,1)S(1)}, u32[]{:S(2)}, u32[]{:S(2)}) %collective-permute-start.7) | collective-permute-done | bytes 331808 | tf_op jit(solution)/shard_map/ppermute | solution.py:50
  52.4 4.1 %shard_map.125.rest_2_ = bf16[3,9,12,8,128]{4,3,2,1,0:T(8,128)(2,1)S(1)} custom-call(bf16[3,12,12,8,128]{4,3,2,1,0:T(8,128)(2,1)S(1)} %bitcast.18, bf16[512,2048]{1,0:T(8,128)(2,1)S(1)} %copy-done.1, bf16[2048,512]{1,0:T(8,128)(2,1)S(1)} %copy-done.2, bf16[108,8,128]{2,1,0:T(8,128)(2,1)S(1)} %get-tuple-element.26.after.rest_0_, ...), custom_call_target="tpu_custom_call" | custom-call | flops 3000000000 | bytes 4000000 | tf_op jit(solution)/shard_map/pallas_call | solution.py:423
  56.5 0.0 collective-permute-done.5.rest_0_
  56.6 1.5 %collective-permute-done.6.rest_1_ = bf16[54,8,128]{2,1,0:T(8,128)(2,1)S(1)} collective-permute-done((bf16[54,8,128]{2,1,0:T(8,128)(2,1)S(1)}, bf16[54,8,128]{2,1,0:T(8,128)(2,1)S(1)}, u32[]{:S(2)}, u32[]{:S(2)}) %collective-permute-start.6) | collective-permute-done | bytes 110624 | tf_op jit(solution)/shard_map/ppermute | solution.py:50
  58.1 2.3 %shard_map.126 = bf16[3,12,12,8,128]{4,3,2,1,0:T(8,128)(2,1)} custom-call(bf16[3,12,12,8,128]{4,3,2,1,0:T(8,128)(2,1)S(1)} %bitcast.19, bf16[512,2048]{1,0:T(8,128)(2,1)S(1)} %copy-done.1, bf16[2048,512]{1,0:T(8,128)(2,1)S(1)} %copy-done.2, bf16[54,8,128]{2,1,0:T(8,128)(2,1)S(1)} %collective-permute-done.5.rest_0_, ...), custom_call_target="tpu_custom_call" | custom-call | flops 1000000000 | bytes 4000000 | tf_op jit(solution)/shard_map/pallas_call | solution.py:423
  (16 shorter events, 0.1 us)
Async XLA Ops:
  0.0 15.2 %copy-start.4 = (f32[8]{0:T(128)S(1)}, f32[8]{0:T(128)}, u32[]{:S(2)}) copy-start(f32[8]{0:T(128)} %param.16) | copy-start | bytes 100
  0.0 15.2 %copy-start.3 = (bf16[512,1536]{1,0:T(8,128)(2,1)S(1)}, bf16[512,1536]{1,0:T(8,128)(2,1)}, u32[]{:S(2)}) copy-start(bf16[512,1536]{1,0:T(8,128)(2,1)} %w_qkv.9) | copy-start | bytes 4718596
  1.4 8.8 %collective-permute-start.1 = (bf16[219,8,128]{2,1,0:T(8,128)(2,1)S(1)}, bf16[219,8,128]{2,1,0:T(8,128)(2,1)S(1)}, u32[]{:S(2)}, u32[]{:S(2)}) collective-permute-start(bf16[219,8,128]{2,1,0:T(8,128)(2,1)S(1)} %get-tuple-element.21), channel_id=1, source_target_pairs={{0,240},{1,241},{2,242},{3,243},{4,244},{5,245},{6,246},{7,247},{8... | collective-permute-start | bytes 1345544 | tf_op jit(solution)/shard_map/ppermute | solution.py:50
  4.3 29.1 %collective-permute-start = (bf16[162,8,128]{2,1,0:T(8,128)(2,1)S(1)}, bf16[162,8,128]{2,1,0:T(8,128)(2,1)S(1)}, u32[]{:S(2)}, u32[]{:S(2)}) collective-permute-start(bf16[162,8,128]{2,1,0:T(8,128)(2,1)S(1)} %get-tuple-element.20.own), channel_id=1, source_target_pairs={{0,256},{1,257},{2,258},{3,259},{4,260},{5,261},{6,262},{7,263},{8... | collective-permute-start | bytes 995336 | tf_op jit(solution)/shard_map/ppermute | solution.py:50
  10.2 6.1 %copy-start.6 = (f32[8]{0:T(128)S(1)}, f32[8]{0:T(128)}, u32[]{:S(2)}) copy-start(f32[8]{0:T(128)} %param.17) | copy-start | bytes 100
  10.2 6.1 %copy-start.8 = (f32[96,432]{1,0:T(8,128)S(1)}, f32[96,432]{1,0:T(8,128)}, u32[]{:S(2)}) copy-start(f32[96,432]{1,0:T(8,128)} %constant.8.clone.pick_row) | copy-start | bytes 497668
  10.2 6.1 %copy-start.10 = (f32[16,432]{1,0:T(8,128)S(1)}, f32[16,432]{1,0:T(8,128)}, u32[]{:S(2)}) copy-start(f32[16,432]{1,0:T(8,128)} %constant.9.clone.pick_lane) | copy-start | bytes 82948
  10.2 23.2 %collective-permute-start.2 = (bf16[162,8,128]{2,1,0:T(8,128)(2,1)S(1)}, bf16[162,8,128]{2,1,0:T(8,128)(2,1)S(1)}, u32[]{:S(2)}, u32[]{:S(2)}) collective-permute-start(bf16[162,8,128]{2,1,0:T(8,128)(2,1)S(1)} %shard_map.118), channel_id=1, source_target_pairs={{0,256},{1,257},{2,258},{3,259},{4,260},{5,261},{6,262},{7,263},{8... | collective-permute-start | bytes 995336 | tf_op jit(solution)/shard_map/ppermute | solution.py:50
  19.6 13.8 %copy-start.5 = (bf16[512,512]{1,0:T(8,128)(2,1)S(1)}, bf16[512,512]{1,0:T(8,128)(2,1)}, u32[]{:S(2)}) copy-start(bf16[512,512]{1,0:T(8,128)(2,1)} %w_out.3) | copy-start | bytes 1572868
  19.6 17.5 %collective-permute-start.4 = (bf16[114,8,128]{2,1,0:T(8,128)(2,1)S(1)}, bf16[114,8,128]{2,1,0:T(8,128)(2,1)S(1)}, u32[]{:S(2)}, u32[]{:S(2)}) collective-permute-start(bf16[114,8,128]{2,1,0:T(8,128)(2,1)S(1)} %shard_map.121), channel_id=1, source_target_pairs={{0,15},{1,0},{2,1},{3,2},{4,3},{5,4},{6,5},{7,6},{8,7},{9,8},{10,9... | collective-permute-start | bytes 700424 | tf_op jit(solution)/shard_map/ppermute | solution.py:50
  29.8 11.1 %collective-permute-start.3 = (bf16[114,8,128]{2,1,0:T(8,128)(2,1)S(1)}, bf16[114,8,128]{2,1,0:T(8,128)(2,1)S(1)}, u32[]{:S(2)}, u32[]{:S(2)}) collective-permute-start(bf16[114,8,128]{2,1,0:T(8,128)(2,1)S(1)} %shard_map.121), channel_id=1, source_target_pairs={{0,271},{1,256},{2,257},{3,258},{4,259},{5,260},{6,261},{7,262},{8... | collective-permute-start | bytes 700424 | tf_op jit(solution)/shard_map/ppermute | solution.py:50
  33.4 3.7 %copy-start.7 = (f32[96,432]{1,0:T(8,128)S(1)}, f32[96,432]{1,0:T(8,128)}, u32[]{:S(2)}) copy-start(f32[96,432]{1,0:T(8,128)} %constant.10.clone.pick_row) | copy-start | bytes 497668
  33.4 3.7 %copy-start.9 = (f32[16,432]{1,0:T(8,128)S(1)}, f32[16,432]{1,0:T(8,128)}, u32[]{:S(2)}) copy-start(f32[16,432]{1,0:T(8,128)} %constant.11.clone.pick_lane) | copy-start | bytes 82948
  40.9 11.5 %copy-start = (bf16[3,2,12,12,512]{4,1,3,2,0:T(2,128)(2,1)S(1)}, bf16[3,2,12,12,512]{4,1,3,2,0:T(2,128)(2,1)}, u32[]{:S(2)}) copy-start(bf16[3,2,12,12,512]{4,1,3,2,0:T(2,128)(2,1)} %param.12) | copy-start | bytes 2654212
  40.9 11.5 %copy-start.1 = (bf16[512,2048]{1,0:T(8,128)(2,1)S(1)}, bf16[512,2048]{1,0:T(8,128)(2,1)}, u32[]{:S(2)}) copy-start(bf16[512,2048]{1,0:T(8,128)(2,1)} %w_up.3) | copy-start | bytes 6291460
  40.9 11.5 %copy-start.2 = (bf16[2048,512]{1,0:T(8,128)(2,1)S(1)}, bf16[2048,512]{1,0:T(8,128)(2,1)}, u32[]{:S(2)}) copy-start(bf16[2048,512]{1,0:T(8,128)(2,1)} %w_down.3) | copy-start | bytes 6291460
  44.7 7.8 %collective-permute-start.7 = (bf16[162,8,128]{2,1,0:T(8,128)(2,1)S(1)}, bf16[162,8,128]{2,1,0:T(8,128)(2,1)S(1)}, u32[]{:S(2)}, u32[]{:S(2)}) collective-permute-start(bf16[162,8,128]{2,1,0:T(8,128)(2,1)S(1)} %get-tuple-element.33), channel_id=1, source_target_pairs={{0,16},{1,17},{2,18},{3,19},{4,20},{5,21},{6,22},{7,23},{8,24},{9,... | collective-permute-start | bytes 995336 | tf_op jit(solution)/shard_map/ppermute | solution.py:50
  44.7 11.9 %collective-permute-start.5 = (bf16[54,8,128]{2,1,0:T(8,128)(2,1)S(1)}, bf16[54,8,128]{2,1,0:T(8,128)(2,1)S(1)}, u32[]{:S(2)}, u32[]{:S(2)}) collective-permute-start(bf16[54,8,128]{2,1,0:T(8,128)(2,1)S(1)} %get-tuple-element.31), channel_id=1, source_target_pairs={{0,1},{1,2},{2,3},{3,4},{4,5},{5,6},{6,7},{7,8},{8,9},{9,10},{10,1... | collective-permute-start | bytes 331784 | tf_op jit(solution)/shard_map/ppermute | solution.py:50
  47.8 10.3 %collective-permute-start.6 = (bf16[54,8,128]{2,1,0:T(8,128)(2,1)S(1)}, bf16[54,8,128]{2,1,0:T(8,128)(2,1)S(1)}, u32[]{:S(2)}, u32[]{:S(2)}) collective-permute-start(bf16[54,8,128]{2,1,0:T(8,128)(2,1)S(1)} %get-tuple-element.32), channel_id=1, source_target_pairs={{0,17},{1,18},{2,19},{3,20},{4,21},{5,22},{6,23},{7,24},{8,25},{9,... | collective-permute-start | bytes 331784 | tf_op jit(solution)/shard_map/ppermute | solution.py:50

commit v5 on v4

--- a/solution.py
+++ b/solution.py
@@ -82,25 +82,17 @@
     return centred * lax.rsqrt(jnp.mean(centred * centred, -1, keepdims=True) + 1e-05)
 
 
-def head_squares(values, head_size):
-    width = 256
-    rows = lax.broadcasted_iota(jnp.int32, (width, width), 0) // head_size
-    cols = lax.broadcasted_iota(jnp.int32, (width, width), 1) // head_size
-    averaging = jnp.where(rows == cols, 1.0 / head_size, 0.0).astype(jnp.bfloat16)
-    squares = (values * values).astype(jnp.bfloat16)
-    return jnp.concatenate(
-        [
-            jnp.dot(
-                squares[:, at : at + width], averaging, preferred_element_type=jnp.float32
-            )
-            for at in range(0, values.shape[1], width)
-        ],
-        axis=1,
-    )
-
-
 def unit_heads(values, head_size):
-    return values * lax.rsqrt(head_squares(values, head_size) + 1e-06)
+    lane = lax.broadcasted_iota(jnp.int32, (1, LANES), 1)
+    parts = []
+    for at in range(0, values.shape[1], LANES):
+        part = values[:, at : at + LANES]
+        squares = part * part
+        left = jnp.sum(jnp.where(lane < head_size, squares, 0.0), 1, keepdims=True)
+        right = jnp.sum(jnp.where(lane < head_size, 0.0, squares), 1, keepdims=True)
+        mean = jnp.where(lane < head_size, left, right) * (1.0 / head_size)
+        parts.append(part * lax.rsqrt(mean + 1e-06))
+    return jnp.concatenate(parts, axis=1)
 
 
 def window_columns(part):

time: 60.9 us -> 60.5 us (level)
  no operation moved by 1% of the time
where the time goes in v5:
time: 60.5 us; the launch traced here: 60.2 us
  starting transfers between devices  31.8 us (53%)
  Pallas kernels  22.8 us (38%)
  waiting for transfers between devices  5.03 us (8%)
    ppermute x8, starting transfers between devices, shifted(): return lax.ppermute(array, axes, pairs)  31.8 us
    pallas_call x9, Pallas kernels, call(): pl.pallas_call(kernel, compiler_params=ROOM, out_shape=outs, in_specs=[VM...  21.5 us
    ppermute x8, waiting for transfers between devices, shifted(): return lax.ppermute(array, axes, pairs)  5.03 us
    pallas_call x1, Pallas kernels, per_device(): pl.pallas_call(pack_kernel, name='pack', compiler_params=ROOM, out_shape=...  1.35 us
  transfers between devices with their start and end apart: 8, of which 3 were waited for; matrix products, arithmetic and copies ran while one was open for 0% of the time, Pallas kernels for 26%

profile of v5, /device:TPU:4, one launch (start us, length us, event | category | flops | bytes accessed | tf_op | source)
XLA Modules:
  0.0 60.2 jit_solution(16816144593988087119)
XLA Ops:
  0.0 1.3 %pack.1 = (bf16[162,8,128]{2,1,0:T(8,128)(2,1)S(1)}, bf16[219,8,128]{2,1,0:T(8,128)(2,1)S(1)}, bf16[57,8,128]{2,1,0:T(8,128)(2,1)S(1)}) custom-call(bf16[3,12,12,8,128]{4,3,2,1,0:T(8,128)(2,1)} %bitcast.17, s32[12,2,12]{2,1,0:T(2,128)} %bitcast.25), custom_call_target="tpu_custom_call" | custom-call | tf_op jit(solution)/shard_map/pack/pallas_call | solution.py:427
  1.4 2.9 %collective-permute-start.1 = (bf16[219,8,128]{2,1,0:T(8,128)(2,1)S(1)}, bf16[219,8,128]{2,1,0:T(8,128)(2,1)S(1)}, u32[]{:S(2)}, u32[]{:S(2)}) collective-permute-start(bf16[219,8,128]{2,1,0:T(8,128)(2,1)S(1)} %get-tuple-element.21), channel_id=1, source_target_pairs={{0,240},{1,241},{2,242},{3,243},{4,244},{5,245},{6,246},{7,247},{8... | collective-permute-start | bytes 1345544 | tf_op jit(solution)/shard_map/ppermute | solution.py:50
  4.3 4.9 %collective-permute-start = (bf16[162,8,128]{2,1,0:T(8,128)(2,1)S(1)}, bf16[162,8,128]{2,1,0:T(8,128)(2,1)S(1)}, u32[]{:S(2)}, u32[]{:S(2)}) collective-permute-start(bf16[162,8,128]{2,1,0:T(8,128)(2,1)S(1)} %get-tuple-element.20.own), channel_id=1, source_target_pairs={{0,256},{1,257},{2,258},{3,259},{4,260},{5,261},{6,262},{7,263},{8... | collective-permute-start | bytes 995336 | tf_op jit(solution)/shard_map/ppermute | solution.py:50
  9.2 1.0 %collective-permute-done.1.east = bf16[219,8,128]{2,1,0:T(8,128)(2,1)S(1)} collective-permute-done((bf16[219,8,128]{2,1,0:T(8,128)(2,1)S(1)}, bf16[219,8,128]{2,1,0:T(8,128)(2,1)S(1)}, u32[]{:S(2)}, u32[]{:S(2)}) %collective-permute-start.1) | collective-permute-done | bytes 448544 | tf_op jit(solution)/shard_map/ppermute | solution.py:50
  10.2 0.0 copy-start.6
  10.2 0.0 copy-start.8
  10.2 0.0 copy-start.10
  10.2 5.0 %collective-permute-start.2 = (bf16[162,8,128]{2,1,0:T(8,128)(2,1)S(1)}, bf16[162,8,128]{2,1,0:T(8,128)(2,1)S(1)}, u32[]{:S(2)}, u32[]{:S(2)}) collective-permute-start(bf16[162,8,128]{2,1,0:T(8,128)(2,1)S(1)} %shard_map.118), channel_id=1, source_target_pairs={{0,256},{1,257},{2,258},{3,259},{4,260},{5,261},{6,262},{7,263},{8... | collective-permute-start | bytes 995336 | tf_op jit(solution)/shard_map/ppermute | solution.py:50
  15.3 1.0 %shard_map.119.south = f32[3,216,512]{2,1,0:T(8,128)S(1)} custom-call(bf16[162,8,128]{2,1,0:T(8,128)(2,1)S(1)} %get-tuple-element.20.own, bf16[512,1536]{1,0:T(8,128)(2,1)S(1)} %copy-done.3, f32[1,8]{1,0:T(1,128)S(1)} %bitcast.20), custom_call_target="tpu_custom_call" | custom-call | flops 300000000 | bytes 4000000 | tf_op jit(solution)/shard_map/pallas_call | solution.py:415
  16.3 3.1 %shard_map.120 = (bf16[432,512]{1,0:T(8,128)(2,1)S(1)}, f32[4,432,256]{2,1,0:T(8,128)S(1)}, f32[16,432]{1,0:T(8,128)S(1)}) custom-call(bf16[162,8,128]{2,1,0:T(8,128)(2,1)S(1)} %get-tuple-element.20.own, bf16[219,8,128]{2,1,0:T(8,128)(2,1)S(1)} %collective-permute-done.1.east, f32[3,216,512]{2,1,0:T(8,128)S(1)} %shard_map.119.south, ...), custom_call_target="tpu_custom_call" | custom-call | flops 3000000000 | bytes 4000000 | tf_op jit(solution)/shard_map/pallas_call | solution.py:415
  19.4 0.0 copy-start.5
  19.5 10.2 %collective-permute-start.4 = (bf16[114,8,128]{2,1,0:T(8,128)(2,1)S(1)}, bf16[114,8,128]{2,1,0:T(8,128)(2,1)S(1)}, u32[]{:S(2)}, u32[]{:S(2)}) collective-permute-start(bf16[114,8,128]{2,1,0:T(8,128)(2,1)S(1)} %shard_map.121), channel_id=1, source_target_pairs={{0,15},{1,0},{2,1},{3,2},{4,3},{5,4},{6,5},{7,6},{8,7},{9,8},{10,9... | collective-permute-start | bytes 700424 | tf_op jit(solution)/shard_map/ppermute | solution.py:50
  29.6 3.6 %collective-permute-start.3 = (bf16[114,8,128]{2,1,0:T(8,128)(2,1)S(1)}, bf16[114,8,128]{2,1,0:T(8,128)(2,1)S(1)}, u32[]{:S(2)}, u32[]{:S(2)}) collective-permute-start(bf16[114,8,128]{2,1,0:T(8,128)(2,1)S(1)} %shard_map.121), channel_id=1, source_target_pairs={{0,271},{1,256},{2,257},{3,258},{4,259},{5,260},{6,261},{7,262},{8... | collective-permute-start | bytes 700424 | tf_op jit(solution)/shard_map/ppermute | solution.py:50
  33.2 0.0 collective-permute-done.own.south
  33.2 0.0 collective-permute-done.2.east
  33.3 0.0 copy-start.7
  33.3 0.0 copy-start.9
  33.3 3.6 %shard_map.122 = (bf16[108,8,128]{2,1,0:T(8,128)(2,1)S(1)}, bf16[108,8,128]{2,1,0:T(8,128)(2,1)S(1)}) custom-call(bf16[162,8,128]{2,1,0:T(8,128)(2,1)S(1)} %collective-permute-done.own.south, bf16[162,8,128]{2,1,0:T(8,128)(2,1)S(1)} %collective-permute-done.2.east, bf16[162,8,128]{2,1,0:T(8,128)(2,1)S(1)} %collective-permute-done.own.south, ...), custom_call_target="tpu_custom_call" | custom-call | flops 3000000000 | bytes 4000000 | tf_op jit(solution)/shard_map/pallas_call | solution.py:415
  36.9 0.0 collective-permute-done.4.south
  37.0 3.5 %shard_map.123 = (bf16[432,512]{1,0:T(8,128)(2,1)S(1)}, f32[4,432,256]{2,1,0:T(8,128)S(1)}, f32[16,432]{1,0:T(8,128)S(1)}) custom-call(bf16[162,8,128]{2,1,0:T(8,128)(2,1)S(1)} %get-tuple-element.20.own, bf16[219,8,128]{2,1,0:T(8,128)(2,1)S(1)} %collective-permute-done.1.east, bf16[114,8,128]{2,1,0:T(8,128)(2,1)S(1)} %collective-permute-done.4.south, ...), custom_call_target="tpu_custom_call" | custom-call | flops 3000000000 | bytes 4000000 | tf_op jit(solution)/shard_map/pallas_call | solution.py:415
  40.5 0.0 collective-permute-done.3.south
  40.5 0.0 copy-start
  40.5 0.0 copy-start.1
  40.5 0.0 copy-start.2
  40.5 3.7 %shard_map.124 = (bf16[54,8,128]{2,1,0:T(8,128)(2,1)S(1)}, bf16[162,8,128]{2,1,0:T(8,128)(2,1)S(1)}, bf16[54,8,128]{2,1,0:T(8,128)(2,1)S(1)}, bf16[54,8,128]{2,1,0:T(8,128)(2,1)S(1)}) custom-call(bf16[162,8,128]{2,1,0:T(8,128)(2,1)S(1)} %collective-permute-done.own.south, bf16[162,8,128]{2,1,0:T(8,128)(2,1)S(1)} %collective-permute-done.2.east, ...), custom_call_target="tpu_custom_call" | custom-call | flops 3000000000 | bytes 4000000 | tf_op jit(solution)/shard_map/pallas_call | solution.py:415
  44.2 0.0 collective-permute-start.7
  44.2 3.1 %collective-permute-start.5 = (bf16[54,8,128]{2,1,0:T(8,128)(2,1)S(1)}, bf16[54,8,128]{2,1,0:T(8,128)(2,1)S(1)}, u32[]{:S(2)}, u32[]{:S(2)}) collective-permute-start(bf16[54,8,128]{2,1,0:T(8,128)(2,1)S(1)} %get-tuple-element.31), channel_id=1, source_target_pairs={{0,1},{1,2},{2,3},{3,4},{4,5},{5,6},{6,7},{7,8},{8,9},{9,10},{10,1... | collective-permute-start | bytes 331784 | tf_op jit(solution)/shard_map/ppermute | solution.py:50
  47.4 2.1 %collective-permute-start.6 = (bf16[54,8,128]{2,1,0:T(8,128)(2,1)S(1)}, bf16[54,8,128]{2,1,0:T(8,128)(2,1)S(1)}, u32[]{:S(2)}, u32[]{:S(2)}) collective-permute-start(bf16[54,8,128]{2,1,0:T(8,128)(2,1)S(1)} %get-tuple-element.32), channel_id=1, source_target_pairs={{0,17},{1,18},{2,19},{3,20},{4,21},{5,22},{6,23},{7,24},{8,25},{9,... | collective-permute-start | bytes 331784 | tf_op jit(solution)/shard_map/ppermute | solution.py:50
  49.5 2.5 %collective-permute-done.7.rest_1_.rest_3_ = bf16[162,8,128]{2,1,0:T(8,128)(2,1)S(1)} collective-permute-done((bf16[162,8,128]{2,1,0:T(8,128)(2,1)S(1)}, bf16[162,8,128]{2,1,0:T(8,128)(2,1)S(1)}, u32[]{:S(2)}, u32[]{:S(2)}) %collective-permute-start.7) | collective-permute-done | bytes 331808 | tf_op jit(solution)/shard_map/ppermute | solution.py:50
  52.0 4.1 %shard_map.125.rest_2_ = bf16[3,9,12,8,128]{4,3,2,1,0:T(8,128)(2,1)S(1)} custom-call(bf16[3,12,12,8,128]{4,3,2,1,0:T(8,128)(2,1)S(1)} %bitcast.18, bf16[512,2048]{1,0:T(8,128)(2,1)S(1)} %copy-done.1, bf16[2048,512]{1,0:T(8,128)(2,1)S(1)} %copy-done.2, bf16[108,8,128]{2,1,0:T(8,128)(2,1)S(1)} %get-tuple-element.26.after.rest_0_, ...), custom_call_target="tpu_custom_call" | custom-call | flops 3000000000 | bytes 4000000 | tf_op jit(solution)/shard_map/pallas_call | solution.py:415
  56.1 1.5 %collective-permute-done.6.rest_1_ = bf16[54,8,128]{2,1,0:T(8,128)(2,1)S(1)} collective-permute-done((bf16[54,8,128]{2,1,0:T(8,128)(2,1)S(1)}, bf16[54,8,128]{2,1,0:T(8,128)(2,1)S(1)}, u32[]{:S(2)}, u32[]{:S(2)}) %collective-permute-start.6) | collective-permute-done | bytes 110624 | tf_op jit(solution)/shard_map/ppermute | solution.py:50
  57.6 2.3 %shard_map.126 = bf16[3,12,12,8,128]{4,3,2,1,0:T(8,128)(2,1)} custom-call(bf16[3,12,12,8,128]{4,3,2,1,0:T(8,128)(2,1)S(1)} %bitcast.19, bf16[512,2048]{1,0:T(8,128)(2,1)S(1)} %copy-done.1, bf16[2048,512]{1,0:T(8,128)(2,1)S(1)} %copy-done.2, bf16[54,8,128]{2,1,0:T(8,128)(2,1)S(1)} %collective-permute-done.5.rest_0_, ...), custom_call_target="tpu_custom_call" | custom-call | flops 1000000000 | bytes 4000000 | tf_op jit(solution)/shard_map/pallas_call | solution.py:415
  (16 shorter events, 0.1 us)
Async XLA Ops:
  0.0 15.2 %copy-start.4 = (f32[8]{0:T(128)S(1)}, f32[8]{0:T(128)}, u32[]{:S(2)}) copy-start(f32[8]{0:T(128)} %param.16) | copy-start | bytes 100
  0.0 15.2 %copy-start.3 = (bf16[512,1536]{1,0:T(8,128)(2,1)S(1)}, bf16[512,1536]{1,0:T(8,128)(2,1)}, u32[]{:S(2)}) copy-start(bf16[512,1536]{1,0:T(8,128)(2,1)} %w_qkv.9) | copy-start | bytes 4718596
  1.4 8.8 %collective-permute-start.1 = (bf16[219,8,128]{2,1,0:T(8,128)(2,1)S(1)}, bf16[219,8,128]{2,1,0:T(8,128)(2,1)S(1)}, u32[]{:S(2)}, u32[]{:S(2)}) collective-permute-start(bf16[219,8,128]{2,1,0:T(8,128)(2,1)S(1)} %get-tuple-element.21), channel_id=1, source_target_pairs={{0,240},{1,241},{2,242},{3,243},{4,244},{5,245},{6,246},{7,247},{8... | collective-permute-start | bytes 1345544 | tf_op jit(solution)/shard_map/ppermute | solution.py:50
  4.3 29.0 %collective-permute-start = (bf16[162,8,128]{2,1,0:T(8,128)(2,1)S(1)}, bf16[162,8,128]{2,1,0:T(8,128)(2,1)S(1)}, u32[]{:S(2)}, u32[]{:S(2)}) collective-permute-start(bf16[162,8,128]{2,1,0:T(8,128)(2,1)S(1)} %get-tuple-element.20.own), channel_id=1, source_target_pairs={{0,256},{1,257},{2,258},{3,259},{4,260},{5,261},{6,262},{7,263},{8... | collective-permute-start | bytes 995336 | tf_op jit(solution)/shard_map/ppermute | solution.py:50
  10.2 6.1 %copy-start.6 = (f32[8]{0:T(128)S(1)}, f32[8]{0:T(128)}, u32[]{:S(2)}) copy-start(f32[8]{0:T(128)} %param.17) | copy-start | bytes 100
  10.2 6.1 %copy-start.8 = (f32[96,432]{1,0:T(8,128)S(1)}, f32[96,432]{1,0:T(8,128)}, u32[]{:S(2)}) copy-start(f32[96,432]{1,0:T(8,128)} %constant.8.clone.pick_row) | copy-start | bytes 497668
  10.2 6.1 %copy-start.10 = (f32[16,432]{1,0:T(8,128)S(1)}, f32[16,432]{1,0:T(8,128)}, u32[]{:S(2)}) copy-start(f32[16,432]{1,0:T(8,128)} %constant.9.clone.pick_lane) | copy-start | bytes 82948
  10.2 23.0 %collective-permute-start.2 = (bf16[162,8,128]{2,1,0:T(8,128)(2,1)S(1)}, bf16[162,8,128]{2,1,0:T(8,128)(2,1)S(1)}, u32[]{:S(2)}, u32[]{:S(2)}) collective-permute-start(bf16[162,8,128]{2,1,0:T(8,128)(2,1)S(1)} %shard_map.118), channel_id=1, source_target_pairs={{0,256},{1,257},{2,258},{3,259},{4,260},{5,261},{6,262},{7,263},{8... | collective-permute-start | bytes 995336 | tf_op jit(solution)/shard_map/ppermute | solution.py:50
  19.4 13.8 %copy-start.5 = (bf16[512,512]{1,0:T(8,128)(2,1)S(1)}, bf16[512,512]{1,0:T(8,128)(2,1)}, u32[]{:S(2)}) copy-start(bf16[512,512]{1,0:T(8,128)(2,1)} %w_out.3) | copy-start | bytes 1572868
  19.5 17.5 %collective-permute-start.4 = (bf16[114,8,128]{2,1,0:T(8,128)(2,1)S(1)}, bf16[114,8,128]{2,1,0:T(8,128)(2,1)S(1)}, u32[]{:S(2)}, u32[]{:S(2)}) collective-permute-start(bf16[114,8,128]{2,1,0:T(8,128)(2,1)S(1)} %shard_map.121), channel_id=1, source_target_pairs={{0,15},{1,0},{2,1},{3,2},{4,3},{5,4},{6,5},{7,6},{8,7},{9,8},{10,9... | collective-permute-start | bytes 700424 | tf_op jit(solution)/shard_map/ppermute | solution.py:50
  29.6 10.8 %collective-permute-start.3 = (bf16[114,8,128]{2,1,0:T(8,128)(2,1)S(1)}, bf16[114,8,128]{2,1,0:T(8,128)(2,1)S(1)}, u32[]{:S(2)}, u32[]{:S(2)}) collective-permute-start(bf16[114,8,128]{2,1,0:T(8,128)(2,1)S(1)} %shard_map.121), channel_id=1, source_target_pairs={{0,271},{1,256},{2,257},{3,258},{4,259},{5,260},{6,261},{7,262},{8... | collective-permute-start | bytes 700424 | tf_op jit(solution)/shard_map/ppermute | solution.py:50
  33.3 3.7 %copy-start.7 = (f32[96,432]{1,0:T(8,128)S(1)}, f32[96,432]{1,0:T(8,128)}, u32[]{:S(2)}) copy-start(f32[96,432]{1,0:T(8,128)} %constant.10.clone.pick_row) | copy-start | bytes 497668
  33.3 3.7 %copy-start.9 = (f32[16,432]{1,0:T(8,128)S(1)}, f32[16,432]{1,0:T(8,128)}, u32[]{:S(2)}) copy-start(f32[16,432]{1,0:T(8,128)} %constant.11.clone.pick_lane) | copy-start | bytes 82948
  40.5 11.5 %copy-start = (bf16[3,2,12,12,512]{4,1,3,2,0:T(2,128)(2,1)S(1)}, bf16[3,2,12,12,512]{4,1,3,2,0:T(2,128)(2,1)}, u32[]{:S(2)}) copy-start(bf16[3,2,12,12,512]{4,1,3,2,0:T(2,128)(2,1)} %param.12) | copy-start | bytes 2654212
  40.5 11.5 %copy-start.1 = (bf16[512,2048]{1,0:T(8,128)(2,1)S(1)}, bf16[512,2048]{1,0:T(8,128)(2,1)}, u32[]{:S(2)}) copy-start(bf16[512,2048]{1,0:T(8,128)(2,1)} %w_up.3) | copy-start | bytes 6291460
  40.5 11.5 %copy-start.2 = (bf16[2048,512]{1,0:T(8,128)(2,1)S(1)}, bf16[2048,512]{1,0:T(8,128)(2,1)}, u32[]{:S(2)}) copy-start(bf16[2048,512]{1,0:T(8,128)(2,1)} %w_down.3) | copy-start | bytes 6291460
  44.2 7.8 %collective-permute-start.7 = (bf16[162,8,128]{2,1,0:T(8,128)(2,1)S(1)}, bf16[162,8,128]{2,1,0:T(8,128)(2,1)S(1)}, u32[]{:S(2)}, u32[]{:S(2)}) collective-permute-start(bf16[162,8,128]{2,1,0:T(8,128)(2,1)S(1)} %get-tuple-element.33), channel_id=1, source_target_pairs={{0,16},{1,17},{2,18},{3,19},{4,20},{5,21},{6,22},{7,23},{8,24},{9,... | collective-permute-start | bytes 995336 | tf_op jit(solution)/shard_map/ppermute | solution.py:50
  44.2 11.9 %collective-permute-start.5 = (bf16[54,8,128]{2,1,0:T(8,128)(2,1)S(1)}, bf16[54,8,128]{2,1,0:T(8,128)(2,1)S(1)}, u32[]{:S(2)}, u32[]{:S(2)}) collective-permute-start(bf16[54,8,128]{2,1,0:T(8,128)(2,1)S(1)} %get-tuple-element.31), channel_id=1, source_target_pairs={{0,1},{1,2},{2,3},{3,4},{4,5},{5,6},{6,7},{7,8},{8,9},{9,10},{10,1... | collective-permute-start | bytes 331784 | tf_op jit(solution)/shard_map/ppermute | solution.py:50
  47.4 10.3 %collective-permute-start.6 = (bf16[54,8,128]{2,1,0:T(8,128)(2,1)S(1)}, bf16[54,8,128]{2,1,0:T(8,128)(2,1)S(1)}, u32[]{:S(2)}, u32[]{:S(2)}) collective-permute-start(bf16[54,8,128]{2,1,0:T(8,128)(2,1)S(1)} %get-tuple-element.32), channel_id=1, source_target_pairs={{0,17},{1,18},{2,19},{3,20},{4,21},{5,22},{6,23},{7,24},{8,25},{9,... | collective-permute-start | bytes 331784 | tf_op jit(solution)/shard_map/ppermute | solution.py:50
